TPU v7x, 256 devices: a whole 4x4x8 slice. The times are simulated.
256 devices in a mesh: inter: 32 (over y, z_hi, x), intra: 8 (over z_lo, core).
Axes of the slice: x: 4, y: 4, z: 8 (z_hi: 2, z_lo: 4; z = z_hi * 4 + z_lo), core: 2. Of those that a mesh axis runs over, the one named last changes fastest.
Arguments:
- tokens: bfloat16 [4096, 4096], P('inter', 'intra'), may hold values from -6 to 6
- gate_codes: bfloat16 [7168, 4096], P(('intra', 'inter')), may hold values from -127 to 127
- gate_scales: float32 [7168, 16], P(('intra', 'inter')), may hold values from 0.0001 to 0.0005
- up_codes: bfloat16 [7168, 4096], P(('intra', 'inter')), may hold values from -127 to 127
- up_scales: float32 [7168, 16], P(('intra', 'inter')), may hold values from 0.0001 to 0.0005
- cotangent: bfloat16 [4096, 7168], P('inter', 'intra'), may hold values from -6 to 6
Outputs:
- hidden: bfloat16 [4096, 7168], P('inter', 'intra')
- token_grad: bfloat16 [4096, 4096], P('inter', 'intra')
- gate_grad: float32 [7168, 4096], P(('intra', 'inter'))
- up_grad: float32 [7168, 4096], P(('intra', 'inter'))
All inputs are finite; a program needn't handle non-finite values.
Results may differ from a plain program's by a relative error of at most 0.02.
Values may be sent and summed in bfloat16 or wider, within the bound.
No kernel may reach another device: no remote copies, remote signals or barrier semaphores. Data moves between devices by JAX's collectives and lax.ppermute only.
A program may use at most 192 MiB of HBM per device.

v0:
```python
import functools
import jax
import jax.numpy as jnp
from jax import lax
from jax.experimental import pallas as pl
from jax.experimental.pallas import tpu as pltpu
from jax.sharding import Mesh, PartitionSpec as P


D = 4096
TOK = 128
SLICE = 512
ROWS = 28
BLOCK = 256
NY, NZH, NX, NZL, NC = 4, 2, 4, 4, 2
NZ = NZH * NZL
GROUPS = NY * NZH * NX
REL = (0, -1, 1, 2)
HALF_A, HALF_B = 16, 12
SHARD_A, SHARD_B = 2 * HALF_A, 2 * HALF_B
WIDE_A, WIDE_B = 16 * SHARD_A, 16 * SHARD_B
WIDE = WIDE_A + WIDE_B
F32, BF16 = jnp.float32, jnp.bfloat16


AXES = ("y", "zh", "x", "zl", "core")


def shift(value, dx=0, dy=0, dz=0, dc=0):
    pairs = []
    for y in range(NY):
        for zh in range(NZH):
            for x in range(NX):
                for zl in range(NZL):
                    for c in range(NC):
                        z = (zh * NZL + zl + dz) % NZ
                        source = (((y * NZH + zh) * NX + x) * NZL + zl) * NC + c
                        target = (
                            (((y + dy) % NY * NZH + z // NZL) * NX + (x + dx) % NX) * NZL + z % NZL
                        ) * NC + (c + dc) % NC
                        pairs.append((source, target))
    return lax.ppermute(value, AXES, pairs)


def exchange_z(value):
    return lax.all_to_all(value, ("zh", "zl"), 0, 0, tiled=True)


def call(kernel, outs, megabytes=16, **kw):
    return pl.pallas_call(
        kernel,
        out_shape=outs,
        compiler_params=pltpu.CompilerParams(vmem_limit_bytes=megabytes * 1024 * 1024),
        **kw,
    )


def shape(rows, cols, kind=BF16):
    return jax.ShapeDtypeStruct((rows, cols), kind)


VMEM = pl.BlockSpec(memory_space=pltpu.VMEM)


def dequant_kernel(*refs):
    sources, (a, b), (gc, gs, uc, us), sems = refs[:4], refs[4:6], refs[6:10], refs[10]
    copies = [
        pltpu.make_async_copy(source, target, sems.at[n])
        for n, (source, target) in enumerate(zip(sources, (gc, gs, uc, us)))
    ]
    for copy in copies:
        copy.start()
    for copy in copies:
        copy.wait()
    scales_g, scales_u = gs[...].T, us[...].T
    for n in range(D // BLOCK):
        cols = slice(n * BLOCK, (n + 1) * BLOCK)
        g = gc[:, cols].astype(F32) * scales_g[:, n : n + 1]
        u = uc[:, cols].astype(F32) * scales_u[:, n : n + 1]
        a[:, cols] = jnp.concatenate([g[:HALF_A], u[:HALF_A]], axis=0).astype(BF16)
        b[:, cols] = jnp.concatenate([g[HALF_A:], u[HALF_A:]], axis=0).astype(BF16)


def pair_kernel(first, second, out):
    n = first.shape[0]
    out[:n] = first[...]
    out[n:] = second[...]


def copies_kernel(tokens, out):
    for n in range(NZ):
        out[n] = tokens[...]


def rel_of(n):
    return jnp.where(n == 1, 3, jnp.where(n == 2, 1, jnp.where(n == 3, 2, 0)))


def one_hot(flip):
    y, zh, x = lax.axis_index("y"), lax.axis_index("zh"), lax.axis_index("x")
    half = jnp.bitwise_xor(zh, flip)
    col = lax.broadcasted_iota(jnp.int32, (1, WIDE_A), 1)
    s, r = col // SHARD_A, col % SHARD_A
    yy, xx = (y + rel_of(s // 4)) % NY, (x + rel_of(s % 4)) % NX
    a = jnp.where(r < HALF_A, ((yy * NZH + half) * NX + xx) * ROWS + r, -1)
    col = lax.broadcasted_iota(jnp.int32, (1, WIDE_B), 1)
    s, r = col // SHARD_B, col % SHARD_B
    yy, xx = (y + rel_of(s % 4)) % NY, (x + rel_of(s // 4)) % NX
    b = jnp.where(r < HALF_B, ((yy * NZH + half) * NX + xx) * ROWS + HALF_A + r, -1)
    origin = jnp.concatenate([a, b], axis=1)
    rows = lax.broadcasted_iota(jnp.int32, (GROUPS * ROWS, WIDE), 0)
    return (rows == origin).astype(F32).astype(BF16)


def spread_kernel(cot, mine, partner):
    flip = pl.program_id(0)
    out = jnp.dot(cot[...], one_hot(flip), preferred_element_type=F32).astype(BF16)

    @pl.when(flip == 0)
    def _():
        mine[...] = out

    @pl.when(flip == 1)
    def _():
        partner[...] = out


def collect_kernel(mine, partner, out, acc):
    flip = pl.program_id(0)
    source = jnp.where(flip == 0, mine[...], partner[...])
    dims = (((1,), (1,)), ((), ()))
    part = lax.dot_general(source, one_hot(flip), dims, preferred_element_type=F32)

    @pl.when(flip == 0)
    def _():
        acc[...] = part

    @pl.when(flip == 1)
    def _():
        out[...] = (acc[...] + part).astype(BF16)


def join_kernel(own, other, out):
    c, zh = lax.axis_index("core"), lax.axis_index("zh")
    for t in range(2):
        first = jnp.bitwise_xor(zh, t) * NZL
        for zl in range(NZL):
            rows = slice(t * TOK, (t + 1) * TOK)
            mine = pl.multiple_of((zl * NC + c) * SLICE, SLICE)
            theirs = pl.multiple_of((zl * NC + 1 - c) * SLICE, SLICE)
            out[rows, pl.ds(mine, SLICE)] = own[first + zl]
            out[rows, pl.ds(theirs, SLICE)] = other[first + zl]


def gating(gu, cot, shard, half):
    width = gu.shape[1]
    gate = gu
    up = pltpu.roll(gu, width - half, 1)
    sig = jax.nn.sigmoid(gate)
    act = gate * sig
    d_up = cot * act
    d_gate = cot * up * sig * (1.0 + gate * (1.0 - sig))
    first = lax.broadcasted_iota(jnp.int32, gu.shape, 1) % shard < half
    hidden = jnp.where(first, act * up, 0.0)
    both = jnp.where(first, d_gate, pltpu.roll(d_up, half, 1))
    return hidden.astype(BF16), both.astype(BF16)


def forward_kernel(shard, half, lower, x, cot_mine, cot_partner, *refs):
    w_refs, before = refs[:8], refs[8:-4]
    hidden_mine, hidden_partner, dd, acc = refs[-4:]
    step = pl.program_id(0)

    @pl.when(step == 0)
    def _():
        acc[...] = jnp.zeros_like(acc)

    dims = (((1,), (1,)), ((), ()))
    w = jnp.concatenate([r[...] for r in w_refs], axis=0)
    acc[...] += lax.dot_general(x[...], w, dims, preferred_element_type=F32)

    @pl.when(step == pl.num_programs(0) - 1)
    def _():
        width = acc.shape[1]
        for old, new in zip(before, (hidden_mine, hidden_partner)):
            new[:, :lower] = old[...]
        for rows, cot, hidden in (
            (slice(0, TOK), cot_mine, hidden_mine),
            (slice(TOK, 2 * TOK), cot_partner, hidden_partner),
        ):
            back = cot[:, lower : lower + width].astype(F32)
            h, dd[rows, :] = gating(acc[rows, :], back, shard, half)
            hidden[:, lower : lower + width] = h


def weight_grad_kernel(dd, x, *outs):
    g = lax.dot_general(dd[...], x[...], (((0,), (0,)), ((), ())), preferred_element_type=F32)
    n = outs[0].shape[0]
    for i, out in enumerate(outs):
        out[...] = g[i * n : (i + 1) * n].astype(BF16)


def token_grad_kernel(dd_a, dd_b, *refs):
    w_refs = refs[:16]
    own, other = refs[16:]
    mine = lax.axis_index("core")
    dims = (((1,), (0,)), ((), ()))
    dd = jnp.concatenate([dd_a[...], dd_b[...]], axis=1)
    c = pl.program_id(1)
    cols = pl.ds(pl.multiple_of(c * SLICE, SLICE), SLICE)
    w = jnp.concatenate([r[:, cols] for r in w_refs], axis=0)
    p = lax.dot_general(dd, w, dims, preferred_element_type=F32).astype(BF16)
    p = p.reshape(2, 1, TOK, SLICE)

    @pl.when(mine == c)
    def _():
        own[...] = p

    @pl.when(mine != c)
    def _():
        other[...] = p


def pair_sum_kernel(own, other, out):
    zh = lax.axis_index("zh")
    for t in range(2):
        first = jnp.bitwise_xor(zh, t) * NZL
        for zl in range(NZL):
            s = t * NZL + zl
            out[first + zl] = (own[s].astype(F32) + other[s].astype(F32)).astype(BF16)


def total_kernel(parts, out):
    total = parts[0].astype(F32)
    for n in range(1, NZ):
        total = total + parts[n].astype(F32)
    out[...] = total.astype(BF16)


def relay_kernel(left, right, from_right, from_left, left_out, right_out):
    left_out[...] = (left[...].astype(F32) + from_right[...].astype(F32)).astype(BF16)
    right_out[...] = (right[...].astype(F32) + from_left[...].astype(F32)).astype(BF16)


def stage_kernel(own_lo, own_hi, r_lo, r_hi, l_lo, l_hi, *outs):
    rows = own_lo.shape[0] // 2
    lo = own_lo[...].astype(F32) + r_lo[...].astype(F32) + l_lo[...].astype(F32)
    hi = own_hi[...].astype(F32) + r_hi[...].astype(F32) + l_hi[...].astype(F32)
    outs[0][...] = lo[:rows].astype(BF16)
    outs[1][...] = lo[rows:].astype(BF16)
    outs[2][...] = hi[:rows].astype(BF16)
    outs[3][...] = hi[rows:].astype(BF16)


def finish_kernel(*refs):
    a, b, gate, up = refs[:4], refs[4:8], refs[8], refs[9]
    ta = sum(r[...].astype(F32) for r in a) * (1.0 / GROUPS)
    tb = sum(r[...].astype(F32) for r in b) * (1.0 / GROUPS)
    gate[...] = jnp.concatenate([ta[:HALF_A], tb[:HALF_B]], axis=0)
    up[...] = jnp.concatenate([ta[HALF_A:], tb[HALF_B:]], axis=0)


def gather_plane(shard, first, second):
    near = [shard] + [shift(shard, **{first: -r}) for r in REL[1:]]
    two = shape(2 * shard.shape[0], D)
    lo = call(pair_kernel, two, 4)(*near[:2])
    hi = call(pair_kernel, two, 4)(*near[2:])
    left_lo = shift(lo, **{second: 1})
    right_lo = shift(lo, **{second: -1})
    left_hi = shift(hi, **{second: 1})
    right_hi = shift(hi, **{second: -1})
    far_lo = shift(left_lo, **{second: 1})
    far_hi = shift(right_hi, **{second: -1})
    return [lo, hi, left_lo, left_hi, right_lo, right_hi, far_lo, far_hi]


def reduce_plane(parts, first, second):
    own_lo, own_hi, left_lo, left_hi, right_lo, right_hi, far_lo, far_hi = parts
    n = far_lo.shape[0]
    from_right = shift(far_lo, **{second: -1})
    from_left = shift(far_hi, **{second: 1})
    r_hi = shift(left_hi, **{second: -1})
    l_lo = shift(right_lo, **{second: 1})
    left_lo, right_hi = call(relay_kernel, (shape(n, D), shape(n, D)))(
        left_lo, right_hi, from_right, from_left
    )
    r_lo = shift(left_lo, **{second: -1})
    l_hi = shift(right_hi, **{second: 1})
    pieces = call(stage_kernel, tuple(shape(n // 2, D) for _ in REL))(
        own_lo, own_hi, r_lo, r_hi, l_lo, l_hi
    )
    return [pieces[0]] + [shift(p, **{first: r}) for p, r in zip(pieces[1:], REL[1:])]


def body(tokens, gate_codes, gate_scales, up_codes, up_scales, cotangent):
    sources = (gate_codes, gate_scales.T, up_codes, up_scales.T)
    shard_a, shard_b = call(
        dequant_kernel,
        (shape(SHARD_A, D), shape(SHARD_B, D)),
        56,
        in_specs=[pl.BlockSpec(memory_space=pltpu.HBM)] * 4,
        out_specs=(VMEM, VMEM),
        scratch_shapes=[pltpu.VMEM(v.shape, v.dtype) for v in sources]
        + [pltpu.SemaphoreType.DMA((4,))],
    )(*sources)
    wa = gather_plane(shard_a, "dx", "dy")
    wb = gather_plane(shard_b, "dy", "dx")

    cube_shape = jax.ShapeDtypeStruct((NZ, TOK, SLICE), BF16)
    copies = call(copies_kernel, cube_shape, 4)(tokens)
    mine = exchange_z(copies)
    theirs = shift(mine, dc=1)
    whole = call(join_kernel, shape(2 * TOK, D), 8)(mine, theirs)

    def full(*dims):
        return pl.BlockSpec(dims, lambda *_: (0,) * len(dims))

    cot_mine, cot_sent = call(
        spread_kernel,
        (shape(TOK, WIDE), shape(TOK, WIDE)),
        grid=(2,),
        in_specs=[full(TOK, GROUPS * ROWS)],
        out_specs=(full(TOK, WIDE), full(TOK, WIDE)),
    )(cotangent)
    cot_partner = shift(cot_sent, dz=4)

    chunk = 512
    grid = (D // chunk,)

    def cols(rows, width=chunk):
        return pl.BlockSpec((rows, width), lambda j, *_: (0, j))

    def forward(w, half, lower, *before):
        shard = 2 * half
        width = 16 * shard
        total = lower + width
        return call(
            functools.partial(forward_kernel, shard, half, lower),
            (shape(TOK, total), shape(TOK, total), shape(2 * TOK, width)),
            grid=grid,
            in_specs=[cols(2 * TOK), full(TOK, WIDE), full(TOK, WIDE)]
            + [cols(p.shape[0]) for p in w]
            + [full(*p.shape) for p in before],
            out_specs=(full(TOK, total), full(TOK, total), full(2 * TOK, width)),
            scratch_shapes=[pltpu.VMEM((2 * TOK, width), F32)],
        )(whole, cot_mine, cot_partner, *w, *before)

    def weight_grad(dd, parts):
        return call(
            weight_grad_kernel,
            tuple(shape(p.shape[0], D) for p in parts),
            grid=grid,
            in_specs=[full(*dd.shape), cols(2 * TOK)],
            out_specs=tuple(cols(p.shape[0]) for p in parts),
        )(dd, whole)

    hm_a, hp_a, dd_a = forward(wa, HALF_A, 0)
    hidden_mine, hidden_sent, dd_b = forward(wb, HALF_B, WIDE_A, hm_a, hp_a)
    sums_a = reduce_plane(weight_grad(dd_a, wa), "dx", "dy")
    sums_b = reduce_plane(weight_grad(dd_b, wb), "dy", "dx")
    gate_grad, up_grad = call(
        finish_kernel, (shape(ROWS, D, F32), shape(ROWS, D, F32))
    )(*sums_a, *sums_b)

    quad = pl.BlockSpec((2, 1, TOK, SLICE), lambda j, c: (0, j, 0, 0))
    quad_shape = jax.ShapeDtypeStruct((2, NZL, TOK, SLICE), BF16)
    own_tg, other_tg = call(
        token_grad_kernel,
        (quad_shape, quad_shape),
        megabytes=24,
        grid=(NZL, NC),
        in_specs=[full(2 * TOK, WIDE_A), full(2 * TOK, WIDE_B)]
        + [cols(w.shape[0], NC * SLICE) for w in wa + wb],
        out_specs=(quad, quad),
    )(dd_a, dd_b, *wa, *wb)
    cube = (NZ, TOK, SLICE)
    received = shift(other_tg, dc=1)
    blocks = call(pair_sum_kernel, cube_shape, 8)(
        own_tg.reshape(cube), received.reshape(cube)
    )
    token_grad = call(total_kernel, shape(TOK, SLICE))(exchange_z(blocks))

    hidden = call(
        collect_kernel,
        shape(TOK, GROUPS * ROWS),
        grid=(2,),
        in_specs=[full(TOK, WIDE), full(TOK, WIDE)],
        out_specs=full(TOK, GROUPS * ROWS),
        scratch_shapes=[pltpu.VMEM((TOK, GROUPS * ROWS), F32)],
    )(hidden_mine, shift(hidden_sent, dz=4))
    return hidden, token_grad, gate_grad, up_grad


def solution(mesh):
    fine = Mesh(mesh.devices.reshape(NY, NZH, NX, NZL, NC), AXES)
    inter, intra = ("y", "zh", "x"), ("zl", "core")
    rows, toks = P(intra + inter, None), P(inter, intra)
    return jax.shard_map(
        body,
        mesh=fine,
        in_specs=(toks, rows, rows, rows, rows, toks),
        out_specs=(toks, toks, rows, rows),
        check_vma=False,
    )
```

profile of v0, /device:TPU:1, one launch (start us, length us, event | category | flops | bytes accessed | tf_op | source)
XLA Modules:
  0.0 187.8 jit_solution(14656421083023316572)
XLA Ops:
  2.6 9.0 %all-to-all-start = ((bf16[8,128,512]{2,1,0:T(8,128)(2,1)}), bf16[8,128,512]{2,1,0:T(8,128)(2,1)S(1)}, u32[]{:S(2)}, u32[]{:S(2)}) async-start(bf16[8,128,512]{2,1,0:T(8,128)(2,1)} %shard_map.93), calls=%async_computation | async-start | bytes 2097152 | tf_op jit(solution)/shard_map/all_to_all | solution.py:46
  11.6 2.2 %shard_map.96 = (bf16[32,4096]{1,0:T(8,128)(2,1)}, bf16[24,4096]{1,0:T(8,128)(2,1)}) custom-call(bf16[28,4096]{1,0:T(8,128)(2,1)} %refs_0_.1, f32[16,28]{1,0:T(8,128)} %bitcast.6, bf16[28,4096]{1,0:T(8,128)(2,1)} %refs_2_.1, f32[16,28]{1,0:T(8,128)} %bitcast.7), custom_call_target="tpu_custom_call" | custom-call | tf_op jit(solution)/shard_map/pallas_call | solution.py:297
  22.2 2.9 %collective-permute-start.4 = (bf16[24,4096]{1,0:T(8,128)(2,1)}, bf16[24,4096]{1,0:T(8,128)(2,1)}, u32[]{:S(2)}, u32[]{:S(2)}) collective-permute-start(bf16[24,4096]{1,0:T(8,128)(2,1)} %get-tuple-element.48.first), channel_id=1, source_target_pairs={{0,128},{1,129},{2,130},{3,131},{4,132},{5,133},{6,134},{7,135},{8... | collective-permute-start | bytes 589832 | tf_op jit(solution)/shard_map/ppermute | solution.py:42
  26.6 14.2 %all-to-all-done.own = bf16[8,128,512]{2,1,0:T(8,128)(2,1)S(1)} async-done(((bf16[8,128,512]{2,1,0:T(8,128)(2,1)}), bf16[8,128,512]{2,1,0:T(8,128)(2,1)S(1)}, u32[]{:S(2)}, u32[]{:S(2)}) %all-to-all-start) | async-done | bytes 1048608 | tf_op jit(solution)/shard_map/all_to_all | solution.py:46
  47.6 12.2 %collective-permute-done.1.cot_partner = bf16[128,896]{1,0:T(8,128)(2,1)S(1)} collective-permute-done((bf16[128,896]{1,0:T(8,128)(2,1)S(1)}, bf16[128,896]{1,0:T(8,128)(2,1)S(1)}, u32[]{:S(2)}, u32[]{:S(2)}) %collective-permute-start.1) | collective-permute-done | bytes 229408 | tf_op jit(solution)/shard_map/ppermute | solution.py:42
  59.8 2.8 %collective-permute-start.17 = (bf16[64,4096]{1,0:T(8,128)(2,1)S(1)}, bf16[64,4096]{1,0:T(8,128)(2,1)S(1)}, u32[]{:S(2)}, u32[]{:S(2)}) collective-permute-start(bf16[64,4096]{1,0:T(8,128)(2,1)S(1)} %shard_map.100.refs_1_), channel_id=1, source_target_pairs={{0,192},{1,193},{2,194},{3,195},{4,196},{5,197},{6,198},{7,199},{8... | collective-permute-start | bytes 1572872 | tf_op jit(solution)/shard_map/ppermute | solution.py:42
  62.6 2.7 %collective-permute-start.16 = (bf16[64,4096]{1,0:T(8,128)(2,1)S(1)}, bf16[64,4096]{1,0:T(8,128)(2,1)S(1)}, u32[]{:S(2)}, u32[]{:S(2)}) collective-permute-start(bf16[64,4096]{1,0:T(8,128)(2,1)S(1)} %shard_map.99.refs_0_), channel_id=1, source_target_pairs={{0,192},{1,193},{2,194},{3,195},{4,196},{5,197},{6,198},{7,199},{8... | collective-permute-start | bytes 1572872 | tf_op jit(solution)/shard_map/ppermute | solution.py:42
  65.3 6.9 %collective-permute-done.17.refs_5_ = bf16[64,4096]{1,0:T(8,128)(2,1)S(1)} collective-permute-done((bf16[64,4096]{1,0:T(8,128)(2,1)S(1)}, bf16[64,4096]{1,0:T(8,128)(2,1)S(1)}, u32[]{:S(2)}, u32[]{:S(2)}) %collective-permute-start.17) | collective-permute-done | bytes 524320 | tf_op jit(solution)/shard_map/ppermute | solution.py:42
  72.2 3.4 %collective-permute-start.19 = (bf16[64,4096]{1,0:T(8,128)(2,1)S(1)}, bf16[64,4096]{1,0:T(8,128)(2,1)S(1)}, u32[]{:S(2)}, u32[]{:S(2)}) collective-permute-start(bf16[64,4096]{1,0:T(8,128)(2,1)S(1)} %collective-permute-done.17.refs_5_), channel_id=1, source_target_pairs={{0,192},{1,193},{2,194},{3,195},{4,196},{5,197},{6,198},{7,199},{8... | collective-permute-start | bytes 1572872 | tf_op jit(solution)/shard_map/ppermute | solution.py:42
  75.7 7.8 %collective-permute-done.16.refs_4_ = bf16[64,4096]{1,0:T(8,128)(2,1)S(1)} collective-permute-done((bf16[64,4096]{1,0:T(8,128)(2,1)S(1)}, bf16[64,4096]{1,0:T(8,128)(2,1)S(1)}, u32[]{:S(2)}, u32[]{:S(2)}) %collective-permute-start.16) | collective-permute-done | bytes 524320 | tf_op jit(solution)/shard_map/ppermute | solution.py:42
  86.6 2.6 %collective-permute-start.10 = (bf16[48,4096]{1,0:T(8,128)(2,1)S(1)}, bf16[48,4096]{1,0:T(8,128)(2,1)S(1)}, u32[]{:S(2)}, u32[]{:S(2)}) collective-permute-start(bf16[48,4096]{1,0:T(8,128)(2,1)S(1)} %collective-permute-done.8.refs_5_.refs_13_), channel_id=1, source_target_pairs={{0,24},{1,25},{2,26},{3,27},{4,28},{5,29},{6,30},{7,31},{8,0},{9,1... | collective-permute-start | bytes 1179656 | tf_op jit(solution)/shard_map/ppermute | solution.py:42
  90.6 4.0 %collective-permute-done.19.refs_7_ = bf16[64,4096]{1,0:T(8,128)(2,1)S(1)} collective-permute-done((bf16[64,4096]{1,0:T(8,128)(2,1)S(1)}, bf16[64,4096]{1,0:T(8,128)(2,1)S(1)}, u32[]{:S(2)}, u32[]{:S(2)}) %collective-permute-start.19) | collective-permute-done | bytes 524320 | tf_op jit(solution)/shard_map/ppermute | solution.py:42
  94.7 3.8 %shard_map.101 = (bf16[128,512]{1,0:T(8,128)(2,1)S(1)}, bf16[128,512]{1,0:T(8,128)(2,1)S(1)}, bf16[256,512]{1,0:T(8,128)(2,1)S(1)}) custom-call(bf16[256,4096]{1,0:T(8,128)(2,1)S(1)} %shard_map.94.x, bf16[128,896]{1,0:T(8,128)(2,1)S(1)} %get-tuple-element.46.cot_mine, bf16[128,896]{1,0:T(8,128)(2,1)S(1)} %collective-permute-done.1.cot_partner, ...), custom_call_target="tpu_custom_call" | custom-call | tf_op jit(solution)/shard_map/pallas_call | solution.py:337
  98.5 3.6 %shard_map.102 = (bf16[128,896]{1,0:T(8,128)(2,1)S(1)}, bf16[128,896]{1,0:T(8,128)(2,1)S(1)}, bf16[256,384]{1,0:T(8,128)(2,1)S(1)}) custom-call(bf16[256,4096]{1,0:T(8,128)(2,1)S(1)} %shard_map.94.x, bf16[128,896]{1,0:T(8,128)(2,1)S(1)} %get-tuple-element.46.cot_mine, bf16[128,896]{1,0:T(8,128)(2,1)S(1)} %collective-permute-done.1.cot_partner, ...), custom_call_target="tpu_custom_call" | custom-call | tf_op jit(solution)/shard_map/pallas_call | solution.py:337
  102.2 5.0 %shard_map.104 = (bf16[2,4,128,512]{3,2,1,0:T(8,128)(2,1)S(1)}, bf16[2,4,128,512]{3,2,1,0:T(8,128)(2,1)S(1)}) custom-call(bf16[256,512]{1,0:T(8,128)(2,1)S(1)} %get-tuple-element.54.dd_a.dd, bf16[256,384]{1,0:T(8,128)(2,1)S(1)} %get-tuple-element.55.dd_b.dd, bf16[64,4096]{1,0:T(8,128)(2,1)S(1)} %shard_map.99.refs_0_, ...), custom_call_target="tpu_custom_call" | custom-call | tf_op jit(solution)/shard_map/pallas_call | solution.py:367
  107.3 4.9 %collective-permute-start.21 = (bf16[2,4,128,512]{3,2,1,0:T(8,128)(2,1)S(1)}, bf16[2,4,128,512]{3,2,1,0:T(8,128)(2,1)S(1)}, u32[]{:S(2)}, u32[]{:S(2)}) collective-permute-start(bf16[2,4,128,512]{3,2,1,0:T(8,128)(2,1)S(1)} %get-tuple-element.57), channel_id=1, source_target_pairs={{0,1},{1,0},{2,3},{3,2},{4,5},{5,4},{6,7},{7,6},{8,9},{9,8},{10,11... | collective-permute-start | bytes 3145736 | tf_op jit(solution)/shard_map/ppermute | solution.py:42
  112.2 2.3 %collective-permute-done.21 = bf16[2,4,128,512]{3,2,1,0:T(8,128)(2,1)S(1)} collective-permute-done((bf16[2,4,128,512]{3,2,1,0:T(8,128)(2,1)S(1)}, bf16[2,4,128,512]{3,2,1,0:T(8,128)(2,1)S(1)}, u32[]{:S(2)}, u32[]{:S(2)}) %collective-permute-start.21) | collective-permute-done | bytes 1048608 | tf_op jit(solution)/shard_map/ppermute | solution.py:42
  115.7 6.2 %all-to-all-start.1 = ((bf16[8,128,512]{2,1,0:T(8,128)(2,1)}), bf16[8,128,512]{2,1,0:T(8,128)(2,1)S(1)}, u32[]{:S(2)}, u32[]{:S(2)}) async-start(bf16[8,128,512]{2,1,0:T(8,128)(2,1)} %shard_map.105), calls=%async_computation.1 | async-start | bytes 2097152 | tf_op jit(solution)/shard_map/all_to_all | solution.py:46
  122.8 2.8 %shard_map.110 = (bf16[48,4096]{1,0:T(8,128)(2,1)S(1)}, bf16[48,4096]{1,0:T(8,128)(2,1)S(1)}, bf16[48,4096]{1,0:T(8,128)(2,1)S(1)}, bf16[48,4096]{1,0:T(8,128)(2...) custom-call(bf16[256,384]{1,0:T(8,128)(2,1)S(1)} %copy-done.3, ...), custom_call_target="tpu_custom_call" | custom-call | tf_op jit(solution)/shard_map/pallas_call | solution.py:349
  125.6 2.5 %collective-permute-start.31 = (bf16[48,4096]{1,0:T(8,128)(2,1)S(1)}, bf16[48,4096]{1,0:T(8,128)(2,1)S(1)}, u32[]{:S(2)}, u32[]{:S(2)}) collective-permute-start(bf16[48,4096]{1,0:T(8,128)(2,1)S(1)} %get-tuple-element.76), channel_id=1, source_target_pairs={{0,24},{1,25},{2,26},{3,27},{4,28},{5,29},{6,30},{7,31},{8,0},{9,1... | collective-permute-start | bytes 1179656 | tf_op jit(solution)/shard_map/ppermute | solution.py:42
  128.2 3.1 %shard_map.107 = (bf16[64,4096]{1,0:T(8,128)(2,1)S(1)}, bf16[64,4096]{1,0:T(8,128)(2,1)S(1)}, bf16[64,4096]{1,0:T(8,128)(2,1)S(1)}, bf16[64,4096]{1,0:T(8,128)(2...) custom-call(bf16[256,512]{1,0:T(8,128)(2,1)S(1)} %get-tuple-element., ...), custom_call_target="tpu_custom_call" | custom-call | tf_op jit(solution)/shard_map/pallas_call | solution.py:349
  131.3 3.5 %collective-permute-start.22 = (bf16[64,4096]{1,0:T(8,128)(2,1)S(1)}, bf16[64,4096]{1,0:T(8,128)(2,1)S(1)}, u32[]{:S(2)}, u32[]{:S(2)}) collective-permute-start(bf16[64,4096]{1,0:T(8,128)(2,1)S(1)} %get-tuple-element.62), channel_id=1, source_target_pairs={{0,192},{1,193},{2,194},{3,195},{4,196},{5,197},{6,198},{7,199},{8... | collective-permute-start | bytes 1572872 | tf_op jit(solution)/shard_map/ppermute | solution.py:42
  134.8 2.7 %collective-permute-start.34 = (bf16[48,4096]{1,0:T(8,128)(2,1)S(1)}, bf16[48,4096]{1,0:T(8,128)(2,1)S(1)}, u32[]{:S(2)}, u32[]{:S(2)}) collective-permute-start(bf16[48,4096]{1,0:T(8,128)(2,1)S(1)} %get-tuple-element.79), channel_id=1, source_target_pairs={{0,24},{1,25},{2,26},{3,27},{4,28},{5,29},{6,30},{7,31},{8,0},{9,1... | collective-permute-start | bytes 1179656 | tf_op jit(solution)/shard_map/ppermute | solution.py:42
  140.6 4.5 %collective-permute-done.22.from_right = bf16[64,4096]{1,0:T(8,128)(2,1)S(1)} collective-permute-done((bf16[64,4096]{1,0:T(8,128)(2,1)S(1)}, bf16[64,4096]{1,0:T(8,128)(2,1)S(1)}, u32[]{:S(2)}, u32[]{:S(2)}) %collective-permute-start.22) | collective-permute-done | bytes 524320 | tf_op jit(solution)/shard_map/ppermute | solution.py:42
  145.1 3.4 %collective-permute-start.25 = (bf16[64,4096]{1,0:T(8,128)(2,1)S(1)}, bf16[64,4096]{1,0:T(8,128)(2,1)S(1)}, u32[]{:S(2)}, u32[]{:S(2)}) collective-permute-start(bf16[64,4096]{1,0:T(8,128)(2,1)S(1)} %get-tuple-element.65), channel_id=1, source_target_pairs={{0,192},{1,193},{2,194},{3,195},{4,196},{5,197},{6,198},{7,199},{8... | collective-permute-start | bytes 1572872 | tf_op jit(solution)/shard_map/ppermute | solution.py:42
  148.9 2.7 %collective-permute-start.24 = (bf16[64,4096]{1,0:T(8,128)(2,1)S(1)}, bf16[64,4096]{1,0:T(8,128)(2,1)S(1)}, u32[]{:S(2)}, u32[]{:S(2)}) collective-permute-start(bf16[64,4096]{1,0:T(8,128)(2,1)S(1)} %get-tuple-element.64), channel_id=1, source_target_pairs={{0,192},{1,193},{2,194},{3,195},{4,196},{5,197},{6,198},{7,199},{8... | collective-permute-start | bytes 1572872 | tf_op jit(solution)/shard_map/ppermute | solution.py:42
  153.5 4.9 %collective-permute-done.36.l_hi = bf16[48,4096]{1,0:T(8,128)(2,1)S(1)} collective-permute-done((bf16[48,4096]{1,0:T(8,128)(2,1)S(1)}, bf16[48,4096]{1,0:T(8,128)(2,1)S(1)}, u32[]{:S(2)}, u32[]{:S(2)}) %collective-permute-start.36) | collective-permute-done | bytes 393248 | tf_op jit(solution)/shard_map/ppermute | solution.py:42
  158.4 4.8 %collective-permute-start.20 = (bf16[128,896]{1,0:T(8,128)(2,1)S(1)}, bf16[128,896]{1,0:T(8,128)(2,1)S(1)}, u32[]{:S(2)}, u32[]{:S(2)}) collective-permute-start(bf16[128,896]{1,0:T(8,128)(2,1)S(1)} %copy-done.11), channel_id=1, source_target_pairs={{0,32},{1,33},{2,34},{3,35},{4,36},{5,37},{6,38},{7,39},{8,40},{9,... | collective-permute-start | bytes 688136 | tf_op jit(solution)/shard_map/ppermute | solution.py:42
  164.4 4.9 %collective-permute-done.24.r_lo = bf16[64,4096]{1,0:T(8,128)(2,1)S(1)} collective-permute-done((bf16[64,4096]{1,0:T(8,128)(2,1)S(1)}, bf16[64,4096]{1,0:T(8,128)(2,1)S(1)}, u32[]{:S(2)}, u32[]{:S(2)}) %collective-permute-start.24) | collective-permute-done | bytes 524320 | tf_op jit(solution)/shard_map/ppermute | solution.py:42
  169.3 3.5 %collective-permute-done.27.l_hi = bf16[64,4096]{1,0:T(8,128)(2,1)S(1)} collective-permute-done((bf16[64,4096]{1,0:T(8,128)(2,1)S(1)}, bf16[64,4096]{1,0:T(8,128)(2,1)S(1)}, u32[]{:S(2)}, u32[]{:S(2)}) %collective-permute-start.27) | collective-permute-done | bytes 524320 | tf_op jit(solution)/shard_map/ppermute | solution.py:42
  173.1 2.5 %collective-permute-start.28 = (bf16[32,4096]{1,0:T(8,128)(2,1)S(1)}, bf16[32,4096]{1,0:T(8,128)(2,1)S(1)}, u32[]{:S(2)}, u32[]{:S(2)}) collective-permute-start(bf16[32,4096]{1,0:T(8,128)(2,1)S(1)} %get-tuple-element.69), channel_id=1, source_target_pairs={{0,24},{1,25},{2,26},{3,27},{4,28},{5,29},{6,30},{7,31},{8,0},{9,1... | collective-permute-start | bytes 786440 | tf_op jit(solution)/shard_map/ppermute | solution.py:42
  180.2 5.7 %collective-permute-done.38.refs_6_ = bf16[24,4096]{1,0:T(8,128)(2,1)S(1)} collective-permute-done((bf16[24,4096]{1,0:T(8,128)(2,1)S(1)}, bf16[24,4096]{1,0:T(8,128)(2,1)S(1)}, u32[]{:S(2)}, u32[]{:S(2)}) %collective-permute-start.38) | collective-permute-done | bytes 196640 | tf_op jit(solution)/shard_map/ppermute | solution.py:42
  (97 shorter events, 39.0 us)
Async XLA Ops:
  2.6 38.2 %all-to-all-start = ((bf16[8,128,512]{2,1,0:T(8,128)(2,1)}), bf16[8,128,512]{2,1,0:T(8,128)(2,1)S(1)}, u32[]{:S(2)}, u32[]{:S(2)}) async-start(bf16[8,128,512]{2,1,0:T(8,128)(2,1)} %shard_map.93), calls=%async_computation | async-start | bytes 2097152 | tf_op jit(solution)/shard_map/all_to_all | solution.py:46
  17.9 26.7 %collective-permute-start.12 = (bf16[32,4096]{1,0:T(8,128)(2,1)}, bf16[32,4096]{1,0:T(8,128)(2,1)S(1)}, u32[]{:S(2)}, u32[]{:S(2)}) collective-permute-start(bf16[32,4096]{1,0:T(8,128)(2,1)} %get-tuple-element.49.first), channel_id=1, source_target_pairs={{0,24},{1,25},{2,26},{3,27},{4,28},{5,29},{6,30},{7,31},{8,0},{9,1... | collective-permute-start | bytes 786440 | tf_op jit(solution)/shard_map/ppermute | solution.py:42
  19.3 27.9 %collective-permute-start.13 = (bf16[32,4096]{1,0:T(8,128)(2,1)}, bf16[32,4096]{1,0:T(8,128)(2,1)S(1)}, u32[]{:S(2)}, u32[]{:S(2)}) collective-permute-start(bf16[32,4096]{1,0:T(8,128)(2,1)} %get-tuple-element.49.first), channel_id=1, source_target_pairs={{0,16},{1,17},{2,18},{3,19},{4,20},{5,21},{6,22},{7,23},{8,24},{9,... | collective-permute-start | bytes 786440 | tf_op jit(solution)/shard_map/ppermute | solution.py:42
  22.2 20.0 %collective-permute-start.4 = (bf16[24,4096]{1,0:T(8,128)(2,1)}, bf16[24,4096]{1,0:T(8,128)(2,1)}, u32[]{:S(2)}, u32[]{:S(2)}) collective-permute-start(bf16[24,4096]{1,0:T(8,128)(2,1)} %get-tuple-element.48.first), channel_id=1, source_target_pairs={{0,128},{1,129},{2,130},{3,131},{4,132},{5,133},{6,134},{7,135},{8... | collective-permute-start | bytes 589832 | tf_op jit(solution)/shard_map/ppermute | solution.py:42
  26.2 39.1 %collective-permute-start.14 = (bf16[64,4096]{1,0:T(8,128)(2,1)S(1)}, bf16[64,4096]{1,0:T(8,128)(2,1)S(1)}, u32[]{:S(2)}, u32[]{:S(2)}) collective-permute-start(bf16[64,4096]{1,0:T(8,128)(2,1)S(1)} %shard_map.99.refs_0_), channel_id=1, source_target_pairs={{0,64},{1,65},{2,66},{3,67},{4,68},{5,69},{6,70},{7,71},{8,72},{9,... | collective-permute-start | bytes 1572872 | tf_op jit(solution)/shard_map/ppermute | solution.py:42
  40.8 45.8 %collective-permute-start = (bf16[8,128,512]{2,1,0:T(8,128)(2,1)S(1)}, bf16[8,128,512]{2,1,0:T(8,128)(2,1)S(1)}, u32[]{:S(2)}, u32[]{:S(2)}) collective-permute-start(bf16[8,128,512]{2,1,0:T(8,128)(2,1)S(1)} %all-to-all-done.own), channel_id=1, source_target_pairs={{0,1},{1,0},{2,3},{3,2},{4,5},{5,4},{6,7},{7,6},{8,9},{9,8},{10,11... | collective-permute-start | bytes 3145736 | tf_op jit(solution)/shard_map/ppermute | solution.py:42
  42.3 20.3 %collective-permute-start.5 = (bf16[48,4096]{1,0:T(8,128)(2,1)S(1)}, bf16[48,4096]{1,0:T(8,128)(2,1)S(1)}, u32[]{:S(2)}, u32[]{:S(2)}) collective-permute-start(bf16[48,4096]{1,0:T(8,128)(2,1)S(1)} %shard_map.97.refs_0_.refs_8_), channel_id=1, source_target_pairs={{0,8},{1,9},{2,10},{3,11},{4,12},{5,13},{6,14},{7,15},{8,16},{9,17... | collective-permute-start | bytes 1179656 | tf_op jit(solution)/shard_map/ppermute | solution.py:42
  44.5 18.1 %collective-permute-start.8 = (bf16[48,4096]{1,0:T(8,128)(2,1)S(1)}, bf16[48,4096]{1,0:T(8,128)(2,1)S(1)}, u32[]{:S(2)}, u32[]{:S(2)}) collective-permute-start(bf16[48,4096]{1,0:T(8,128)(2,1)S(1)} %shard_map.98.refs_1_.refs_9_), channel_id=1, source_target_pairs={{0,24},{1,25},{2,26},{3,27},{4,28},{5,29},{6,30},{7,31},{8,0},{9,1... | collective-permute-start | bytes 1179656 | tf_op jit(solution)/shard_map/ppermute | solution.py:42
  47.2 12.6 %collective-permute-start.1 = (bf16[128,896]{1,0:T(8,128)(2,1)S(1)}, bf16[128,896]{1,0:T(8,128)(2,1)S(1)}, u32[]{:S(2)}, u32[]{:S(2)}) collective-permute-start(bf16[128,896]{1,0:T(8,128)(2,1)S(1)} %get-tuple-element.47), channel_id=1, source_target_pairs={{0,32},{1,33},{2,34},{3,35},{4,36},{5,37},{6,38},{7,39},{8,40},{9,... | collective-permute-start | bytes 688136 | tf_op jit(solution)/shard_map/ppermute | solution.py:42
  59.8 12.4 %collective-permute-start.17 = (bf16[64,4096]{1,0:T(8,128)(2,1)S(1)}, bf16[64,4096]{1,0:T(8,128)(2,1)S(1)}, u32[]{:S(2)}, u32[]{:S(2)}) collective-permute-start(bf16[64,4096]{1,0:T(8,128)(2,1)S(1)} %shard_map.100.refs_1_), channel_id=1, source_target_pairs={{0,192},{1,193},{2,194},{3,195},{4,196},{5,197},{6,198},{7,199},{8... | collective-permute-start | bytes 1572872 | tf_op jit(solution)/shard_map/ppermute | solution.py:42
  62.6 13.0 %collective-permute-start.15 = (bf16[64,4096]{1,0:T(8,128)(2,1)S(1)}, bf16[64,4096]{1,0:T(8,128)(2,1)S(1)}, u32[]{:S(2)}, u32[]{:S(2)}) collective-permute-start(bf16[64,4096]{1,0:T(8,128)(2,1)S(1)} %shard_map.100.refs_1_), channel_id=1, source_target_pairs={{0,64},{1,65},{2,66},{3,67},{4,68},{5,69},{6,70},{7,71},{8,72},{9,... | collective-permute-start | bytes 1572872 | tf_op jit(solution)/shard_map/ppermute | solution.py:42
  62.6 20.8 %collective-permute-start.16 = (bf16[64,4096]{1,0:T(8,128)(2,1)S(1)}, bf16[64,4096]{1,0:T(8,128)(2,1)S(1)}, u32[]{:S(2)}, u32[]{:S(2)}) collective-permute-start(bf16[64,4096]{1,0:T(8,128)(2,1)S(1)} %shard_map.99.refs_0_), channel_id=1, source_target_pairs={{0,192},{1,193},{2,194},{3,195},{4,196},{5,197},{6,198},{7,199},{8... | collective-permute-start | bytes 1572872 | tf_op jit(solution)/shard_map/ppermute | solution.py:42
  65.3 21.3 %collective-permute-start.18 = (bf16[64,4096]{1,0:T(8,128)(2,1)S(1)}, bf16[64,4096]{1,0:T(8,128)(2,1)S(1)}, u32[]{:S(2)}, u32[]{:S(2)}) collective-permute-start(bf16[64,4096]{1,0:T(8,128)(2,1)S(1)} %collective-permute-done.14.refs_2_), channel_id=1, source_target_pairs={{0,64},{1,65},{2,66},{3,67},{4,68},{5,69},{6,70},{7,71},{8,72},{9,... | collective-permute-start | bytes 1572872 | tf_op jit(solution)/shard_map/ppermute | solution.py:42
  72.2 22.5 %collective-permute-start.19 = (bf16[64,4096]{1,0:T(8,128)(2,1)S(1)}, bf16[64,4096]{1,0:T(8,128)(2,1)S(1)}, u32[]{:S(2)}, u32[]{:S(2)}) collective-permute-start(bf16[64,4096]{1,0:T(8,128)(2,1)S(1)} %collective-permute-done.17.refs_5_), channel_id=1, source_target_pairs={{0,192},{1,193},{2,194},{3,195},{4,196},{5,197},{6,198},{7,199},{8... | collective-permute-start | bytes 1572872 | tf_op jit(solution)/shard_map/ppermute | solution.py:42
  75.6 22.9 %collective-permute-start.6 = (bf16[48,4096]{1,0:T(8,128)(2,1)S(1)}, bf16[48,4096]{1,0:T(8,128)(2,1)S(1)}, u32[]{:S(2)}, u32[]{:S(2)}) collective-permute-start(bf16[48,4096]{1,0:T(8,128)(2,1)S(1)} %shard_map.98.refs_1_.refs_9_), channel_id=1, source_target_pairs={{0,8},{1,9},{2,10},{3,11},{4,12},{5,13},{6,14},{7,15},{8,16},{9,17... | collective-permute-start | bytes 1179656 | tf_op jit(solution)/shard_map/ppermute | solution.py:42
  83.4 15.1 %collective-permute-start.7 = (bf16[48,4096]{1,0:T(8,128)(2,1)S(1)}, bf16[48,4096]{1,0:T(8,128)(2,1)S(1)}, u32[]{:S(2)}, u32[]{:S(2)}) collective-permute-start(bf16[48,4096]{1,0:T(8,128)(2,1)S(1)} %shard_map.97.refs_0_.refs_8_), channel_id=1, source_target_pairs={{0,24},{1,25},{2,26},{3,27},{4,28},{5,29},{6,30},{7,31},{8,0},{9,1... | collective-permute-start | bytes 1179656 | tf_op jit(solution)/shard_map/ppermute | solution.py:42
  86.6 12.0 %collective-permute-start.9 = (bf16[48,4096]{1,0:T(8,128)(2,1)S(1)}, bf16[48,4096]{1,0:T(8,128)(2,1)S(1)}, u32[]{:S(2)}, u32[]{:S(2)}) collective-permute-start(bf16[48,4096]{1,0:T(8,128)(2,1)S(1)} %collective-permute-done.5.refs_2_.refs_10_), channel_id=1, source_target_pairs={{0,8},{1,9},{2,10},{3,11},{4,12},{5,13},{6,14},{7,15},{8,16},{9,17... | collective-permute-start | bytes 1179656 | tf_op jit(solution)/shard_map/ppermute | solution.py:42
  86.6 11.9 %collective-permute-start.10 = (bf16[48,4096]{1,0:T(8,128)(2,1)S(1)}, bf16[48,4096]{1,0:T(8,128)(2,1)S(1)}, u32[]{:S(2)}, u32[]{:S(2)}) collective-permute-start(bf16[48,4096]{1,0:T(8,128)(2,1)S(1)} %collective-permute-done.8.refs_5_.refs_13_), channel_id=1, source_target_pairs={{0,24},{1,25},{2,26},{3,27},{4,28},{5,29},{6,30},{7,31},{8,0},{9,1... | collective-permute-start | bytes 1179656 | tf_op jit(solution)/shard_map/ppermute | solution.py:42
  115.7 71.2 %all-to-all-start.1 = ((bf16[8,128,512]{2,1,0:T(8,128)(2,1)}), bf16[8,128,512]{2,1,0:T(8,128)(2,1)S(1)}, u32[]{:S(2)}, u32[]{:S(2)}) async-start(bf16[8,128,512]{2,1,0:T(8,128)(2,1)} %shard_map.105), calls=%async_computation.1 | async-start | bytes 2097152 | tf_op jit(solution)/shard_map/all_to_all | solution.py:46
  125.6 11.9 %collective-permute-start.31 = (bf16[48,4096]{1,0:T(8,128)(2,1)S(1)}, bf16[48,4096]{1,0:T(8,128)(2,1)S(1)}, u32[]{:S(2)}, u32[]{:S(2)}) collective-permute-start(bf16[48,4096]{1,0:T(8,128)(2,1)S(1)} %get-tuple-element.76), channel_id=1, source_target_pairs={{0,24},{1,25},{2,26},{3,27},{4,28},{5,29},{6,30},{7,31},{8,0},{9,1... | collective-permute-start | bytes 1179656 | tf_op jit(solution)/shard_map/ppermute | solution.py:42
  131.3 13.8 %collective-permute-start.22 = (bf16[64,4096]{1,0:T(8,128)(2,1)S(1)}, bf16[64,4096]{1,0:T(8,128)(2,1)S(1)}, u32[]{:S(2)}, u32[]{:S(2)}) collective-permute-start(bf16[64,4096]{1,0:T(8,128)(2,1)S(1)} %get-tuple-element.62), channel_id=1, source_target_pairs={{0,192},{1,193},{2,194},{3,195},{4,196},{5,197},{6,198},{7,199},{8... | collective-permute-start | bytes 1572872 | tf_op jit(solution)/shard_map/ppermute | solution.py:42
  134.8 13.8 %collective-permute-start.23 = (bf16[64,4096]{1,0:T(8,128)(2,1)S(1)}, bf16[64,4096]{1,0:T(8,128)(2,1)S(1)}, u32[]{:S(2)}, u32[]{:S(2)}) collective-permute-start(bf16[64,4096]{1,0:T(8,128)(2,1)S(1)} %get-tuple-element.63), channel_id=1, source_target_pairs={{0,64},{1,65},{2,66},{3,67},{4,68},{5,69},{6,70},{7,71},{8,72},{9,... | collective-permute-start | bytes 1572872 | tf_op jit(solution)/shard_map/ppermute | solution.py:42
  134.8 14.0 %collective-permute-start.34 = (bf16[48,4096]{1,0:T(8,128)(2,1)S(1)}, bf16[48,4096]{1,0:T(8,128)(2,1)S(1)}, u32[]{:S(2)}, u32[]{:S(2)}) collective-permute-start(bf16[48,4096]{1,0:T(8,128)(2,1)S(1)} %get-tuple-element.79), channel_id=1, source_target_pairs={{0,24},{1,25},{2,26},{3,27},{4,28},{5,29},{6,30},{7,31},{8,0},{9,1... | collective-permute-start | bytes 1179656 | tf_op jit(solution)/shard_map/ppermute | solution.py:42
  137.5 11.4 %collective-permute-start.35 = (bf16[48,4096]{1,0:T(8,128)(2,1)S(1)}, bf16[48,4096]{1,0:T(8,128)(2,1)S(1)}, u32[]{:S(2)}, u32[]{:S(2)}) collective-permute-start(bf16[48,4096]{1,0:T(8,128)(2,1)S(1)} %get-tuple-element.80), channel_id=1, source_target_pairs={{0,8},{1,9},{2,10},{3,11},{4,12},{5,13},{6,14},{7,15},{8,16},{9,17... | collective-permute-start | bytes 1179656 | tf_op jit(solution)/shard_map/ppermute | solution.py:42
  139.3 13.6 %collective-permute-start.33 = (bf16[48,4096]{1,0:T(8,128)(2,1)S(1)}, bf16[48,4096]{1,0:T(8,128)(2,1)S(1)}, u32[]{:S(2)}, u32[]{:S(2)}) collective-permute-start(bf16[48,4096]{1,0:T(8,128)(2,1)S(1)} %get-tuple-element.78), channel_id=1, source_target_pairs={{0,24},{1,25},{2,26},{3,27},{4,28},{5,29},{6,30},{7,31},{8,0},{9,1... | collective-permute-start | bytes 1179656 | tf_op jit(solution)/shard_map/ppermute | solution.py:42
  145.1 18.4 %collective-permute-start.25 = (bf16[64,4096]{1,0:T(8,128)(2,1)S(1)}, bf16[64,4096]{1,0:T(8,128)(2,1)S(1)}, u32[]{:S(2)}, u32[]{:S(2)}) collective-permute-start(bf16[64,4096]{1,0:T(8,128)(2,1)S(1)} %get-tuple-element.65), channel_id=1, source_target_pairs={{0,192},{1,193},{2,194},{3,195},{4,196},{5,197},{6,198},{7,199},{8... | collective-permute-start | bytes 1572872 | tf_op jit(solution)/shard_map/ppermute | solution.py:42
  148.8 15.6 %collective-permute-start.26 = (bf16[64,4096]{1,0:T(8,128)(2,1)S(1)}, bf16[64,4096]{1,0:T(8,128)(2,1)S(1)}, u32[]{:S(2)}, u32[]{:S(2)}) collective-permute-start(bf16[64,4096]{1,0:T(8,128)(2,1)S(1)} %get-tuple-element.66), channel_id=1, source_target_pairs={{0,64},{1,65},{2,66},{3,67},{4,68},{5,69},{6,70},{7,71},{8,72},{9,... | collective-permute-start | bytes 1572872 | tf_op jit(solution)/shard_map/ppermute | solution.py:42
  148.9 20.4 %collective-permute-start.24 = (bf16[64,4096]{1,0:T(8,128)(2,1)S(1)}, bf16[64,4096]{1,0:T(8,128)(2,1)S(1)}, u32[]{:S(2)}, u32[]{:S(2)}) collective-permute-start(bf16[64,4096]{1,0:T(8,128)(2,1)S(1)} %get-tuple-element.64), channel_id=1, source_target_pairs={{0,192},{1,193},{2,194},{3,195},{4,196},{5,197},{6,198},{7,199},{8... | collective-permute-start | bytes 1572872 | tf_op jit(solution)/shard_map/ppermute | solution.py:42
  152.9 19.9 %collective-permute-start.27 = (bf16[64,4096]{1,0:T(8,128)(2,1)S(1)}, bf16[64,4096]{1,0:T(8,128)(2,1)S(1)}, u32[]{:S(2)}, u32[]{:S(2)}) collective-permute-start(bf16[64,4096]{1,0:T(8,128)(2,1)S(1)} %get-tuple-element.67), channel_id=1, source_target_pairs={{0,64},{1,65},{2,66},{3,67},{4,68},{5,69},{6,70},{7,71},{8,72},{9,... | collective-permute-start | bytes 1572872 | tf_op jit(solution)/shard_map/ppermute | solution.py:42
  158.4 19.3 %collective-permute-start.20 = (bf16[128,896]{1,0:T(8,128)(2,1)S(1)}, bf16[128,896]{1,0:T(8,128)(2,1)S(1)}, u32[]{:S(2)}, u32[]{:S(2)}) collective-permute-start(bf16[128,896]{1,0:T(8,128)(2,1)S(1)} %copy-done.11), channel_id=1, source_target_pairs={{0,32},{1,33},{2,34},{3,35},{4,36},{5,37},{6,38},{7,39},{8,40},{9,... | collective-permute-start | bytes 688136 | tf_op jit(solution)/shard_map/ppermute | solution.py:42
  163.5 14.2 %collective-permute-start.37 = (bf16[24,4096]{1,0:T(8,128)(2,1)S(1)}, bf16[24,4096]{1,0:T(8,128)(2,1)S(1)}, u32[]{:S(2)}, u32[]{:S(2)}) collective-permute-start(bf16[24,4096]{1,0:T(8,128)(2,1)S(1)} %get-tuple-element.83), channel_id=1, source_target_pairs={{0,192},{1,193},{2,194},{3,195},{4,196},{5,197},{6,198},{7,199},{8... | collective-permute-start | bytes 589832 | tf_op jit(solution)/shard_map/ppermute | solution.py:42
  173.1 12.7 %collective-permute-start.28 = (bf16[32,4096]{1,0:T(8,128)(2,1)S(1)}, bf16[32,4096]{1,0:T(8,128)(2,1)S(1)}, u32[]{:S(2)}, u32[]{:S(2)}) collective-permute-start(bf16[32,4096]{1,0:T(8,128)(2,1)S(1)} %get-tuple-element.69), channel_id=1, source_target_pairs={{0,24},{1,25},{2,26},{3,27},{4,28},{5,29},{6,30},{7,31},{8,0},{9,1... | collective-permute-start | bytes 786440 | tf_op jit(solution)/shard_map/ppermute | solution.py:42
  (22 other events, 236.4 us)
where the time goes:
time: 191 us; the launch traced here: 188 us
  waiting for transfers between devices  77 us (40%)
  starting transfers between devices  74.6 us (39%)
  Pallas kernels  30.2 us (16%)
  local copies, waits for them, and re-layouts  4.96 us (3%)
    ppermute x40, waiting for transfers between devices, shift(): return lax.ppermute(value, AXES, pairs)  62.9 us
    ppermute x40, starting transfers between devices, shift(): return lax.ppermute(value, AXES, pairs)  59.4 us
    all_to_all x2, starting transfers between devices, exchange_z(): return lax.all_to_all(value, ('zh', 'zl'), 0, 0, tiled=True)  15.2 us
    all_to_all x2, waiting for transfers between devices, exchange_z(): return lax.all_to_all(value, ('zh', 'zl'), 0, 0, tiled=True)  14.2 us
    pallas_call x2, Pallas kernels, forward(): call(functools.partial(forward_kernel, shard, half, lower), (shape(TOK, t...  7.46 us
    pallas_call x2, Pallas kernels, weight_grad(): call(weight_grad_kernel, tuple((shape(p.shape[0], D) for p in parts)), gr...  5.93 us
    pallas_call x1, Pallas kernels, body(): call(token_grad_kernel, (quad_shape, quad_shape), megabytes=24, grid=(NZL...  5.01 us
    unnamed x24, local copies, waits for them, and re-layouts  4.96 us
  transfers between devices with their start and end apart: 42, of which 15 were waited for; matrix products, arithmetic and copies ran while one was open for 0% of the time, Pallas kernels for 10%

commit v1 on v0

--- a/solution.py
+++ b/solution.py
@@ -10,6 +10,7 @@
 D = 4096
 TOK = 128
 SLICE = 512
+WIDTH = 1024
 ROWS = 28
 BLOCK = 256
 NY, NZH, NX, NZL, NC = 4, 2, 4, 4, 2
@@ -60,6 +61,10 @@
 
 
 VMEM = pl.BlockSpec(memory_space=pltpu.VMEM)
+
+
+def whole_block(*dims):
+    return pl.BlockSpec(dims, lambda n: (0,) * len(dims))
 
 
 def dequant_kernel(*refs):
@@ -112,17 +117,9 @@
     return (rows == origin).astype(F32).astype(BF16)
 
 
-def spread_kernel(cot, mine, partner):
-    flip = pl.program_id(0)
-    out = jnp.dot(cot[...], one_hot(flip), preferred_element_type=F32).astype(BF16)
-
-    @pl.when(flip == 0)
-    def _():
-        mine[...] = out
-
-    @pl.when(flip == 1)
-    def _():
-        partner[...] = out
+def spread_kernel(mine, partner, out):
+    both = jnp.concatenate([mine[...], partner[...]], axis=0)
+    out[...] = jnp.dot(both, one_hot(0), preferred_element_type=F32).astype(BF16)
 
 
 def collect_kernel(mine, partner, out, acc):
@@ -166,59 +163,64 @@
     return hidden.astype(BF16), both.astype(BF16)
 
 
-def forward_kernel(shard, half, lower, x, cot_mine, cot_partner, *refs):
+def chunk(n, width):
+    return pl.ds(pl.multiple_of(n * width, width), width)
+
+
+def forward_kernel(shard, half, lower, x, cot, *refs):
     w_refs, before = refs[:8], refs[8:-4]
     hidden_mine, hidden_partner, dd, acc = refs[-4:]
-    step = pl.program_id(0)
-
-    @pl.when(step == 0)
-    def _():
-        acc[...] = jnp.zeros_like(acc)
-
     dims = (((1,), (1,)), ((), ()))
-    w = jnp.concatenate([r[...] for r in w_refs], axis=0)
-    acc[...] += lax.dot_general(x[...], w, dims, preferred_element_type=F32)
-
-    @pl.when(step == pl.num_programs(0) - 1)
-    def _():
-        width = acc.shape[1]
-        for old, new in zip(before, (hidden_mine, hidden_partner)):
-            new[:, :lower] = old[...]
-        for rows, cot, hidden in (
-            (slice(0, TOK), cot_mine, hidden_mine),
-            (slice(TOK, 2 * TOK), cot_partner, hidden_partner),
-        ):
-            back = cot[:, lower : lower + width].astype(F32)
-            h, dd[rows, :] = gating(acc[rows, :], back, shard, half)
-            hidden[:, lower : lower + width] = h
+    acc[...] = jnp.zeros_like(acc)
+
+    @pl.loop(0, D // WIDTH)
+    def _(n):
+        cols = chunk(n, WIDTH)
+        w = jnp.concatenate([r[:, cols] for r in w_refs], axis=0)
+        acc[...] += lax.dot_general(x[:, cols], w, dims, preferred_element_type=F32)
+
+    width = acc.shape[1]
+    for old, new in zip(before, (hidden_mine, hidden_partner)):
+        new[:, :lower] = old[...]
+    back = cot[:, lower : lower + width].astype(F32)
+    h, dd[...] = gating(acc[...], back, shard, half)
+    hidden_mine[:, lower : lower + width] = h[:TOK]
+    hidden_partner[:, lower : lower + width] = h[TOK:]
 
 
 def weight_grad_kernel(dd, x, *outs):
-    g = lax.dot_general(dd[...], x[...], (((0,), (0,)), ((), ())), preferred_element_type=F32)
+    turned = dd[...].T
     n = outs[0].shape[0]
-    for i, out in enumerate(outs):
-        out[...] = g[i * n : (i + 1) * n].astype(BF16)
+
+    @pl.loop(0, D // WIDTH)
+    def _(m):
+        cols = chunk(m, WIDTH)
+        g = jnp.dot(turned, x[:, cols], preferred_element_type=F32)
+        for i, out in enumerate(outs):
+            out[:, cols] = g[i * n : (i + 1) * n].astype(BF16)
 
 
 def token_grad_kernel(dd_a, dd_b, *refs):
     w_refs = refs[:16]
     own, other = refs[16:]
     mine = lax.axis_index("core")
-    dims = (((1,), (0,)), ((), ()))
     dd = jnp.concatenate([dd_a[...], dd_b[...]], axis=1)
-    c = pl.program_id(1)
-    cols = pl.ds(pl.multiple_of(c * SLICE, SLICE), SLICE)
-    w = jnp.concatenate([r[:, cols] for r in w_refs], axis=0)
-    p = lax.dot_general(dd, w, dims, preferred_element_type=F32).astype(BF16)
-    p = p.reshape(2, 1, TOK, SLICE)
-
-    @pl.when(mine == c)
-    def _():
-        own[...] = p
-
-    @pl.when(mine != c)
-    def _():
-        other[...] = p
+
+    @pl.loop(0, NZL * NC)
+    def _(n):
+        cols = chunk(n, SLICE)
+        w = jnp.concatenate([r[:, cols] for r in w_refs], axis=0)
+        p = jnp.dot(dd, w, preferred_element_type=F32).astype(BF16)
+        p = p.reshape(2, 1, TOK, SLICE)
+        there = pl.ds(n // NC, 1)
+
+        @pl.when(mine == n % NC)
+        def _():
+            own[:, there] = p
+
+        @pl.when(mine != n % NC)
+        def _():
+            other[:, there] = p
 
 
 def pair_sum_kernel(own, other, out):
@@ -312,23 +314,7 @@
     theirs = shift(mine, dc=1)
     whole = call(join_kernel, shape(2 * TOK, D), 8)(mine, theirs)
 
-    def full(*dims):
-        return pl.BlockSpec(dims, lambda *_: (0,) * len(dims))
-
-    cot_mine, cot_sent = call(
-        spread_kernel,
-        (shape(TOK, WIDE), shape(TOK, WIDE)),
-        grid=(2,),
-        in_specs=[full(TOK, GROUPS * ROWS)],
-        out_specs=(full(TOK, WIDE), full(TOK, WIDE)),
-    )(cotangent)
-    cot_partner = shift(cot_sent, dz=4)
-
-    chunk = 512
-    grid = (D // chunk,)
-
-    def cols(rows, width=chunk):
-        return pl.BlockSpec((rows, width), lambda j, *_: (0, j))
+    cot = call(spread_kernel, shape(2 * TOK, WIDE))(cotangent, shift(cotangent, dz=4))
 
     def forward(w, half, lower, *before):
         shard = 2 * half
@@ -337,22 +323,13 @@
         return call(
             functools.partial(forward_kernel, shard, half, lower),
             (shape(TOK, total), shape(TOK, total), shape(2 * TOK, width)),
-            grid=grid,
-            in_specs=[cols(2 * TOK), full(TOK, WIDE), full(TOK, WIDE)]
-            + [cols(p.shape[0]) for p in w]
-            + [full(*p.shape) for p in before],
-            out_specs=(full(TOK, total), full(TOK, total), full(2 * TOK, width)),
             scratch_shapes=[pltpu.VMEM((2 * TOK, width), F32)],
-        )(whole, cot_mine, cot_partner, *w, *before)
+        )(whole, cot, *w, *before)
 
     def weight_grad(dd, parts):
-        return call(
-            weight_grad_kernel,
-            tuple(shape(p.shape[0], D) for p in parts),
-            grid=grid,
-            in_specs=[full(*dd.shape), cols(2 * TOK)],
-            out_specs=tuple(cols(p.shape[0]) for p in parts),
-        )(dd, whole)
+        return call(weight_grad_kernel, tuple(shape(p.shape[0], D) for p in parts))(
+            dd, whole
+        )
 
     hm_a, hp_a, dd_a = forward(wa, HALF_A, 0)
     hidden_mine, hidden_sent, dd_b = forward(wb, HALF_B, WIDE_A, hm_a, hp_a)
@@ -362,17 +339,8 @@
         finish_kernel, (shape(ROWS, D, F32), shape(ROWS, D, F32))
     )(*sums_a, *sums_b)
 
-    quad = pl.BlockSpec((2, 1, TOK, SLICE), lambda j, c: (0, j, 0, 0))
-    quad_shape = jax.ShapeDtypeStruct((2, NZL, TOK, SLICE), BF16)
-    own_tg, other_tg = call(
-        token_grad_kernel,
-        (quad_shape, quad_shape),
-        megabytes=24,
-        grid=(NZL, NC),
-        in_specs=[full(2 * TOK, WIDE_A), full(2 * TOK, WIDE_B)]
-        + [cols(w.shape[0], NC * SLICE) for w in wa + wb],
-        out_specs=(quad, quad),
-    )(dd_a, dd_b, *wa, *wb)
+    quad = jax.ShapeDtypeStruct((2, NZL, TOK, SLICE), BF16)
+    own_tg, other_tg = call(token_grad_kernel, (quad, quad), 20)(dd_a, dd_b, *wa, *wb)
     cube = (NZ, TOK, SLICE)
     received = shift(other_tg, dc=1)
     blocks = call(pair_sum_kernel, cube_shape, 8)(
@@ -384,8 +352,8 @@
         collect_kernel,
         shape(TOK, GROUPS * ROWS),
         grid=(2,),
-        in_specs=[full(TOK, WIDE), full(TOK, WIDE)],
-        out_specs=full(TOK, GROUPS * ROWS),
+        in_specs=[whole_block(TOK, WIDE), whole_block(TOK, WIDE)],
+        out_specs=whole_block(TOK, GROUPS * ROWS),
         scratch_shapes=[pltpu.VMEM((TOK, GROUPS * ROWS), F32)],
     )(hidden_mine, shift(hidden_sent, dz=4))
     return hidden, token_grad, gate_grad, up_grad

time: 191 us -> 186 us (0.974)
  the two profiles are of different devices: /device:TPU:1 before, /device:TPU:2 now
where the time goes in v1:
time: 186 us; the launch traced here: 185 us
  starting transfers between devices  84.5 us (45%)
  waiting for transfers between devices  70.9 us (38%)
  Pallas kernels  23.3 us (13%)
  local copies, waits for them, and re-layouts  5.86 us (3%)
    ppermute x40, starting transfers between devices, shift(): return lax.ppermute(value, AXES, pairs)  69.7 us
    ppermute x40, waiting for transfers between devices, shift(): return lax.ppermute(value, AXES, pairs)  58.5 us
    all_to_all x2, starting transfers between devices, exchange_z(): return lax.all_to_all(value, ('zh', 'zl'), 0, 0, tiled=True)  14.8 us
    all_to_all x2, waiting for transfers between devices, exchange_z(): return lax.all_to_all(value, ('zh', 'zl'), 0, 0, tiled=True)  12.4 us
    unnamed x24, local copies, waits for them, and re-layouts  5.86 us
    pallas_call x2, Pallas kernels, forward(): call(functools.partial(forward_kernel, shard, half, lower), (shape(TOK, t...  4.6 us
    pallas_call x1, Pallas kernels, body(): call(token_grad_kernel, (quad, quad), 20)(dd_a, dd_b, *wa, *wb)  3.8 us
  transfers between devices with their start and end apart: 42, of which 17 were waited for; matrix products, arithmetic and copies ran while one was open for 0% of the time, Pallas kernels for 8%

profile of v1, /device:TPU:2, one launch (start us, length us, event | category | flops | bytes accessed | tf_op | source)
XLA Modules:
  0.0 185.5 jit_solution(14703218265072129586)
XLA Ops:
  2.6 8.5 %all-to-all-start = ((bf16[8,128,512]{2,1,0:T(8,128)(2,1)}), bf16[8,128,512]{2,1,0:T(8,128)(2,1)S(1)}, u32[]{:S(2)}, u32[]{:S(2)}) async-start(bf16[8,128,512]{2,1,0:T(8,128)(2,1)} %shard_map.93), calls=%async_computation | async-start | bytes 2097152 | tf_op jit(solution)/shard_map/all_to_all | solution.py:47
  11.1 2.2 %shard_map.96 = (bf16[32,4096]{1,0:T(8,128)(2,1)}, bf16[24,4096]{1,0:T(8,128)(2,1)}) custom-call(bf16[28,4096]{1,0:T(8,128)(2,1)} %refs_0_.1, f32[16,28]{1,0:T(8,128)} %bitcast.6, bf16[28,4096]{1,0:T(8,128)(2,1)} %refs_2_.1, f32[16,28]{1,0:T(8,128)} %bitcast.7), custom_call_target="tpu_custom_call" | custom-call | tf_op jit(solution)/shard_map/pallas_call | solution.py:299
  18.6 2.1 %collective-permute-start.13 = (bf16[32,4096]{1,0:T(8,128)(2,1)}, bf16[32,4096]{1,0:T(8,128)(2,1)S(1)}, u32[]{:S(2)}, u32[]{:S(2)}) collective-permute-start(bf16[32,4096]{1,0:T(8,128)(2,1)} %get-tuple-element.45.first), channel_id=1, source_target_pairs={{0,16},{1,17},{2,18},{3,19},{4,20},{5,21},{6,22},{7,23},{8,24},{9,... | collective-permute-start | bytes 786440 | tf_op jit(solution)/shard_map/ppermute | solution.py:43
  21.4 4.3 %collective-permute-start.4 = (bf16[24,4096]{1,0:T(8,128)(2,1)}, bf16[24,4096]{1,0:T(8,128)(2,1)}, u32[]{:S(2)}, u32[]{:S(2)}) collective-permute-start(bf16[24,4096]{1,0:T(8,128)(2,1)} %get-tuple-element.44.first), channel_id=1, source_target_pairs={{0,128},{1,129},{2,130},{3,131},{4,132},{5,133},{6,134},{7,135},{8... | collective-permute-start | bytes 589832 | tf_op jit(solution)/shard_map/ppermute | solution.py:43
  27.5 12.4 %all-to-all-done.own = bf16[8,128,512]{2,1,0:T(8,128)(2,1)S(1)} async-done(((bf16[8,128,512]{2,1,0:T(8,128)(2,1)}), bf16[8,128,512]{2,1,0:T(8,128)(2,1)S(1)}, u32[]{:S(2)}, u32[]{:S(2)}) %all-to-all-start) | async-done | bytes 1048608 | tf_op jit(solution)/shard_map/all_to_all | solution.py:47
  44.8 12.8 %collective-permute-done.1.partner = bf16[128,896]{1,0:T(8,128)(2,1)S(1)} collective-permute-done((bf16[128,896]{1,0:T(8,128)(2,1)S(1)}, bf16[128,896]{1,0:T(8,128)(2,1)S(1)}, u32[]{:S(2)}, u32[]{:S(2)}) %collective-permute-start.1) | collective-permute-done | bytes 229408 | tf_op jit(solution)/shard_map/ppermute | solution.py:43
  57.6 3.0 %collective-permute-start.17 = (bf16[64,4096]{1,0:T(8,128)(2,1)S(1)}, bf16[64,4096]{1,0:T(8,128)(2,1)S(1)}, u32[]{:S(2)}, u32[]{:S(2)}) collective-permute-start(bf16[64,4096]{1,0:T(8,128)(2,1)S(1)} %shard_map.100.refs_1_), channel_id=1, source_target_pairs={{0,192},{1,193},{2,194},{3,195},{4,196},{5,197},{6,198},{7,199},{8... | collective-permute-start | bytes 1572872 | tf_op jit(solution)/shard_map/ppermute | solution.py:43
  60.6 3.2 %collective-permute-start.16 = (bf16[64,4096]{1,0:T(8,128)(2,1)S(1)}, bf16[64,4096]{1,0:T(8,128)(2,1)S(1)}, u32[]{:S(2)}, u32[]{:S(2)}) collective-permute-start(bf16[64,4096]{1,0:T(8,128)(2,1)S(1)} %shard_map.99.refs_0_), channel_id=1, source_target_pairs={{0,192},{1,193},{2,194},{3,195},{4,196},{5,197},{6,198},{7,199},{8... | collective-permute-start | bytes 1572872 | tf_op jit(solution)/shard_map/ppermute | solution.py:43
  63.9 9.1 %collective-permute-done.17.refs_5_ = bf16[64,4096]{1,0:T(8,128)(2,1)S(1)} collective-permute-done((bf16[64,4096]{1,0:T(8,128)(2,1)S(1)}, bf16[64,4096]{1,0:T(8,128)(2,1)S(1)}, u32[]{:S(2)}, u32[]{:S(2)}) %collective-permute-start.17) | collective-permute-done | bytes 524320 | tf_op jit(solution)/shard_map/ppermute | solution.py:43
  72.9 3.7 %collective-permute-start.19 = (bf16[64,4096]{1,0:T(8,128)(2,1)S(1)}, bf16[64,4096]{1,0:T(8,128)(2,1)S(1)}, u32[]{:S(2)}, u32[]{:S(2)}) collective-permute-start(bf16[64,4096]{1,0:T(8,128)(2,1)S(1)} %collective-permute-done.17.refs_5_), channel_id=1, source_target_pairs={{0,192},{1,193},{2,194},{3,195},{4,196},{5,197},{6,198},{7,199},{8... | collective-permute-start | bytes 1572872 | tf_op jit(solution)/shard_map/ppermute | solution.py:43
  78.1 6.0 %collective-permute-done.16.refs_4_ = bf16[64,4096]{1,0:T(8,128)(2,1)S(1)} collective-permute-done((bf16[64,4096]{1,0:T(8,128)(2,1)S(1)}, bf16[64,4096]{1,0:T(8,128)(2,1)S(1)}, u32[]{:S(2)}, u32[]{:S(2)}) %collective-permute-start.16) | collective-permute-done | bytes 524320 | tf_op jit(solution)/shard_map/ppermute | solution.py:43
  90.0 3.2 %collective-permute-done.19.refs_7_ = bf16[64,4096]{1,0:T(8,128)(2,1)S(1)} collective-permute-done((bf16[64,4096]{1,0:T(8,128)(2,1)S(1)}, bf16[64,4096]{1,0:T(8,128)(2,1)S(1)}, u32[]{:S(2)}, u32[]{:S(2)}) %collective-permute-start.19) | collective-permute-done | bytes 524320 | tf_op jit(solution)/shard_map/ppermute | solution.py:43
  93.3 2.4 %shard_map.101 = (bf16[128,512]{1,0:T(8,128)(2,1)S(1)}, bf16[128,512]{1,0:T(8,128)(2,1)S(1)}, bf16[256,512]{1,0:T(8,128)(2,1)S(1)}) custom-call(bf16[256,4096]{1,0:T(8,128)(2,1)S(1)} %shard_map.94.x, bf16[256,896]{1,0:T(8,128)(2,1)S(1)} %shard_map.95.cot, bf16[64,4096]{1,0:T(8,128)(2,1)S(1)} %shard_map.99.refs_0_, bf16[64,4096]{1,0:T(8,128)(2,1)S(1)} %shard_map.100.refs_1_, ...), custom_call_target="tpu_custom_call" | custom-call | tf_op jit(solution)/shard_map/pallas_call | solution.py:323
  95.7 3.9 %collective-permute-done.10.refs_7_.refs_15_ = bf16[48,4096]{1,0:T(8,128)(2,1)S(1)} collective-permute-done((bf16[48,4096]{1,0:T(8,128)(2,1)S(1)}, bf16[48,4096]{1,0:T(8,128)(2,1)S(1)}, u32[]{:S(2)}, u32[]{:S(2)}) %collective-permute-start.10) | collective-permute-done | bytes 393248 | tf_op jit(solution)/shard_map/ppermute | solution.py:43
  99.6 2.2 %shard_map.102 = (bf16[128,896]{1,0:T(8,128)(2,1)S(1)}, bf16[128,896]{1,0:T(8,128)(2,1)S(1)}, bf16[256,384]{1,0:T(8,128)(2,1)S(1)}) custom-call(bf16[256,4096]{1,0:T(8,128)(2,1)S(1)} %shard_map.94.x, bf16[256,896]{1,0:T(8,128)(2,1)S(1)} %shard_map.95.cot, bf16[48,4096]{1,0:T(8,128)(2,1)S(1)} %shard_map.97.refs_0_.refs_8_, ...), custom_call_target="tpu_custom_call" | custom-call | tf_op jit(solution)/shard_map/pallas_call | solution.py:323
  102.5 3.8 %shard_map.104 = (bf16[2,4,128,512]{3,2,1,0:T(8,128)(2,1)S(1)}, bf16[2,4,128,512]{3,2,1,0:T(8,128)(2,1)S(1)}) custom-call(bf16[256,512]{1,0:T(8,128)(2,1)S(1)} %get-tuple-element.50.dd_a.dd, bf16[256,384]{1,0:T(8,128)(2,1)S(1)} %get-tuple-element.51.dd_b.dd, bf16[64,4096]{1,0:T(8,128)(2,1)S(1)} %shard_map.99.refs_0_, ...), custom_call_target="tpu_custom_call" | custom-call | tf_op jit(solution)/shard_map/pallas_call | solution.py:343
  106.4 2.6 %collective-permute-done.21 = bf16[2,4,128,512]{3,2,1,0:T(8,128)(2,1)S(1)} collective-permute-done((bf16[2,4,128,512]{3,2,1,0:T(8,128)(2,1)S(1)}, bf16[2,4,128,512]{3,2,1,0:T(8,128)(2,1)S(1)}, u32[]{:S(2)}, u32[]{:S(2)}) %collective-permute-start.21) | collective-permute-done | bytes 1048608 | tf_op jit(solution)/shard_map/ppermute | solution.py:43
  110.3 6.3 %all-to-all-start.1 = ((bf16[8,128,512]{2,1,0:T(8,128)(2,1)}), bf16[8,128,512]{2,1,0:T(8,128)(2,1)S(1)}, u32[]{:S(2)}, u32[]{:S(2)}) async-start(bf16[8,128,512]{2,1,0:T(8,128)(2,1)} %shard_map.105), calls=%async_computation.1 | async-start | bytes 2097152 | tf_op jit(solution)/shard_map/all_to_all | solution.py:47
  123.2 3.8 %collective-permute-start.22 = (bf16[64,4096]{1,0:T(8,128)(2,1)S(1)}, bf16[64,4096]{1,0:T(8,128)(2,1)S(1)}, u32[]{:S(2)}, u32[]{:S(2)}) collective-permute-start(bf16[64,4096]{1,0:T(8,128)(2,1)S(1)} %get-tuple-element.58), channel_id=1, source_target_pairs={{0,192},{1,193},{2,194},{3,195},{4,196},{5,197},{6,198},{7,199},{8... | collective-permute-start | bytes 1572872 | tf_op jit(solution)/shard_map/ppermute | solution.py:43
  127.0 2.5 %collective-permute-start.34 = (bf16[48,4096]{1,0:T(8,128)(2,1)S(1)}, bf16[48,4096]{1,0:T(8,128)(2,1)S(1)}, u32[]{:S(2)}, u32[]{:S(2)}) collective-permute-start(bf16[48,4096]{1,0:T(8,128)(2,1)S(1)} %get-tuple-element.75), channel_id=1, source_target_pairs={{0,24},{1,25},{2,26},{3,27},{4,28},{5,29},{6,30},{7,31},{8,0},{9,1... | collective-permute-start | bytes 1179656 | tf_op jit(solution)/shard_map/ppermute | solution.py:43
  133.1 2.9 %collective-permute-start.33 = (bf16[48,4096]{1,0:T(8,128)(2,1)S(1)}, bf16[48,4096]{1,0:T(8,128)(2,1)S(1)}, u32[]{:S(2)}, u32[]{:S(2)}) collective-permute-start(bf16[48,4096]{1,0:T(8,128)(2,1)S(1)} %get-tuple-element.74), channel_id=1, source_target_pairs={{0,24},{1,25},{2,26},{3,27},{4,28},{5,29},{6,30},{7,31},{8,0},{9,1... | collective-permute-start | bytes 1179656 | tf_op jit(solution)/shard_map/ppermute | solution.py:43
  137.6 3.7 %collective-permute-start.25 = (bf16[64,4096]{1,0:T(8,128)(2,1)S(1)}, bf16[64,4096]{1,0:T(8,128)(2,1)S(1)}, u32[]{:S(2)}, u32[]{:S(2)}) collective-permute-start(bf16[64,4096]{1,0:T(8,128)(2,1)S(1)} %get-tuple-element.61), channel_id=1, source_target_pairs={{0,192},{1,193},{2,194},{3,195},{4,196},{5,197},{6,198},{7,199},{8... | collective-permute-start | bytes 1572872 | tf_op jit(solution)/shard_map/ppermute | solution.py:43
  141.3 2.2 %collective-permute-start.36 = (bf16[48,4096]{1,0:T(8,128)(2,1)S(1)}, bf16[48,4096]{1,0:T(8,128)(2,1)S(1)}, u32[]{:S(2)}, u32[]{:S(2)}) collective-permute-start(bf16[48,4096]{1,0:T(8,128)(2,1)S(1)} %get-tuple-element.77), channel_id=1, source_target_pairs={{0,8},{1,9},{2,10},{3,11},{4,12},{5,13},{6,14},{7,15},{8,16},{9,17... | collective-permute-start | bytes 1179656 | tf_op jit(solution)/shard_map/ppermute | solution.py:43
  143.9 3.2 %collective-permute-start.24 = (bf16[64,4096]{1,0:T(8,128)(2,1)S(1)}, bf16[64,4096]{1,0:T(8,128)(2,1)S(1)}, u32[]{:S(2)}, u32[]{:S(2)}) collective-permute-start(bf16[64,4096]{1,0:T(8,128)(2,1)S(1)} %get-tuple-element.60), channel_id=1, source_target_pairs={{0,192},{1,193},{2,194},{3,195},{4,196},{5,197},{6,198},{7,199},{8... | collective-permute-start | bytes 1572872 | tf_op jit(solution)/shard_map/ppermute | solution.py:43
  148.0 3.7 %collective-permute-done.36.l_hi = bf16[48,4096]{1,0:T(8,128)(2,1)S(1)} collective-permute-done((bf16[48,4096]{1,0:T(8,128)(2,1)S(1)}, bf16[48,4096]{1,0:T(8,128)(2,1)S(1)}, u32[]{:S(2)}, u32[]{:S(2)}) %collective-permute-start.36) | collective-permute-done | bytes 393248 | tf_op jit(solution)/shard_map/ppermute | solution.py:43
  151.8 5.4 %collective-permute-start.20 = (bf16[128,896]{1,0:T(8,128)(2,1)S(1)}, bf16[128,896]{1,0:T(8,128)(2,1)S(1)}, u32[]{:S(2)}, u32[]{:S(2)}) collective-permute-start(bf16[128,896]{1,0:T(8,128)(2,1)S(1)} %copy-done.11), channel_id=1, source_target_pairs={{0,32},{1,33},{2,34},{3,35},{4,36},{5,37},{6,38},{7,39},{8,40},{9,... | collective-permute-start | bytes 688136 | tf_op jit(solution)/shard_map/ppermute | solution.py:43
  159.9 4.6 %collective-permute-done.24.r_lo = bf16[64,4096]{1,0:T(8,128)(2,1)S(1)} collective-permute-done((bf16[64,4096]{1,0:T(8,128)(2,1)S(1)}, bf16[64,4096]{1,0:T(8,128)(2,1)S(1)}, u32[]{:S(2)}, u32[]{:S(2)}) %collective-permute-start.24) | collective-permute-done | bytes 524320 | tf_op jit(solution)/shard_map/ppermute | solution.py:43
  164.4 3.9 %collective-permute-done.27.l_hi = bf16[64,4096]{1,0:T(8,128)(2,1)S(1)} collective-permute-done((bf16[64,4096]{1,0:T(8,128)(2,1)S(1)}, bf16[64,4096]{1,0:T(8,128)(2,1)S(1)}, u32[]{:S(2)}, u32[]{:S(2)}) %collective-permute-start.27) | collective-permute-done | bytes 524320 | tf_op jit(solution)/shard_map/ppermute | solution.py:43
  171.4 3.1 %collective-permute-start.30 = (bf16[32,4096]{1,0:T(8,128)(2,1)S(1)}, bf16[32,4096]{1,0:T(8,128)(2,1)S(1)}, u32[]{:S(2)}, u32[]{:S(2)}) collective-permute-start(bf16[32,4096]{1,0:T(8,128)(2,1)S(1)} %get-tuple-element.67), channel_id=1, source_target_pairs={{0,16},{1,17},{2,18},{3,19},{4,20},{5,21},{6,22},{7,23},{8,24},{9,... | collective-permute-start | bytes 786440 | tf_op jit(solution)/shard_map/ppermute | solution.py:43
  174.6 3.2 %collective-permute-start.39 = (bf16[24,4096]{1,0:T(8,128)(2,1)S(1)}, bf16[24,4096]{1,0:T(8,128)(2,1)S(1)}, u32[]{:S(2)}, u32[]{:S(2)}) collective-permute-start(bf16[24,4096]{1,0:T(8,128)(2,1)S(1)} %get-tuple-element.81), channel_id=1, source_target_pairs={{0,128},{1,129},{2,130},{3,131},{4,132},{5,133},{6,134},{7,135},{8... | collective-permute-start | bytes 589832 | tf_op jit(solution)/shard_map/ppermute | solution.py:43
  177.8 2.0 %shard_map.103 = bf16[128,896]{1,0:T(8,128)(2,1)} custom-call(bf16[128,896]{1,0:T(8,128)(2,1)S(1)} %copy-done.7, bf16[128,896]{1,0:T(8,128)(2,1)S(1)} %collective-permute-done.20.partner), custom_call_target="tpu_custom_call" | custom-call | tf_op jit(solution)/shard_map/pallas_call | solution.py:351
  181.5 2.1 %collective-permute-done.39.refs_7_ = bf16[24,4096]{1,0:T(8,128)(2,1)S(1)} collective-permute-done((bf16[24,4096]{1,0:T(8,128)(2,1)S(1)}, bf16[24,4096]{1,0:T(8,128)(2,1)S(1)}, u32[]{:S(2)}, u32[]{:S(2)}) %collective-permute-start.39) | collective-permute-done | bytes 196640 | tf_op jit(solution)/shard_map/ppermute | solution.py:43
  (97 shorter events, 46.4 us)
Async XLA Ops:
  2.6 37.2 %all-to-all-start = ((bf16[8,128,512]{2,1,0:T(8,128)(2,1)}), bf16[8,128,512]{2,1,0:T(8,128)(2,1)S(1)}, u32[]{:S(2)}, u32[]{:S(2)}) async-start(bf16[8,128,512]{2,1,0:T(8,128)(2,1)} %shard_map.93), calls=%async_computation | async-start | bytes 2097152 | tf_op jit(solution)/shard_map/all_to_all | solution.py:47
  18.1 25.5 %collective-permute-start.12 = (bf16[32,4096]{1,0:T(8,128)(2,1)}, bf16[32,4096]{1,0:T(8,128)(2,1)S(1)}, u32[]{:S(2)}, u32[]{:S(2)}) collective-permute-start(bf16[32,4096]{1,0:T(8,128)(2,1)} %get-tuple-element.45.first), channel_id=1, source_target_pairs={{0,24},{1,25},{2,26},{3,27},{4,28},{5,29},{6,30},{7,31},{8,0},{9,1... | collective-permute-start | bytes 786440 | tf_op jit(solution)/shard_map/ppermute | solution.py:43
  18.6 25.6 %collective-permute-start.13 = (bf16[32,4096]{1,0:T(8,128)(2,1)}, bf16[32,4096]{1,0:T(8,128)(2,1)S(1)}, u32[]{:S(2)}, u32[]{:S(2)}) collective-permute-start(bf16[32,4096]{1,0:T(8,128)(2,1)} %get-tuple-element.45.first), channel_id=1, source_target_pairs={{0,16},{1,17},{2,18},{3,19},{4,20},{5,21},{6,22},{7,23},{8,24},{9,... | collective-permute-start | bytes 786440 | tf_op jit(solution)/shard_map/ppermute | solution.py:43
  21.4 19.7 %collective-permute-start.4 = (bf16[24,4096]{1,0:T(8,128)(2,1)}, bf16[24,4096]{1,0:T(8,128)(2,1)}, u32[]{:S(2)}, u32[]{:S(2)}) collective-permute-start(bf16[24,4096]{1,0:T(8,128)(2,1)} %get-tuple-element.44.first), channel_id=1, source_target_pairs={{0,128},{1,129},{2,130},{3,131},{4,132},{5,133},{6,134},{7,135},{8... | collective-permute-start | bytes 589832 | tf_op jit(solution)/shard_map/ppermute | solution.py:43
  26.7 37.2 %collective-permute-start.14 = (bf16[64,4096]{1,0:T(8,128)(2,1)S(1)}, bf16[64,4096]{1,0:T(8,128)(2,1)S(1)}, u32[]{:S(2)}, u32[]{:S(2)}) collective-permute-start(bf16[64,4096]{1,0:T(8,128)(2,1)S(1)} %shard_map.99.refs_0_), channel_id=1, source_target_pairs={{0,64},{1,65},{2,66},{3,67},{4,68},{5,69},{6,70},{7,71},{8,72},{9,... | collective-permute-start | bytes 1572872 | tf_op jit(solution)/shard_map/ppermute | solution.py:43
  39.8 47.1 %collective-permute-start = (bf16[8,128,512]{2,1,0:T(8,128)(2,1)S(1)}, bf16[8,128,512]{2,1,0:T(8,128)(2,1)S(1)}, u32[]{:S(2)}, u32[]{:S(2)}) collective-permute-start(bf16[8,128,512]{2,1,0:T(8,128)(2,1)S(1)} %all-to-all-done.own), channel_id=1, source_target_pairs={{0,1},{1,0},{2,3},{3,2},{4,5},{5,4},{6,7},{7,6},{8,9},{9,8},{10,11... | collective-permute-start | bytes 3145736 | tf_op jit(solution)/shard_map/ppermute | solution.py:43
  41.0 19.6 %collective-permute-start.5 = (bf16[48,4096]{1,0:T(8,128)(2,1)S(1)}, bf16[48,4096]{1,0:T(8,128)(2,1)S(1)}, u32[]{:S(2)}, u32[]{:S(2)}) collective-permute-start(bf16[48,4096]{1,0:T(8,128)(2,1)S(1)} %shard_map.97.refs_0_.refs_8_), channel_id=1, source_target_pairs={{0,8},{1,9},{2,10},{3,11},{4,12},{5,13},{6,14},{7,15},{8,16},{9,17... | collective-permute-start | bytes 1179656 | tf_op jit(solution)/shard_map/ppermute | solution.py:43
  43.6 17.0 %collective-permute-start.8 = (bf16[48,4096]{1,0:T(8,128)(2,1)S(1)}, bf16[48,4096]{1,0:T(8,128)(2,1)S(1)}, u32[]{:S(2)}, u32[]{:S(2)}) collective-permute-start(bf16[48,4096]{1,0:T(8,128)(2,1)S(1)} %shard_map.98.refs_1_.refs_9_), channel_id=1, source_target_pairs={{0,24},{1,25},{2,26},{3,27},{4,28},{5,29},{6,30},{7,31},{8,0},{9,1... | collective-permute-start | bytes 1179656 | tf_op jit(solution)/shard_map/ppermute | solution.py:43
  44.2 13.4 %collective-permute-start.1 = (bf16[128,896]{1,0:T(8,128)(2,1)S(1)}, bf16[128,896]{1,0:T(8,128)(2,1)S(1)}, u32[]{:S(2)}, u32[]{:S(2)}) collective-permute-start(bf16[128,896]{1,0:T(8,128)(2,1)S(1)} %copy-done.5), channel_id=1, source_target_pairs={{0,32},{1,33},{2,34},{3,35},{4,36},{5,37},{6,38},{7,39},{8,40},{9,... | collective-permute-start | bytes 688136 | tf_op jit(solution)/shard_map/ppermute | solution.py:43
  57.6 15.3 %collective-permute-start.17 = (bf16[64,4096]{1,0:T(8,128)(2,1)S(1)}, bf16[64,4096]{1,0:T(8,128)(2,1)S(1)}, u32[]{:S(2)}, u32[]{:S(2)}) collective-permute-start(bf16[64,4096]{1,0:T(8,128)(2,1)S(1)} %shard_map.100.refs_1_), channel_id=1, source_target_pairs={{0,192},{1,193},{2,194},{3,195},{4,196},{5,197},{6,198},{7,199},{8... | collective-permute-start | bytes 1572872 | tf_op jit(solution)/shard_map/ppermute | solution.py:43
  60.6 16.0 %collective-permute-start.15 = (bf16[64,4096]{1,0:T(8,128)(2,1)S(1)}, bf16[64,4096]{1,0:T(8,128)(2,1)S(1)}, u32[]{:S(2)}, u32[]{:S(2)}) collective-permute-start(bf16[64,4096]{1,0:T(8,128)(2,1)S(1)} %shard_map.100.refs_1_), channel_id=1, source_target_pairs={{0,64},{1,65},{2,66},{3,67},{4,68},{5,69},{6,70},{7,71},{8,72},{9,... | collective-permute-start | bytes 1572872 | tf_op jit(solution)/shard_map/ppermute | solution.py:43
  60.6 23.5 %collective-permute-start.16 = (bf16[64,4096]{1,0:T(8,128)(2,1)S(1)}, bf16[64,4096]{1,0:T(8,128)(2,1)S(1)}, u32[]{:S(2)}, u32[]{:S(2)}) collective-permute-start(bf16[64,4096]{1,0:T(8,128)(2,1)S(1)} %shard_map.99.refs_0_), channel_id=1, source_target_pairs={{0,192},{1,193},{2,194},{3,195},{4,196},{5,197},{6,198},{7,199},{8... | collective-permute-start | bytes 1572872 | tf_op jit(solution)/shard_map/ppermute | solution.py:43
  63.9 22.1 %collective-permute-start.18 = (bf16[64,4096]{1,0:T(8,128)(2,1)S(1)}, bf16[64,4096]{1,0:T(8,128)(2,1)S(1)}, u32[]{:S(2)}, u32[]{:S(2)}) collective-permute-start(bf16[64,4096]{1,0:T(8,128)(2,1)S(1)} %collective-permute-done.14.refs_2_), channel_id=1, source_target_pairs={{0,64},{1,65},{2,66},{3,67},{4,68},{5,69},{6,70},{7,71},{8,72},{9,... | collective-permute-start | bytes 1572872 | tf_op jit(solution)/shard_map/ppermute | solution.py:43
  72.9 20.3 %collective-permute-start.19 = (bf16[64,4096]{1,0:T(8,128)(2,1)S(1)}, bf16[64,4096]{1,0:T(8,128)(2,1)S(1)}, u32[]{:S(2)}, u32[]{:S(2)}) collective-permute-start(bf16[64,4096]{1,0:T(8,128)(2,1)S(1)} %collective-permute-done.17.refs_5_), channel_id=1, source_target_pairs={{0,192},{1,193},{2,194},{3,195},{4,196},{5,197},{6,198},{7,199},{8... | collective-permute-start | bytes 1572872 | tf_op jit(solution)/shard_map/ppermute | solution.py:43
  76.6 19.1 %collective-permute-start.6 = (bf16[48,4096]{1,0:T(8,128)(2,1)S(1)}, bf16[48,4096]{1,0:T(8,128)(2,1)S(1)}, u32[]{:S(2)}, u32[]{:S(2)}) collective-permute-start(bf16[48,4096]{1,0:T(8,128)(2,1)S(1)} %shard_map.98.refs_1_.refs_9_), channel_id=1, source_target_pairs={{0,8},{1,9},{2,10},{3,11},{4,12},{5,13},{6,14},{7,15},{8,16},{9,17... | collective-permute-start | bytes 1179656 | tf_op jit(solution)/shard_map/ppermute | solution.py:43
  86.9 12.7 %collective-permute-start.10 = (bf16[48,4096]{1,0:T(8,128)(2,1)S(1)}, bf16[48,4096]{1,0:T(8,128)(2,1)S(1)}, u32[]{:S(2)}, u32[]{:S(2)}) collective-permute-start(bf16[48,4096]{1,0:T(8,128)(2,1)S(1)} %collective-permute-done.8.refs_5_.refs_13_), channel_id=1, source_target_pairs={{0,24},{1,25},{2,26},{3,27},{4,28},{5,29},{6,30},{7,31},{8,0},{9,1... | collective-permute-start | bytes 1179656 | tf_op jit(solution)/shard_map/ppermute | solution.py:43
  110.3 74.4 %all-to-all-start.1 = ((bf16[8,128,512]{2,1,0:T(8,128)(2,1)}), bf16[8,128,512]{2,1,0:T(8,128)(2,1)S(1)}, u32[]{:S(2)}, u32[]{:S(2)}) async-start(bf16[8,128,512]{2,1,0:T(8,128)(2,1)} %shard_map.105), calls=%async_computation.1 | async-start | bytes 2097152 | tf_op jit(solution)/shard_map/all_to_all | solution.py:47
  119.2 12.0 %collective-permute-start.31 = (bf16[48,4096]{1,0:T(8,128)(2,1)S(1)}, bf16[48,4096]{1,0:T(8,128)(2,1)S(1)}, u32[]{:S(2)}, u32[]{:S(2)}) collective-permute-start(bf16[48,4096]{1,0:T(8,128)(2,1)S(1)} %get-tuple-element.72), channel_id=1, source_target_pairs={{0,24},{1,25},{2,26},{3,27},{4,28},{5,29},{6,30},{7,31},{8,0},{9,1... | collective-permute-start | bytes 1179656 | tf_op jit(solution)/shard_map/ppermute | solution.py:43
  123.2 14.4 %collective-permute-start.22 = (bf16[64,4096]{1,0:T(8,128)(2,1)S(1)}, bf16[64,4096]{1,0:T(8,128)(2,1)S(1)}, u32[]{:S(2)}, u32[]{:S(2)}) collective-permute-start(bf16[64,4096]{1,0:T(8,128)(2,1)S(1)} %get-tuple-element.58), channel_id=1, source_target_pairs={{0,192},{1,193},{2,194},{3,195},{4,196},{5,197},{6,198},{7,199},{8... | collective-permute-start | bytes 1572872 | tf_op jit(solution)/shard_map/ppermute | solution.py:43
  126.9 14.3 %collective-permute-start.23 = (bf16[64,4096]{1,0:T(8,128)(2,1)S(1)}, bf16[64,4096]{1,0:T(8,128)(2,1)S(1)}, u32[]{:S(2)}, u32[]{:S(2)}) collective-permute-start(bf16[64,4096]{1,0:T(8,128)(2,1)S(1)} %get-tuple-element.59), channel_id=1, source_target_pairs={{0,64},{1,65},{2,66},{3,67},{4,68},{5,69},{6,70},{7,71},{8,72},{9,... | collective-permute-start | bytes 1572872 | tf_op jit(solution)/shard_map/ppermute | solution.py:43
  127.0 16.8 %collective-permute-start.34 = (bf16[48,4096]{1,0:T(8,128)(2,1)S(1)}, bf16[48,4096]{1,0:T(8,128)(2,1)S(1)}, u32[]{:S(2)}, u32[]{:S(2)}) collective-permute-start(bf16[48,4096]{1,0:T(8,128)(2,1)S(1)} %get-tuple-element.75), channel_id=1, source_target_pairs={{0,24},{1,25},{2,26},{3,27},{4,28},{5,29},{6,30},{7,31},{8,0},{9,1... | collective-permute-start | bytes 1179656 | tf_op jit(solution)/shard_map/ppermute | solution.py:43
  131.2 12.7 %collective-permute-start.35 = (bf16[48,4096]{1,0:T(8,128)(2,1)S(1)}, bf16[48,4096]{1,0:T(8,128)(2,1)S(1)}, u32[]{:S(2)}, u32[]{:S(2)}) collective-permute-start(bf16[48,4096]{1,0:T(8,128)(2,1)S(1)} %get-tuple-element.76), channel_id=1, source_target_pairs={{0,8},{1,9},{2,10},{3,11},{4,12},{5,13},{6,14},{7,15},{8,16},{9,17... | collective-permute-start | bytes 1179656 | tf_op jit(solution)/shard_map/ppermute | solution.py:43
  133.1 14.0 %collective-permute-start.33 = (bf16[48,4096]{1,0:T(8,128)(2,1)S(1)}, bf16[48,4096]{1,0:T(8,128)(2,1)S(1)}, u32[]{:S(2)}, u32[]{:S(2)}) collective-permute-start(bf16[48,4096]{1,0:T(8,128)(2,1)S(1)} %get-tuple-element.74), channel_id=1, source_target_pairs={{0,24},{1,25},{2,26},{3,27},{4,28},{5,29},{6,30},{7,31},{8,0},{9,1... | collective-permute-start | bytes 1179656 | tf_op jit(solution)/shard_map/ppermute | solution.py:43
  137.6 19.8 %collective-permute-start.25 = (bf16[64,4096]{1,0:T(8,128)(2,1)S(1)}, bf16[64,4096]{1,0:T(8,128)(2,1)S(1)}, u32[]{:S(2)}, u32[]{:S(2)}) collective-permute-start(bf16[64,4096]{1,0:T(8,128)(2,1)S(1)} %get-tuple-element.61), channel_id=1, source_target_pairs={{0,192},{1,193},{2,194},{3,195},{4,196},{5,197},{6,198},{7,199},{8... | collective-permute-start | bytes 1572872 | tf_op jit(solution)/shard_map/ppermute | solution.py:43
  143.8 16.1 %collective-permute-start.26 = (bf16[64,4096]{1,0:T(8,128)(2,1)S(1)}, bf16[64,4096]{1,0:T(8,128)(2,1)S(1)}, u32[]{:S(2)}, u32[]{:S(2)}) collective-permute-start(bf16[64,4096]{1,0:T(8,128)(2,1)S(1)} %get-tuple-element.62), channel_id=1, source_target_pairs={{0,64},{1,65},{2,66},{3,67},{4,68},{5,69},{6,70},{7,71},{8,72},{9,... | collective-permute-start | bytes 1572872 | tf_op jit(solution)/shard_map/ppermute | solution.py:43
  143.9 20.5 %collective-permute-start.24 = (bf16[64,4096]{1,0:T(8,128)(2,1)S(1)}, bf16[64,4096]{1,0:T(8,128)(2,1)S(1)}, u32[]{:S(2)}, u32[]{:S(2)}) collective-permute-start(bf16[64,4096]{1,0:T(8,128)(2,1)S(1)} %get-tuple-element.60), channel_id=1, source_target_pairs={{0,192},{1,193},{2,194},{3,195},{4,196},{5,197},{6,198},{7,199},{8... | collective-permute-start | bytes 1572872 | tf_op jit(solution)/shard_map/ppermute | solution.py:43
  147.1 21.2 %collective-permute-start.27 = (bf16[64,4096]{1,0:T(8,128)(2,1)S(1)}, bf16[64,4096]{1,0:T(8,128)(2,1)S(1)}, u32[]{:S(2)}, u32[]{:S(2)}) collective-permute-start(bf16[64,4096]{1,0:T(8,128)(2,1)S(1)} %get-tuple-element.63), channel_id=1, source_target_pairs={{0,64},{1,65},{2,66},{3,67},{4,68},{5,69},{6,70},{7,71},{8,72},{9,... | collective-permute-start | bytes 1572872 | tf_op jit(solution)/shard_map/ppermute | solution.py:43
  151.8 22.8 %collective-permute-start.20 = (bf16[128,896]{1,0:T(8,128)(2,1)S(1)}, bf16[128,896]{1,0:T(8,128)(2,1)S(1)}, u32[]{:S(2)}, u32[]{:S(2)}) collective-permute-start(bf16[128,896]{1,0:T(8,128)(2,1)S(1)} %copy-done.11), channel_id=1, source_target_pairs={{0,32},{1,33},{2,34},{3,35},{4,36},{5,37},{6,38},{7,39},{8,40},{9,... | collective-permute-start | bytes 688136 | tf_op jit(solution)/shard_map/ppermute | solution.py:43
  157.4 17.1 %collective-permute-start.37 = (bf16[24,4096]{1,0:T(8,128)(2,1)S(1)}, bf16[24,4096]{1,0:T(8,128)(2,1)S(1)}, u32[]{:S(2)}, u32[]{:S(2)}) collective-permute-start(bf16[24,4096]{1,0:T(8,128)(2,1)S(1)} %get-tuple-element.79), channel_id=1, source_target_pairs={{0,192},{1,193},{2,194},{3,195},{4,196},{5,197},{6,198},{7,199},{8... | collective-permute-start | bytes 589832 | tf_op jit(solution)/shard_map/ppermute | solution.py:43
  168.7 14.9 %collective-permute-start.28 = (bf16[32,4096]{1,0:T(8,128)(2,1)S(1)}, bf16[32,4096]{1,0:T(8,128)(2,1)S(1)}, u32[]{:S(2)}, u32[]{:S(2)}) collective-permute-start(bf16[32,4096]{1,0:T(8,128)(2,1)S(1)} %get-tuple-element.65), channel_id=1, source_target_pairs={{0,24},{1,25},{2,26},{3,27},{4,28},{5,29},{6,30},{7,31},{8,0},{9,1... | collective-permute-start | bytes 786440 | tf_op jit(solution)/shard_map/ppermute | solution.py:43
  169.5 14.0 %collective-permute-start.29 = (bf16[32,4096]{1,0:T(8,128)(2,1)S(1)}, bf16[32,4096]{1,0:T(8,128)(2,1)S(1)}, u32[]{:S(2)}, u32[]{:S(2)}) collective-permute-start(bf16[32,4096]{1,0:T(8,128)(2,1)S(1)} %get-tuple-element.66), channel_id=1, source_target_pairs={{0,8},{1,9},{2,10},{3,11},{4,12},{5,13},{6,14},{7,15},{8,16},{9,17... | collective-permute-start | bytes 786440 | tf_op jit(solution)/shard_map/ppermute | solution.py:43
  171.4 12.1 %collective-permute-start.30 = (bf16[32,4096]{1,0:T(8,128)(2,1)S(1)}, bf16[32,4096]{1,0:T(8,128)(2,1)S(1)}, u32[]{:S(2)}, u32[]{:S(2)}) collective-permute-start(bf16[32,4096]{1,0:T(8,128)(2,1)S(1)} %get-tuple-element.67), channel_id=1, source_target_pairs={{0,16},{1,17},{2,18},{3,19},{4,20},{5,21},{6,22},{7,23},{8,24},{9,... | collective-permute-start | bytes 786440 | tf_op jit(solution)/shard_map/ppermute | solution.py:43
  (22 other events, 236.9 us)

commit v2 on v1

--- a/solution.py
+++ b/solution.py
@@ -63,19 +63,24 @@
 VMEM = pl.BlockSpec(memory_space=pltpu.VMEM)
 
 
+def in_hbm(value):
+    return pltpu.with_memory_space_constraint(value, pltpu.HBM)
+
+
 def whole_block(*dims):
     return pl.BlockSpec(dims, lambda n: (0,) * len(dims))
 
 
-def dequant_kernel(*refs):
-    sources, (a, b), (gc, gs, uc, us), sems = refs[:4], refs[4:6], refs[6:10], refs[10]
+def dequant_kernel(tokens, *refs):
+    sources, (a, b, spread), (gc, gs, uc, us), sems = refs[:4], refs[4:7], refs[7:11], refs[11]
+    pairs = list(zip(sources, (gc, gs, uc, us))) + [(tokens, spread.at[n]) for n in range(NZ)]
     copies = [
         pltpu.make_async_copy(source, target, sems.at[n])
-        for n, (source, target) in enumerate(zip(sources, (gc, gs, uc, us)))
+        for n, (source, target) in enumerate(pairs)
     ]
     for copy in copies:
         copy.start()
-    for copy in copies:
+    for copy in copies[:4]:
         copy.wait()
     scales_g, scales_u = gs[...].T, us[...].T
     for n in range(D // BLOCK):
@@ -84,17 +89,14 @@
         u = uc[:, cols].astype(F32) * scales_u[:, n : n + 1]
         a[:, cols] = jnp.concatenate([g[:HALF_A], u[:HALF_A]], axis=0).astype(BF16)
         b[:, cols] = jnp.concatenate([g[HALF_A:], u[HALF_A:]], axis=0).astype(BF16)
+    for copy in copies[4:]:
+        copy.wait()
 
 
 def pair_kernel(first, second, out):
     n = first.shape[0]
     out[:n] = first[...]
     out[n:] = second[...]
-
-
-def copies_kernel(tokens, out):
-    for n in range(NZ):
-        out[n] = tokens[...]
 
 
 def rel_of(n):
@@ -296,20 +298,20 @@
 
 def body(tokens, gate_codes, gate_scales, up_codes, up_scales, cotangent):
     sources = (gate_codes, gate_scales.T, up_codes, up_scales.T)
-    shard_a, shard_b = call(
+    cube_shape = jax.ShapeDtypeStruct((NZ, TOK, SLICE), BF16)
+    hbm = pl.BlockSpec(memory_space=pltpu.HBM)
+    shard_a, shard_b, copies = call(
         dequant_kernel,
-        (shape(SHARD_A, D), shape(SHARD_B, D)),
-        56,
-        in_specs=[pl.BlockSpec(memory_space=pltpu.HBM)] * 4,
-        out_specs=(VMEM, VMEM),
+        (shape(SHARD_A, D), shape(SHARD_B, D), cube_shape),
+        4,
+        in_specs=[hbm] * 5,
+        out_specs=(VMEM, VMEM, hbm),
         scratch_shapes=[pltpu.VMEM(v.shape, v.dtype) for v in sources]
-        + [pltpu.SemaphoreType.DMA((4,))],
-    )(*sources)
+        + [pltpu.SemaphoreType.DMA((4 + NZ,))],
+    )(in_hbm(tokens), *[in_hbm(v) for v in sources])
     wa = gather_plane(shard_a, "dx", "dy")
     wb = gather_plane(shard_b, "dy", "dx")
 
-    cube_shape = jax.ShapeDtypeStruct((NZ, TOK, SLICE), BF16)
-    copies = call(copies_kernel, cube_shape, 4)(tokens)
     mine = exchange_z(copies)
     theirs = shift(mine, dc=1)
     whole = call(join_kernel, shape(2 * TOK, D), 8)(mine, theirs)

time: 186 us -> 217 us (1.17)
  the two profiles are of different devices: /device:TPU:2 before, /device:TPU:1 now
where the time goes in v2:
time: 217 us; the launch traced here: 213 us
  waiting for transfers between devices  78.1 us (36%)
  starting transfers between devices  76.8 us (35%)
  Pallas kernels  53 us (24%)
  local copies, waits for them, and re-layouts  4.45 us (2%)
    ppermute x40, starting transfers between devices, shift(): return lax.ppermute(value, AXES, pairs)  61.5 us
    ppermute x40, waiting for transfers between devices, shift(): return lax.ppermute(value, AXES, pairs)  61.1 us
    pallas_call x1, Pallas kernels, body(): call(dequant_kernel, (shape(SHARD_A, D), shape(SHARD_B, D), cube_shape),...  33 us
    all_to_all x2, waiting for transfers between devices, exchange_z(): return lax.all_to_all(value, ('zh', 'zl'), 0, 0, tiled=True)  17 us
    all_to_all x2, starting transfers between devices, exchange_z(): return lax.all_to_all(value, ('zh', 'zl'), 0, 0, tiled=True)  15.3 us
    pallas_call x2, Pallas kernels, forward(): call(functools.partial(forward_kernel, shard, half, lower), (shape(TOK, t...  4.6 us
    unnamed x22, local copies, waits for them, and re-layouts  4.45 us
  transfers between devices with their start and end apart: 42, of which 16 were waited for; matrix products, arithmetic and copies ran while one was open for 0% of the time, Pallas kernels for 6%

profile of v2, /device:TPU:1, one launch (start us, length us, event | category | flops | bytes accessed | tf_op | source)
XLA Modules:
  0.0 213.3 jit_solution(10382160613971075635)
XLA Ops:
  0.6 33.0 %shard_map.93 = (bf16[32,4096]{1,0:T(8,128)(2,1)S(1)}, bf16[24,4096]{1,0:T(8,128)(2,1)S(1)}, bf16[8,128,512]{2,1,0:T(8,128)(2,1)}) custom-call(bf16[128,512]{1,0:T(8,128)(2,1)} %tokens.1, bf16[28,4096]{1,0:T(8,128)(2,1)} %refs_0_.1, f32[16,28]{1,0:T(8,128)} %bitcast.6, bf16[28,4096]{1,0:T(8,128)(2,1)} %refs_2_.1, f32[16,28]{1,0:T(8,128)} %bitcast.7), custom_call_target="tpu_custom_call" | custom-call | tf_op jit(solution)/shard_map/pallas_call | solution.py:303
  33.6 9.1 %all-to-all-start = ((bf16[8,128,512]{2,1,0:T(8,128)(2,1)}), bf16[8,128,512]{2,1,0:T(8,128)(2,1)S(1)}, u32[]{:S(2)}, u32[]{:S(2)}) async-start(bf16[8,128,512]{2,1,0:T(8,128)(2,1)} %get-tuple-element.45), calls=%async_computation | async-start | bytes 2097152 | tf_op jit(solution)/shard_map/all_to_all | solution.py:47
  50.9 2.9 %collective-permute-start.4 = (bf16[24,4096]{1,0:T(8,128)(2,1)S(1)}, bf16[24,4096]{1,0:T(8,128)(2,1)}, u32[]{:S(2)}, u32[]{:S(2)}) collective-permute-start(bf16[24,4096]{1,0:T(8,128)(2,1)S(1)} %get-tuple-element.46.first), channel_id=1, source_target_pairs={{0,128},{1,129},{2,130},{3,131},{4,132},{5,133},{6,134},{7,135},{8... | collective-permute-start | bytes 589832 | tf_op jit(solution)/shard_map/ppermute | solution.py:43
  54.9 17.0 %all-to-all-done.own = bf16[8,128,512]{2,1,0:T(8,128)(2,1)S(1)} async-done(((bf16[8,128,512]{2,1,0:T(8,128)(2,1)}), bf16[8,128,512]{2,1,0:T(8,128)(2,1)S(1)}, u32[]{:S(2)}, u32[]{:S(2)}) %all-to-all-start) | async-done | bytes 1048608 | tf_op jit(solution)/shard_map/all_to_all | solution.py:47
  77.6 12.2 %collective-permute-done.1.partner = bf16[128,896]{1,0:T(8,128)(2,1)S(1)} collective-permute-done((bf16[128,896]{1,0:T(8,128)(2,1)S(1)}, bf16[128,896]{1,0:T(8,128)(2,1)S(1)}, u32[]{:S(2)}, u32[]{:S(2)}) %collective-permute-start.1) | collective-permute-done | bytes 229408 | tf_op jit(solution)/shard_map/ppermute | solution.py:43
  89.8 2.7 %collective-permute-start.17 = (bf16[64,4096]{1,0:T(8,128)(2,1)S(1)}, bf16[64,4096]{1,0:T(8,128)(2,1)S(1)}, u32[]{:S(2)}, u32[]{:S(2)}) collective-permute-start(bf16[64,4096]{1,0:T(8,128)(2,1)S(1)} %shard_map.99.refs_1_), channel_id=1, source_target_pairs={{0,192},{1,193},{2,194},{3,195},{4,196},{5,197},{6,198},{7,199},{8... | collective-permute-start | bytes 1572872 | tf_op jit(solution)/shard_map/ppermute | solution.py:43
  92.5 2.7 %collective-permute-start.16 = (bf16[64,4096]{1,0:T(8,128)(2,1)S(1)}, bf16[64,4096]{1,0:T(8,128)(2,1)S(1)}, u32[]{:S(2)}, u32[]{:S(2)}) collective-permute-start(bf16[64,4096]{1,0:T(8,128)(2,1)S(1)} %shard_map.98.refs_0_), channel_id=1, source_target_pairs={{0,192},{1,193},{2,194},{3,195},{4,196},{5,197},{6,198},{7,199},{8... | collective-permute-start | bytes 1572872 | tf_op jit(solution)/shard_map/ppermute | solution.py:43
  95.2 6.9 %collective-permute-done.17.refs_5_ = bf16[64,4096]{1,0:T(8,128)(2,1)S(1)} collective-permute-done((bf16[64,4096]{1,0:T(8,128)(2,1)S(1)}, bf16[64,4096]{1,0:T(8,128)(2,1)S(1)}, u32[]{:S(2)}, u32[]{:S(2)}) %collective-permute-start.17) | collective-permute-done | bytes 524320 | tf_op jit(solution)/shard_map/ppermute | solution.py:43
  102.1 3.4 %collective-permute-start.19 = (bf16[64,4096]{1,0:T(8,128)(2,1)S(1)}, bf16[64,4096]{1,0:T(8,128)(2,1)S(1)}, u32[]{:S(2)}, u32[]{:S(2)}) collective-permute-start(bf16[64,4096]{1,0:T(8,128)(2,1)S(1)} %collective-permute-done.17.refs_5_), channel_id=1, source_target_pairs={{0,192},{1,193},{2,194},{3,195},{4,196},{5,197},{6,198},{7,199},{8... | collective-permute-start | bytes 1572872 | tf_op jit(solution)/shard_map/ppermute | solution.py:43
  105.5 7.8 %collective-permute-done.16.refs_4_ = bf16[64,4096]{1,0:T(8,128)(2,1)S(1)} collective-permute-done((bf16[64,4096]{1,0:T(8,128)(2,1)S(1)}, bf16[64,4096]{1,0:T(8,128)(2,1)S(1)}, u32[]{:S(2)}, u32[]{:S(2)}) %collective-permute-start.16) | collective-permute-done | bytes 524320 | tf_op jit(solution)/shard_map/ppermute | solution.py:43
  116.5 2.7 %collective-permute-start.10 = (bf16[48,4096]{1,0:T(8,128)(2,1)S(1)}, bf16[48,4096]{1,0:T(8,128)(2,1)S(1)}, u32[]{:S(2)}, u32[]{:S(2)}) collective-permute-start(bf16[48,4096]{1,0:T(8,128)(2,1)S(1)} %collective-permute-done.8.refs_5_.refs_13_), channel_id=1, source_target_pairs={{0,24},{1,25},{2,26},{3,27},{4,28},{5,29},{6,30},{7,31},{8,0},{9,1... | collective-permute-start | bytes 1179656 | tf_op jit(solution)/shard_map/ppermute | solution.py:43
  121.3 3.3 %collective-permute-done.19.refs_7_ = bf16[64,4096]{1,0:T(8,128)(2,1)S(1)} collective-permute-done((bf16[64,4096]{1,0:T(8,128)(2,1)S(1)}, bf16[64,4096]{1,0:T(8,128)(2,1)S(1)}, u32[]{:S(2)}, u32[]{:S(2)}) %collective-permute-start.19) | collective-permute-done | bytes 524320 | tf_op jit(solution)/shard_map/ppermute | solution.py:43
  124.6 2.4 %shard_map.100 = (bf16[128,512]{1,0:T(8,128)(2,1)S(1)}, bf16[128,512]{1,0:T(8,128)(2,1)S(1)}, bf16[256,512]{1,0:T(8,128)(2,1)S(1)}) custom-call(bf16[256,4096]{1,0:T(8,128)(2,1)S(1)} %shard_map.94.x, bf16[256,896]{1,0:T(8,128)(2,1)S(1)} %shard_map.95.cot, bf16[64,4096]{1,0:T(8,128)(2,1)S(1)} %shard_map.98.refs_0_, bf16[64,4096]{1,0:T(8,128)(2,1)S(1)} %shard_map.99.refs_1_, ...), custom_call_target="tpu_custom_call" | custom-call | tf_op jit(solution)/shard_map/pallas_call | solution.py:325
  130.7 3.8 %shard_map.103 = (bf16[2,4,128,512]{3,2,1,0:T(8,128)(2,1)S(1)}, bf16[2,4,128,512]{3,2,1,0:T(8,128)(2,1)S(1)}) custom-call(bf16[256,512]{1,0:T(8,128)(2,1)S(1)} %get-tuple-element.52.dd_a.dd, bf16[256,384]{1,0:T(8,128)(2,1)S(1)} %get-tuple-element.53.dd_b.dd, bf16[64,4096]{1,0:T(8,128)(2,1)S(1)} %shard_map.98.refs_0_, ...), custom_call_target="tpu_custom_call" | custom-call | tf_op jit(solution)/shard_map/pallas_call | solution.py:345
  134.5 5.6 %collective-permute-start.21 = (bf16[2,4,128,512]{3,2,1,0:T(8,128)(2,1)S(1)}, bf16[2,4,128,512]{3,2,1,0:T(8,128)(2,1)S(1)}, u32[]{:S(2)}, u32[]{:S(2)}) collective-permute-start(bf16[2,4,128,512]{3,2,1,0:T(8,128)(2,1)S(1)} %get-tuple-element.55), channel_id=1, source_target_pairs={{0,1},{1,0},{2,3},{3,2},{4,5},{5,4},{6,7},{7,6},{8,9},{9,8},{10,11... | collective-permute-start | bytes 3145736 | tf_op jit(solution)/shard_map/ppermute | solution.py:43
  140.1 2.3 %collective-permute-done.21 = bf16[2,4,128,512]{3,2,1,0:T(8,128)(2,1)S(1)} collective-permute-done((bf16[2,4,128,512]{3,2,1,0:T(8,128)(2,1)S(1)}, bf16[2,4,128,512]{3,2,1,0:T(8,128)(2,1)S(1)}, u32[]{:S(2)}, u32[]{:S(2)}) %collective-permute-start.21) | collective-permute-done | bytes 1048608 | tf_op jit(solution)/shard_map/ppermute | solution.py:43
  143.7 6.2 %all-to-all-start.1 = ((bf16[8,128,512]{2,1,0:T(8,128)(2,1)}), bf16[8,128,512]{2,1,0:T(8,128)(2,1)S(1)}, u32[]{:S(2)}, u32[]{:S(2)}) async-start(bf16[8,128,512]{2,1,0:T(8,128)(2,1)} %shard_map.104), calls=%async_computation.1 | async-start | bytes 2097152 | tf_op jit(solution)/shard_map/all_to_all | solution.py:47
  152.4 2.6 %collective-permute-start.31 = (bf16[48,4096]{1,0:T(8,128)(2,1)S(1)}, bf16[48,4096]{1,0:T(8,128)(2,1)S(1)}, u32[]{:S(2)}, u32[]{:S(2)}) collective-permute-start(bf16[48,4096]{1,0:T(8,128)(2,1)S(1)} %get-tuple-element.74), channel_id=1, source_target_pairs={{0,24},{1,25},{2,26},{3,27},{4,28},{5,29},{6,30},{7,31},{8,0},{9,1... | collective-permute-start | bytes 1179656 | tf_op jit(solution)/shard_map/ppermute | solution.py:43
  156.8 3.5 %collective-permute-start.22 = (bf16[64,4096]{1,0:T(8,128)(2,1)S(1)}, bf16[64,4096]{1,0:T(8,128)(2,1)S(1)}, u32[]{:S(2)}, u32[]{:S(2)}) collective-permute-start(bf16[64,4096]{1,0:T(8,128)(2,1)S(1)} %get-tuple-element.60), channel_id=1, source_target_pairs={{0,192},{1,193},{2,194},{3,195},{4,196},{5,197},{6,198},{7,199},{8... | collective-permute-start | bytes 1572872 | tf_op jit(solution)/shard_map/ppermute | solution.py:43
  160.3 2.7 %collective-permute-start.34 = (bf16[48,4096]{1,0:T(8,128)(2,1)S(1)}, bf16[48,4096]{1,0:T(8,128)(2,1)S(1)}, u32[]{:S(2)}, u32[]{:S(2)}) collective-permute-start(bf16[48,4096]{1,0:T(8,128)(2,1)S(1)} %get-tuple-element.77), channel_id=1, source_target_pairs={{0,24},{1,25},{2,26},{3,27},{4,28},{5,29},{6,30},{7,31},{8,0},{9,1... | collective-permute-start | bytes 1179656 | tf_op jit(solution)/shard_map/ppermute | solution.py:43
  163.0 2.9 %collective-permute-done.32.from_left = bf16[48,4096]{1,0:T(8,128)(2,1)S(1)} collective-permute-done((bf16[48,4096]{1,0:T(8,128)(2,1)S(1)}, bf16[48,4096]{1,0:T(8,128)(2,1)S(1)}, u32[]{:S(2)}, u32[]{:S(2)}) %collective-permute-start.32) | collective-permute-done | bytes 393248 | tf_op jit(solution)/shard_map/ppermute | solution.py:43
  166.7 4.0 %collective-permute-done.22.from_right = bf16[64,4096]{1,0:T(8,128)(2,1)S(1)} collective-permute-done((bf16[64,4096]{1,0:T(8,128)(2,1)S(1)}, bf16[64,4096]{1,0:T(8,128)(2,1)S(1)}, u32[]{:S(2)}, u32[]{:S(2)}) %collective-permute-start.22) | collective-permute-done | bytes 524320 | tf_op jit(solution)/shard_map/ppermute | solution.py:43
  170.7 3.4 %collective-permute-start.25 = (bf16[64,4096]{1,0:T(8,128)(2,1)S(1)}, bf16[64,4096]{1,0:T(8,128)(2,1)S(1)}, u32[]{:S(2)}, u32[]{:S(2)}) collective-permute-start(bf16[64,4096]{1,0:T(8,128)(2,1)S(1)} %get-tuple-element.63), channel_id=1, source_target_pairs={{0,192},{1,193},{2,194},{3,195},{4,196},{5,197},{6,198},{7,199},{8... | collective-permute-start | bytes 1572872 | tf_op jit(solution)/shard_map/ppermute | solution.py:43
  174.4 2.7 %collective-permute-start.24 = (bf16[64,4096]{1,0:T(8,128)(2,1)S(1)}, bf16[64,4096]{1,0:T(8,128)(2,1)S(1)}, u32[]{:S(2)}, u32[]{:S(2)}) collective-permute-start(bf16[64,4096]{1,0:T(8,128)(2,1)S(1)} %get-tuple-element.62), channel_id=1, source_target_pairs={{0,192},{1,193},{2,194},{3,195},{4,196},{5,197},{6,198},{7,199},{8... | collective-permute-start | bytes 1572872 | tf_op jit(solution)/shard_map/ppermute | solution.py:43
  177.1 2.2 %collective-permute-done.33.r_lo = bf16[48,4096]{1,0:T(8,128)(2,1)S(1)} collective-permute-done((bf16[48,4096]{1,0:T(8,128)(2,1)S(1)}, bf16[48,4096]{1,0:T(8,128)(2,1)S(1)}, u32[]{:S(2)}, u32[]{:S(2)}) %collective-permute-start.33) | collective-permute-done | bytes 393248 | tf_op jit(solution)/shard_map/ppermute | solution.py:43
  180.4 3.5 %collective-permute-done.36.l_hi = bf16[48,4096]{1,0:T(8,128)(2,1)S(1)} collective-permute-done((bf16[48,4096]{1,0:T(8,128)(2,1)S(1)}, bf16[48,4096]{1,0:T(8,128)(2,1)S(1)}, u32[]{:S(2)}, u32[]{:S(2)}) %collective-permute-start.36) | collective-permute-done | bytes 393248 | tf_op jit(solution)/shard_map/ppermute | solution.py:43
  183.9 4.8 %collective-permute-start.20 = (bf16[128,896]{1,0:T(8,128)(2,1)S(1)}, bf16[128,896]{1,0:T(8,128)(2,1)S(1)}, u32[]{:S(2)}, u32[]{:S(2)}) collective-permute-start(bf16[128,896]{1,0:T(8,128)(2,1)S(1)} %copy-done.10), channel_id=1, source_target_pairs={{0,32},{1,33},{2,34},{3,35},{4,36},{5,37},{6,38},{7,39},{8,40},{9,... | collective-permute-start | bytes 688136 | tf_op jit(solution)/shard_map/ppermute | solution.py:43
  189.0 2.9 %collective-permute-start.37 = (bf16[24,4096]{1,0:T(8,128)(2,1)S(1)}, bf16[24,4096]{1,0:T(8,128)(2,1)S(1)}, u32[]{:S(2)}, u32[]{:S(2)}) collective-permute-start(bf16[24,4096]{1,0:T(8,128)(2,1)S(1)} %get-tuple-element.81), channel_id=1, source_target_pairs={{0,192},{1,193},{2,194},{3,195},{4,196},{5,197},{6,198},{7,199},{8... | collective-permute-start | bytes 589832 | tf_op jit(solution)/shard_map/ppermute | solution.py:43
  191.9 2.9 %collective-permute-done.24.r_lo = bf16[64,4096]{1,0:T(8,128)(2,1)S(1)} collective-permute-done((bf16[64,4096]{1,0:T(8,128)(2,1)S(1)}, bf16[64,4096]{1,0:T(8,128)(2,1)S(1)}, u32[]{:S(2)}, u32[]{:S(2)}) %collective-permute-start.24) | collective-permute-done | bytes 524320 | tf_op jit(solution)/shard_map/ppermute | solution.py:43
  194.8 3.5 %collective-permute-done.27.l_hi = bf16[64,4096]{1,0:T(8,128)(2,1)S(1)} collective-permute-done((bf16[64,4096]{1,0:T(8,128)(2,1)S(1)}, bf16[64,4096]{1,0:T(8,128)(2,1)S(1)}, u32[]{:S(2)}, u32[]{:S(2)}) %collective-permute-start.27) | collective-permute-done | bytes 524320 | tf_op jit(solution)/shard_map/ppermute | solution.py:43
  198.7 2.5 %collective-permute-start.28 = (bf16[32,4096]{1,0:T(8,128)(2,1)S(1)}, bf16[32,4096]{1,0:T(8,128)(2,1)S(1)}, u32[]{:S(2)}, u32[]{:S(2)}) collective-permute-start(bf16[32,4096]{1,0:T(8,128)(2,1)S(1)} %get-tuple-element.67), channel_id=1, source_target_pairs={{0,24},{1,25},{2,26},{3,27},{4,28},{5,29},{6,30},{7,31},{8,0},{9,1... | collective-permute-start | bytes 786440 | tf_op jit(solution)/shard_map/ppermute | solution.py:43
  205.7 5.7 %collective-permute-done.38.refs_6_ = bf16[24,4096]{1,0:T(8,128)(2,1)S(1)} collective-permute-done((bf16[24,4096]{1,0:T(8,128)(2,1)S(1)}, bf16[24,4096]{1,0:T(8,128)(2,1)S(1)}, u32[]{:S(2)}, u32[]{:S(2)}) %collective-permute-start.38) | collective-permute-done | bytes 196640 | tf_op jit(solution)/shard_map/ppermute | solution.py:43
  (94 shorter events, 38.7 us)
Async XLA Ops:
  33.6 38.3 %all-to-all-start = ((bf16[8,128,512]{2,1,0:T(8,128)(2,1)}), bf16[8,128,512]{2,1,0:T(8,128)(2,1)S(1)}, u32[]{:S(2)}, u32[]{:S(2)}) async-start(bf16[8,128,512]{2,1,0:T(8,128)(2,1)} %get-tuple-element.45), calls=%async_computation | async-start | bytes 2097152 | tf_op jit(solution)/shard_map/all_to_all | solution.py:47
  46.7 29.0 %collective-permute-start.12 = (bf16[32,4096]{1,0:T(8,128)(2,1)S(1)}, bf16[32,4096]{1,0:T(8,128)(2,1)S(1)}, u32[]{:S(2)}, u32[]{:S(2)}) collective-permute-start(bf16[32,4096]{1,0:T(8,128)(2,1)S(1)} %get-tuple-element.47.first), channel_id=1, source_target_pairs={{0,24},{1,25},{2,26},{3,27},{4,28},{5,29},{6,30},{7,31},{8,0},{9,1... | collective-permute-start | bytes 786440 | tf_op jit(solution)/shard_map/ppermute | solution.py:43
  48.2 29.0 %collective-permute-start.13 = (bf16[32,4096]{1,0:T(8,128)(2,1)S(1)}, bf16[32,4096]{1,0:T(8,128)(2,1)S(1)}, u32[]{:S(2)}, u32[]{:S(2)}) collective-permute-start(bf16[32,4096]{1,0:T(8,128)(2,1)S(1)} %get-tuple-element.47.first), channel_id=1, source_target_pairs={{0,16},{1,17},{2,18},{3,19},{4,20},{5,21},{6,22},{7,23},{8,24},{9,... | collective-permute-start | bytes 786440 | tf_op jit(solution)/shard_map/ppermute | solution.py:43
  50.9 22.5 %collective-permute-start.4 = (bf16[24,4096]{1,0:T(8,128)(2,1)S(1)}, bf16[24,4096]{1,0:T(8,128)(2,1)}, u32[]{:S(2)}, u32[]{:S(2)}) collective-permute-start(bf16[24,4096]{1,0:T(8,128)(2,1)S(1)} %get-tuple-element.46.first), channel_id=1, source_target_pairs={{0,128},{1,129},{2,130},{3,131},{4,132},{5,133},{6,134},{7,135},{8... | collective-permute-start | bytes 589832 | tf_op jit(solution)/shard_map/ppermute | solution.py:43
  54.5 40.7 %collective-permute-start.14 = (bf16[64,4096]{1,0:T(8,128)(2,1)S(1)}, bf16[64,4096]{1,0:T(8,128)(2,1)S(1)}, u32[]{:S(2)}, u32[]{:S(2)}) collective-permute-start(bf16[64,4096]{1,0:T(8,128)(2,1)S(1)} %shard_map.98.refs_0_), channel_id=1, source_target_pairs={{0,64},{1,65},{2,66},{3,67},{4,68},{5,69},{6,70},{7,71},{8,72},{9,... | collective-permute-start | bytes 1572872 | tf_op jit(solution)/shard_map/ppermute | solution.py:43
  72.0 44.5 %collective-permute-start = (bf16[8,128,512]{2,1,0:T(8,128)(2,1)S(1)}, bf16[8,128,512]{2,1,0:T(8,128)(2,1)S(1)}, u32[]{:S(2)}, u32[]{:S(2)}) collective-permute-start(bf16[8,128,512]{2,1,0:T(8,128)(2,1)S(1)} %all-to-all-done.own), channel_id=1, source_target_pairs={{0,1},{1,0},{2,3},{3,2},{4,5},{5,4},{6,7},{7,6},{8,9},{9,8},{10,11... | collective-permute-start | bytes 3145736 | tf_op jit(solution)/shard_map/ppermute | solution.py:43
  73.4 19.1 %collective-permute-start.5 = (bf16[48,4096]{1,0:T(8,128)(2,1)S(1)}, bf16[48,4096]{1,0:T(8,128)(2,1)S(1)}, u32[]{:S(2)}, u32[]{:S(2)}) collective-permute-start(bf16[48,4096]{1,0:T(8,128)(2,1)S(1)} %shard_map.96.refs_0_.refs_8_), channel_id=1, source_target_pairs={{0,8},{1,9},{2,10},{3,11},{4,12},{5,13},{6,14},{7,15},{8,16},{9,17... | collective-permute-start | bytes 1179656 | tf_op jit(solution)/shard_map/ppermute | solution.py:43
  75.7 16.8 %collective-permute-start.8 = (bf16[48,4096]{1,0:T(8,128)(2,1)S(1)}, bf16[48,4096]{1,0:T(8,128)(2,1)S(1)}, u32[]{:S(2)}, u32[]{:S(2)}) collective-permute-start(bf16[48,4096]{1,0:T(8,128)(2,1)S(1)} %shard_map.97.refs_1_.refs_9_), channel_id=1, source_target_pairs={{0,24},{1,25},{2,26},{3,27},{4,28},{5,29},{6,30},{7,31},{8,0},{9,1... | collective-permute-start | bytes 1179656 | tf_op jit(solution)/shard_map/ppermute | solution.py:43
  77.2 12.5 %collective-permute-start.1 = (bf16[128,896]{1,0:T(8,128)(2,1)S(1)}, bf16[128,896]{1,0:T(8,128)(2,1)S(1)}, u32[]{:S(2)}, u32[]{:S(2)}) collective-permute-start(bf16[128,896]{1,0:T(8,128)(2,1)S(1)} %copy-done.4), channel_id=1, source_target_pairs={{0,32},{1,33},{2,34},{3,35},{4,36},{5,37},{6,38},{7,39},{8,40},{9,... | collective-permute-start | bytes 688136 | tf_op jit(solution)/shard_map/ppermute | solution.py:43
  89.8 12.3 %collective-permute-start.17 = (bf16[64,4096]{1,0:T(8,128)(2,1)S(1)}, bf16[64,4096]{1,0:T(8,128)(2,1)S(1)}, u32[]{:S(2)}, u32[]{:S(2)}) collective-permute-start(bf16[64,4096]{1,0:T(8,128)(2,1)S(1)} %shard_map.99.refs_1_), channel_id=1, source_target_pairs={{0,192},{1,193},{2,194},{3,195},{4,196},{5,197},{6,198},{7,199},{8... | collective-permute-start | bytes 1572872 | tf_op jit(solution)/shard_map/ppermute | solution.py:43
  92.5 13.0 %collective-permute-start.15 = (bf16[64,4096]{1,0:T(8,128)(2,1)S(1)}, bf16[64,4096]{1,0:T(8,128)(2,1)S(1)}, u32[]{:S(2)}, u32[]{:S(2)}) collective-permute-start(bf16[64,4096]{1,0:T(8,128)(2,1)S(1)} %shard_map.99.refs_1_), channel_id=1, source_target_pairs={{0,64},{1,65},{2,66},{3,67},{4,68},{5,69},{6,70},{7,71},{8,72},{9,... | collective-permute-start | bytes 1572872 | tf_op jit(solution)/shard_map/ppermute | solution.py:43
  92.5 20.8 %collective-permute-start.16 = (bf16[64,4096]{1,0:T(8,128)(2,1)S(1)}, bf16[64,4096]{1,0:T(8,128)(2,1)S(1)}, u32[]{:S(2)}, u32[]{:S(2)}) collective-permute-start(bf16[64,4096]{1,0:T(8,128)(2,1)S(1)} %shard_map.98.refs_0_), channel_id=1, source_target_pairs={{0,192},{1,193},{2,194},{3,195},{4,196},{5,197},{6,198},{7,199},{8... | collective-permute-start | bytes 1572872 | tf_op jit(solution)/shard_map/ppermute | solution.py:43
  95.2 21.3 %collective-permute-start.18 = (bf16[64,4096]{1,0:T(8,128)(2,1)S(1)}, bf16[64,4096]{1,0:T(8,128)(2,1)S(1)}, u32[]{:S(2)}, u32[]{:S(2)}) collective-permute-start(bf16[64,4096]{1,0:T(8,128)(2,1)S(1)} %collective-permute-done.14.refs_2_), channel_id=1, source_target_pairs={{0,64},{1,65},{2,66},{3,67},{4,68},{5,69},{6,70},{7,71},{8,72},{9,... | collective-permute-start | bytes 1572872 | tf_op jit(solution)/shard_map/ppermute | solution.py:43
  102.1 22.5 %collective-permute-start.19 = (bf16[64,4096]{1,0:T(8,128)(2,1)S(1)}, bf16[64,4096]{1,0:T(8,128)(2,1)S(1)}, u32[]{:S(2)}, u32[]{:S(2)}) collective-permute-start(bf16[64,4096]{1,0:T(8,128)(2,1)S(1)} %collective-permute-done.17.refs_5_), channel_id=1, source_target_pairs={{0,192},{1,193},{2,194},{3,195},{4,196},{5,197},{6,198},{7,199},{8... | collective-permute-start | bytes 1572872 | tf_op jit(solution)/shard_map/ppermute | solution.py:43
  105.5 21.5 %collective-permute-start.6 = (bf16[48,4096]{1,0:T(8,128)(2,1)S(1)}, bf16[48,4096]{1,0:T(8,128)(2,1)S(1)}, u32[]{:S(2)}, u32[]{:S(2)}) collective-permute-start(bf16[48,4096]{1,0:T(8,128)(2,1)S(1)} %shard_map.97.refs_1_.refs_9_), channel_id=1, source_target_pairs={{0,8},{1,9},{2,10},{3,11},{4,12},{5,13},{6,14},{7,15},{8,16},{9,17... | collective-permute-start | bytes 1179656 | tf_op jit(solution)/shard_map/ppermute | solution.py:43
  113.4 13.6 %collective-permute-start.7 = (bf16[48,4096]{1,0:T(8,128)(2,1)S(1)}, bf16[48,4096]{1,0:T(8,128)(2,1)S(1)}, u32[]{:S(2)}, u32[]{:S(2)}) collective-permute-start(bf16[48,4096]{1,0:T(8,128)(2,1)S(1)} %shard_map.96.refs_0_.refs_8_), channel_id=1, source_target_pairs={{0,24},{1,25},{2,26},{3,27},{4,28},{5,29},{6,30},{7,31},{8,0},{9,1... | collective-permute-start | bytes 1179656 | tf_op jit(solution)/shard_map/ppermute | solution.py:43
  116.5 11.3 %collective-permute-start.10 = (bf16[48,4096]{1,0:T(8,128)(2,1)S(1)}, bf16[48,4096]{1,0:T(8,128)(2,1)S(1)}, u32[]{:S(2)}, u32[]{:S(2)}) collective-permute-start(bf16[48,4096]{1,0:T(8,128)(2,1)S(1)} %collective-permute-done.8.refs_5_.refs_13_), channel_id=1, source_target_pairs={{0,24},{1,25},{2,26},{3,27},{4,28},{5,29},{6,30},{7,31},{8,0},{9,1... | collective-permute-start | bytes 1179656 | tf_op jit(solution)/shard_map/ppermute | solution.py:43
  143.7 68.8 %all-to-all-start.1 = ((bf16[8,128,512]{2,1,0:T(8,128)(2,1)}), bf16[8,128,512]{2,1,0:T(8,128)(2,1)S(1)}, u32[]{:S(2)}, u32[]{:S(2)}) async-start(bf16[8,128,512]{2,1,0:T(8,128)(2,1)} %shard_map.104), calls=%async_computation.1 | async-start | bytes 2097152 | tf_op jit(solution)/shard_map/all_to_all | solution.py:47
  152.4 10.6 %collective-permute-start.31 = (bf16[48,4096]{1,0:T(8,128)(2,1)S(1)}, bf16[48,4096]{1,0:T(8,128)(2,1)S(1)}, u32[]{:S(2)}, u32[]{:S(2)}) collective-permute-start(bf16[48,4096]{1,0:T(8,128)(2,1)S(1)} %get-tuple-element.74), channel_id=1, source_target_pairs={{0,24},{1,25},{2,26},{3,27},{4,28},{5,29},{6,30},{7,31},{8,0},{9,1... | collective-permute-start | bytes 1179656 | tf_op jit(solution)/shard_map/ppermute | solution.py:43
  154.9 10.9 %collective-permute-start.32 = (bf16[48,4096]{1,0:T(8,128)(2,1)S(1)}, bf16[48,4096]{1,0:T(8,128)(2,1)S(1)}, u32[]{:S(2)}, u32[]{:S(2)}) collective-permute-start(bf16[48,4096]{1,0:T(8,128)(2,1)S(1)} %get-tuple-element.75), channel_id=1, source_target_pairs={{0,8},{1,9},{2,10},{3,11},{4,12},{5,13},{6,14},{7,15},{8,16},{9,17... | collective-permute-start | bytes 1179656 | tf_op jit(solution)/shard_map/ppermute | solution.py:43
  156.8 13.8 %collective-permute-start.22 = (bf16[64,4096]{1,0:T(8,128)(2,1)S(1)}, bf16[64,4096]{1,0:T(8,128)(2,1)S(1)}, u32[]{:S(2)}, u32[]{:S(2)}) collective-permute-start(bf16[64,4096]{1,0:T(8,128)(2,1)S(1)} %get-tuple-element.60), channel_id=1, source_target_pairs={{0,192},{1,193},{2,194},{3,195},{4,196},{5,197},{6,198},{7,199},{8... | collective-permute-start | bytes 1572872 | tf_op jit(solution)/shard_map/ppermute | solution.py:43
  160.3 13.8 %collective-permute-start.23 = (bf16[64,4096]{1,0:T(8,128)(2,1)S(1)}, bf16[64,4096]{1,0:T(8,128)(2,1)S(1)}, u32[]{:S(2)}, u32[]{:S(2)}) collective-permute-start(bf16[64,4096]{1,0:T(8,128)(2,1)S(1)} %get-tuple-element.61), channel_id=1, source_target_pairs={{0,64},{1,65},{2,66},{3,67},{4,68},{5,69},{6,70},{7,71},{8,72},{9,... | collective-permute-start | bytes 1572872 | tf_op jit(solution)/shard_map/ppermute | solution.py:43
  160.3 14.0 %collective-permute-start.34 = (bf16[48,4096]{1,0:T(8,128)(2,1)S(1)}, bf16[48,4096]{1,0:T(8,128)(2,1)S(1)}, u32[]{:S(2)}, u32[]{:S(2)}) collective-permute-start(bf16[48,4096]{1,0:T(8,128)(2,1)S(1)} %get-tuple-element.77), channel_id=1, source_target_pairs={{0,24},{1,25},{2,26},{3,27},{4,28},{5,29},{6,30},{7,31},{8,0},{9,1... | collective-permute-start | bytes 1179656 | tf_op jit(solution)/shard_map/ppermute | solution.py:43
  163.0 11.4 %collective-permute-start.35 = (bf16[48,4096]{1,0:T(8,128)(2,1)S(1)}, bf16[48,4096]{1,0:T(8,128)(2,1)S(1)}, u32[]{:S(2)}, u32[]{:S(2)}) collective-permute-start(bf16[48,4096]{1,0:T(8,128)(2,1)S(1)} %get-tuple-element.78), channel_id=1, source_target_pairs={{0,8},{1,9},{2,10},{3,11},{4,12},{5,13},{6,14},{7,15},{8,16},{9,17... | collective-permute-start | bytes 1179656 | tf_op jit(solution)/shard_map/ppermute | solution.py:43
  166.1 13.3 %collective-permute-start.33 = (bf16[48,4096]{1,0:T(8,128)(2,1)S(1)}, bf16[48,4096]{1,0:T(8,128)(2,1)S(1)}, u32[]{:S(2)}, u32[]{:S(2)}) collective-permute-start(bf16[48,4096]{1,0:T(8,128)(2,1)S(1)} %get-tuple-element.76), channel_id=1, source_target_pairs={{0,24},{1,25},{2,26},{3,27},{4,28},{5,29},{6,30},{7,31},{8,0},{9,1... | collective-permute-start | bytes 1179656 | tf_op jit(solution)/shard_map/ppermute | solution.py:43
  170.7 18.3 %collective-permute-start.25 = (bf16[64,4096]{1,0:T(8,128)(2,1)S(1)}, bf16[64,4096]{1,0:T(8,128)(2,1)S(1)}, u32[]{:S(2)}, u32[]{:S(2)}) collective-permute-start(bf16[64,4096]{1,0:T(8,128)(2,1)S(1)} %get-tuple-element.63), channel_id=1, source_target_pairs={{0,192},{1,193},{2,194},{3,195},{4,196},{5,197},{6,198},{7,199},{8... | collective-permute-start | bytes 1572872 | tf_op jit(solution)/shard_map/ppermute | solution.py:43
  174.3 17.6 %collective-permute-start.26 = (bf16[64,4096]{1,0:T(8,128)(2,1)S(1)}, bf16[64,4096]{1,0:T(8,128)(2,1)S(1)}, u32[]{:S(2)}, u32[]{:S(2)}) collective-permute-start(bf16[64,4096]{1,0:T(8,128)(2,1)S(1)} %get-tuple-element.64), channel_id=1, source_target_pairs={{0,64},{1,65},{2,66},{3,67},{4,68},{5,69},{6,70},{7,71},{8,72},{9,... | collective-permute-start | bytes 1572872 | tf_op jit(solution)/shard_map/ppermute | solution.py:43
  174.4 20.4 %collective-permute-start.24 = (bf16[64,4096]{1,0:T(8,128)(2,1)S(1)}, bf16[64,4096]{1,0:T(8,128)(2,1)S(1)}, u32[]{:S(2)}, u32[]{:S(2)}) collective-permute-start(bf16[64,4096]{1,0:T(8,128)(2,1)S(1)} %get-tuple-element.62), channel_id=1, source_target_pairs={{0,192},{1,193},{2,194},{3,195},{4,196},{5,197},{6,198},{7,199},{8... | collective-permute-start | bytes 1572872 | tf_op jit(solution)/shard_map/ppermute | solution.py:43
  179.3 19.0 %collective-permute-start.27 = (bf16[64,4096]{1,0:T(8,128)(2,1)S(1)}, bf16[64,4096]{1,0:T(8,128)(2,1)S(1)}, u32[]{:S(2)}, u32[]{:S(2)}) collective-permute-start(bf16[64,4096]{1,0:T(8,128)(2,1)S(1)} %get-tuple-element.65), channel_id=1, source_target_pairs={{0,64},{1,65},{2,66},{3,67},{4,68},{5,69},{6,70},{7,71},{8,72},{9,... | collective-permute-start | bytes 1572872 | tf_op jit(solution)/shard_map/ppermute | solution.py:43
  183.9 19.3 %collective-permute-start.20 = (bf16[128,896]{1,0:T(8,128)(2,1)S(1)}, bf16[128,896]{1,0:T(8,128)(2,1)S(1)}, u32[]{:S(2)}, u32[]{:S(2)}) collective-permute-start(bf16[128,896]{1,0:T(8,128)(2,1)S(1)} %copy-done.10), channel_id=1, source_target_pairs={{0,32},{1,33},{2,34},{3,35},{4,36},{5,37},{6,38},{7,39},{8,40},{9,... | collective-permute-start | bytes 688136 | tf_op jit(solution)/shard_map/ppermute | solution.py:43
  189.0 14.2 %collective-permute-start.37 = (bf16[24,4096]{1,0:T(8,128)(2,1)S(1)}, bf16[24,4096]{1,0:T(8,128)(2,1)S(1)}, u32[]{:S(2)}, u32[]{:S(2)}) collective-permute-start(bf16[24,4096]{1,0:T(8,128)(2,1)S(1)} %get-tuple-element.81), channel_id=1, source_target_pairs={{0,192},{1,193},{2,194},{3,195},{4,196},{5,197},{6,198},{7,199},{8... | collective-permute-start | bytes 589832 | tf_op jit(solution)/shard_map/ppermute | solution.py:43
  198.7 12.7 %collective-permute-start.28 = (bf16[32,4096]{1,0:T(8,128)(2,1)S(1)}, bf16[32,4096]{1,0:T(8,128)(2,1)S(1)}, u32[]{:S(2)}, u32[]{:S(2)}) collective-permute-start(bf16[32,4096]{1,0:T(8,128)(2,1)S(1)} %get-tuple-element.67), channel_id=1, source_target_pairs={{0,24},{1,25},{2,26},{3,27},{4,28},{5,29},{6,30},{7,31},{8,0},{9,1... | collective-permute-start | bytes 786440 | tf_op jit(solution)/shard_map/ppermute | solution.py:43
  (21 other events, 237.2 us)

commit v3 on v2

--- a/solution.py
+++ b/solution.py
@@ -16,6 +16,7 @@
 NY, NZH, NX, NZL, NC = 4, 2, 4, 4, 2
 NZ = NZH * NZL
 GROUPS = NY * NZH * NX
+HALF = NX * ROWS
 REL = (0, -1, 1, 2)
 HALF_A, HALF_B = 16, 12
 SHARD_A, SHARD_B = 2 * HALF_A, 2 * HALF_B
@@ -71,16 +72,20 @@
     return pl.BlockSpec(dims, lambda n: (0,) * len(dims))
 
 
-def dequant_kernel(tokens, *refs):
-    sources, (a, b, spread), (gc, gs, uc, us), sems = refs[:4], refs[4:7], refs[7:11], refs[11]
-    pairs = list(zip(sources, (gc, gs, uc, us))) + [(tokens, spread.at[n]) for n in range(NZ)]
-    copies = [
+def dequant_kernel(tokens, cot, *refs):
+    sources, (a, b, spread, sent), scratch, sems = refs[:4], refs[4:8], refs[8:14], refs[14]
+    gc, gs, uc, us, toks, back = scratch
+    inputs = [
         pltpu.make_async_copy(source, target, sems.at[n])
-        for n, (source, target) in enumerate(pairs)
+        for n, (source, target) in enumerate(zip((*sources, tokens, cot), scratch))
     ]
+    copies = [pltpu.make_async_copy(toks, spread.at[n], sems.at[6 + n]) for n in range(NZ)]
+    for copy in inputs:
+        copy.start()
+    inputs[4].wait()
     for copy in copies:
         copy.start()
-    for copy in copies[:4]:
+    for copy in inputs[:4]:
         copy.wait()
     scales_g, scales_u = gs[...].T, us[...].T
     for n in range(D // BLOCK):
@@ -89,7 +94,15 @@
         u = uc[:, cols].astype(F32) * scales_u[:, n : n + 1]
         a[:, cols] = jnp.concatenate([g[:HALF_A], u[:HALF_A]], axis=0).astype(BF16)
         b[:, cols] = jnp.concatenate([g[HALF_A:], u[HALF_A:]], axis=0).astype(BF16)
-    for copy in copies[4:]:
+    inputs[5].wait()
+    even, odd = (
+        jnp.concatenate(
+            [back[:, (2 * n + half) * HALF : (2 * n + half + 1) * HALF] for n in range(NY)], axis=1
+        )
+        for half in range(NZH)
+    )
+    sent[...] = jnp.where(lax.axis_index("zh") == 0, odd, even)
+    for copy in copies:
         copy.wait()
 
 
@@ -103,25 +116,26 @@
     return jnp.where(n == 1, 3, jnp.where(n == 2, 1, jnp.where(n == 3, 2, 0)))
 
 
-def one_hot(flip):
+def one_hot(flip, compact=False):
     y, zh, x = lax.axis_index("y"), lax.axis_index("zh"), lax.axis_index("x")
-    half = jnp.bitwise_xor(zh, flip)
+    halves = 1 if compact else NZH
+    half = 0 if compact else jnp.bitwise_xor(zh, flip)
     col = lax.broadcasted_iota(jnp.int32, (1, WIDE_A), 1)
     s, r = col // SHARD_A, col % SHARD_A
     yy, xx = (y + rel_of(s // 4)) % NY, (x + rel_of(s % 4)) % NX
-    a = jnp.where(r < HALF_A, ((yy * NZH + half) * NX + xx) * ROWS + r, -1)
+    a = jnp.where(r < HALF_A, ((yy * halves + half) * NX + xx) * ROWS + r, -1)
     col = lax.broadcasted_iota(jnp.int32, (1, WIDE_B), 1)
     s, r = col // SHARD_B, col % SHARD_B
     yy, xx = (y + rel_of(s % 4)) % NY, (x + rel_of(s // 4)) % NX
-    b = jnp.where(r < HALF_B, ((yy * NZH + half) * NX + xx) * ROWS + HALF_A + r, -1)
+    b = jnp.where(r < HALF_B, ((yy * halves + half) * NX + xx) * ROWS + HALF_A + r, -1)
     origin = jnp.concatenate([a, b], axis=1)
-    rows = lax.broadcasted_iota(jnp.int32, (GROUPS * ROWS, WIDE), 0)
+    rows = lax.broadcasted_iota(jnp.int32, (NY * halves * HALF, WIDE), 0)
     return (rows == origin).astype(F32).astype(BF16)
 
 
 def spread_kernel(mine, partner, out):
-    both = jnp.concatenate([mine[...], partner[...]], axis=0)
-    out[...] = jnp.dot(both, one_hot(0), preferred_element_type=F32).astype(BF16)
+    out[:TOK] = jnp.dot(mine[...], one_hot(0), preferred_element_type=F32).astype(BF16)
+    out[TOK:] = jnp.dot(partner[...], one_hot(0, True), preferred_element_type=F32).astype(BF16)
 
 
 def collect_kernel(mine, partner, out, acc):
@@ -241,19 +255,13 @@
     out[...] = total.astype(BF16)
 
 
-def relay_kernel(left, right, from_right, from_left, left_out, right_out):
-    left_out[...] = (left[...].astype(F32) + from_right[...].astype(F32)).astype(BF16)
-    right_out[...] = (right[...].astype(F32) + from_left[...].astype(F32)).astype(BF16)
-
-
-def stage_kernel(own_lo, own_hi, r_lo, r_hi, l_lo, l_hi, *outs):
-    rows = own_lo.shape[0] // 2
-    lo = own_lo[...].astype(F32) + r_lo[...].astype(F32) + l_lo[...].astype(F32)
-    hi = own_hi[...].astype(F32) + r_hi[...].astype(F32) + l_hi[...].astype(F32)
-    outs[0][...] = lo[:rows].astype(BF16)
-    outs[1][...] = lo[rows:].astype(BF16)
-    outs[2][...] = hi[:rows].astype(BF16)
-    outs[3][...] = hi[rows:].astype(BF16)
+def stage_kernel(own, right, left, far, *outs):
+    rows = own.shape[0] // 4
+    for n, out in enumerate(outs):
+        part = slice(n * rows, (n + 1) * rows)
+        total = own[part].astype(F32) + right[part].astype(F32)
+        total = total + (left[part].astype(F32) + far[part].astype(F32))
+        out[...] = total.astype(BF16)
 
 
 def finish_kernel(*refs):
@@ -279,20 +287,9 @@
 
 
 def reduce_plane(parts, first, second):
-    own_lo, own_hi, left_lo, left_hi, right_lo, right_hi, far_lo, far_hi = parts
-    n = far_lo.shape[0]
-    from_right = shift(far_lo, **{second: -1})
-    from_left = shift(far_hi, **{second: 1})
-    r_hi = shift(left_hi, **{second: -1})
-    l_lo = shift(right_lo, **{second: 1})
-    left_lo, right_hi = call(relay_kernel, (shape(n, D), shape(n, D)))(
-        left_lo, right_hi, from_right, from_left
-    )
-    r_lo = shift(left_lo, **{second: -1})
-    l_hi = shift(right_hi, **{second: 1})
-    pieces = call(stage_kernel, tuple(shape(n // 2, D) for _ in REL))(
-        own_lo, own_hi, r_lo, r_hi, l_lo, l_hi
-    )
+    arrived = [parts[0]] + [shift(p, **{second: r}) for p, r in zip(parts[1:], REL[1:])]
+    rows = parts[0].shape[0] // 4
+    pieces = call(stage_kernel, tuple(shape(rows, D) for _ in REL))(*arrived)
     return [pieces[0]] + [shift(p, **{first: r}) for p, r in zip(pieces[1:], REL[1:])]
 
 
@@ -300,15 +297,16 @@
     sources = (gate_codes, gate_scales.T, up_codes, up_scales.T)
     cube_shape = jax.ShapeDtypeStruct((NZ, TOK, SLICE), BF16)
     hbm = pl.BlockSpec(memory_space=pltpu.HBM)
-    shard_a, shard_b, copies = call(
+    inputs = sources + (tokens, cotangent)
+    shard_a, shard_b, copies, cot_sent = call(
         dequant_kernel,
-        (shape(SHARD_A, D), shape(SHARD_B, D), cube_shape),
-        4,
-        in_specs=[hbm] * 5,
-        out_specs=(VMEM, VMEM, hbm),
-        scratch_shapes=[pltpu.VMEM(v.shape, v.dtype) for v in sources]
-        + [pltpu.SemaphoreType.DMA((4 + NZ,))],
-    )(in_hbm(tokens), *[in_hbm(v) for v in sources])
+        (shape(SHARD_A, D), shape(SHARD_B, D), cube_shape, shape(TOK, NY * HALF)),
+        8,
+        in_specs=[hbm] * 6,
+        out_specs=(VMEM, VMEM, hbm, VMEM),
+        scratch_shapes=[pltpu.VMEM(v.shape, v.dtype) for v in inputs]
+        + [pltpu.SemaphoreType.DMA((len(inputs) + NZ,))],
+    )(in_hbm(tokens), in_hbm(cotangent), *[in_hbm(v) for v in sources])
     wa = gather_plane(shard_a, "dx", "dy")
     wb = gather_plane(shard_b, "dy", "dx")
 
@@ -316,7 +314,7 @@
     theirs = shift(mine, dc=1)
     whole = call(join_kernel, shape(2 * TOK, D), 8)(mine, theirs)
 
-    cot = call(spread_kernel, shape(2 * TOK, WIDE))(cotangent, shift(cotangent, dz=4))
+    cot = call(spread_kernel, shape(2 * TOK, WIDE))(cotangent, shift(cot_sent, dz=4))
 
     def forward(w, half, lower, *before):
         shard = 2 * half
@@ -328,26 +326,25 @@
             scratch_shapes=[pltpu.VMEM((2 * TOK, width), F32)],
         )(whole, cot, *w, *before)
 
-    def weight_grad(dd, parts):
-        return call(weight_grad_kernel, tuple(shape(p.shape[0], D) for p in parts))(
-            dd, whole
-        )
+    def weight_grad(dd):
+        outs = tuple(shape(dd.shape[1] // 4, D) for _ in REL)
+        return call(weight_grad_kernel, outs)(dd, whole)
 
     hm_a, hp_a, dd_a = forward(wa, HALF_A, 0)
     hidden_mine, hidden_sent, dd_b = forward(wb, HALF_B, WIDE_A, hm_a, hp_a)
-    sums_a = reduce_plane(weight_grad(dd_a, wa), "dx", "dy")
-    sums_b = reduce_plane(weight_grad(dd_b, wb), "dy", "dx")
+    sums_a = reduce_plane(weight_grad(dd_a), "dx", "dy")
+    sums_b = reduce_plane(weight_grad(dd_b), "dy", "dx")
     gate_grad, up_grad = call(
         finish_kernel, (shape(ROWS, D, F32), shape(ROWS, D, F32))
     )(*sums_a, *sums_b)
 
     quad = jax.ShapeDtypeStruct((2, NZL, TOK, SLICE), BF16)
-    own_tg, other_tg = call(token_grad_kernel, (quad, quad), 20)(dd_a, dd_b, *wa, *wb)
+    own_tg, other_tg = call(token_grad_kernel, (quad, quad), 20)(
+        dd_a, dd_b, *wa, *wb
+    )
     cube = (NZ, TOK, SLICE)
     received = shift(other_tg, dc=1)
-    blocks = call(pair_sum_kernel, cube_shape, 8)(
-        own_tg.reshape(cube), received.reshape(cube)
-    )
+    blocks = call(pair_sum_kernel, cube_shape, 8)(own_tg.reshape(cube), received.reshape(cube))
     token_grad = call(total_kernel, shape(TOK, SLICE))(exchange_z(blocks))
 
     hidden = call(

time: 217 us -> 194 us (0.89)
  Pallas kernels: 53 us -> 24 us
  waiting for transfers between devices: 78.1 us -> 87.2 us
  starting transfers between devices: 76.8 us -> 74 us
    pallas_call x8 -> x6, Pallas kernels: 38.2 us -> 9.26 us  [the longest x2 4.32 us: weight_grad(): return call(weight_grad_kernel, outs)(dd, whole)]
    ppermute x40 -> x34, waiting for transfers between devices: 61.1 us -> 68.3 us  [shift(): return lax.ppermute(value, AXES, pairs)]
    ppermute x40 -> x34, starting transfers between devices: 61.5 us -> 58.5 us  [shift(): return lax.ppermute(value, AXES, pairs)]
    unnamed x22 -> x28, local copies, waits for them, and re-layouts: 4.45 us -> 6.25 us
  transfers between devices with their start and end apart: 42 -> 36, of which waited for: 16 -> 16; matrix products, arithmetic and copies ran while one was open for 0% -> 0% of each run, Pallas kernels for 6% -> 8%
where the time goes in v3:
time: 194 us; the launch traced here: 192 us
  waiting for transfers between devices  87.2 us (45%)
  starting transfers between devices  74 us (38%)
  Pallas kernels  24 us (12%)
  local copies, waits for them, and re-layouts  6.25 us (3%)
    ppermute x34, waiting for transfers between devices, shift(): return lax.ppermute(value, AXES, pairs)  68.3 us
    ppermute x34, starting transfers between devices, shift(): return lax.ppermute(value, AXES, pairs)  58.5 us
    all_to_all x2, waiting for transfers between devices, exchange_z(): return lax.all_to_all(value, ('zh', 'zl'), 0, 0, tiled=True)  18.9 us
    all_to_all x2, starting transfers between devices, exchange_z(): return lax.all_to_all(value, ('zh', 'zl'), 0, 0, tiled=True)  15.5 us
    unnamed x28, local copies, waits for them, and re-layouts  6.25 us
    pallas_call x2, Pallas kernels, forward(): call(functools.partial(forward_kernel, shard, half, lower), (shape(TOK, t...  4.6 us
    pallas_call x2, Pallas kernels, weight_grad(): return call(weight_grad_kernel, outs)(dd, whole)  4.32 us
  transfers between devices with their start and end apart: 36, of which 16 were waited for; matrix products, arithmetic and copies ran while one was open for 0% of the time, Pallas kernels for 8%

profile of v3, /device:TPU:1, one launch (start us, length us, event | category | flops | bytes accessed | tf_op | source)
XLA Modules:
  0.0 192.3 jit_solution(4370625839281952740)
XLA Ops:
  0.6 2.2 %shard_map.93 = (bf16[32,4096]{1,0:T(8,128)(2,1)S(1)}, bf16[24,4096]{1,0:T(8,128)(2,1)S(1)}, bf16[8,128,512]{2,1,0:T(8,128)(2,1)}, bf16[128,448]{1,0:T(8,128)(2,1)S(1)}) custom-call(bf16[128,512]{1,0:T(8,128)(2,1)} %tokens.1, bf16[128,896]{1,0:T(8,128)(2,1)} %mine.1, bf16[28,4096]{1,0:T(8,128)(2,1)} %refs_0_.1, f32[16,28]{1,0:T(8,128)} %bitcast.6, ...), custom_call_target="tpu_custom_call" | custom-call | tf_op jit(solution)/shard_map/pallas_call | solution.py:301
  2.9 9.0 %all-to-all-start = ((bf16[8,128,512]{2,1,0:T(8,128)(2,1)}), bf16[8,128,512]{2,1,0:T(8,128)(2,1)S(1)}, u32[]{:S(2)}, u32[]{:S(2)}) async-start(bf16[8,128,512]{2,1,0:T(8,128)(2,1)} %get-tuple-element.34), calls=%async_computation | async-start | bytes 2097152 | tf_op jit(solution)/shard_map/all_to_all | solution.py:48
  22.2 18.9 %all-to-all-done.own = bf16[8,128,512]{2,1,0:T(8,128)(2,1)S(1)} async-done(((bf16[8,128,512]{2,1,0:T(8,128)(2,1)}), bf16[8,128,512]{2,1,0:T(8,128)(2,1)S(1)}, u32[]{:S(2)}, u32[]{:S(2)}) %all-to-all-start) | async-done | bytes 1048608 | tf_op jit(solution)/shard_map/all_to_all | solution.py:48
  41.6 2.7 %collective-permute-start.13 = (bf16[32,4096]{1,0:T(8,128)(2,1)S(1)}, bf16[32,4096]{1,0:T(8,128)(2,1)S(1)}, u32[]{:S(2)}, u32[]{:S(2)}) collective-permute-start(bf16[32,4096]{1,0:T(8,128)(2,1)S(1)} %get-tuple-element.37.first), channel_id=1, source_target_pairs={{0,16},{1,17},{2,18},{3,19},{4,20},{5,21},{6,22},{7,23},{8,24},{9,... | collective-permute-start | bytes 786440 | tf_op jit(solution)/shard_map/ppermute | solution.py:44
  46.6 2.4 %collective-permute-start.8 = (bf16[48,4096]{1,0:T(8,128)(2,1)S(1)}, bf16[48,4096]{1,0:T(8,128)(2,1)S(1)}, u32[]{:S(2)}, u32[]{:S(2)}) collective-permute-start(bf16[48,4096]{1,0:T(8,128)(2,1)S(1)} %shard_map.97.refs_1_.refs_9_), channel_id=1, source_target_pairs={{0,24},{1,25},{2,26},{3,27},{4,28},{5,29},{6,30},{7,31},{8,0},{9,1... | collective-permute-start | bytes 1179656 | tf_op jit(solution)/shard_map/ppermute | solution.py:44
  49.1 1.8 collective-permute-done.13.second
  51.2 7.5 %collective-permute-done.1.partner = bf16[128,448]{1,0:T(8,128)(2,1)S(1)} collective-permute-done((bf16[128,448]{1,0:T(8,128)(2,1)S(1)}, bf16[128,448]{1,0:T(8,128)(2,1)S(1)}, u32[]{:S(2)}, u32[]{:S(2)}) %collective-permute-start.1) | collective-permute-done | bytes 114720 | tf_op jit(solution)/shard_map/ppermute | solution.py:44
  58.7 2.7 %collective-permute-start.17 = (bf16[64,4096]{1,0:T(8,128)(2,1)S(1)}, bf16[64,4096]{1,0:T(8,128)(2,1)S(1)}, u32[]{:S(2)}, u32[]{:S(2)}) collective-permute-start(bf16[64,4096]{1,0:T(8,128)(2,1)S(1)} %shard_map.99.refs_1_), channel_id=1, source_target_pairs={{0,192},{1,193},{2,194},{3,195},{4,196},{5,197},{6,198},{7,199},{8... | collective-permute-start | bytes 1572872 | tf_op jit(solution)/shard_map/ppermute | solution.py:44
  61.5 2.7 %collective-permute-start.16 = (bf16[64,4096]{1,0:T(8,128)(2,1)S(1)}, bf16[64,4096]{1,0:T(8,128)(2,1)S(1)}, u32[]{:S(2)}, u32[]{:S(2)}) collective-permute-start(bf16[64,4096]{1,0:T(8,128)(2,1)S(1)} %shard_map.98.refs_0_), channel_id=1, source_target_pairs={{0,192},{1,193},{2,194},{3,195},{4,196},{5,197},{6,198},{7,199},{8... | collective-permute-start | bytes 1572872 | tf_op jit(solution)/shard_map/ppermute | solution.py:44
  64.1 4.5 %collective-permute-done.17.refs_5_ = bf16[64,4096]{1,0:T(8,128)(2,1)S(1)} collective-permute-done((bf16[64,4096]{1,0:T(8,128)(2,1)S(1)}, bf16[64,4096]{1,0:T(8,128)(2,1)S(1)}, u32[]{:S(2)}, u32[]{:S(2)}) %collective-permute-start.17) | collective-permute-done | bytes 524320 | tf_op jit(solution)/shard_map/ppermute | solution.py:44
  68.7 3.4 %collective-permute-start.19 = (bf16[64,4096]{1,0:T(8,128)(2,1)S(1)}, bf16[64,4096]{1,0:T(8,128)(2,1)S(1)}, u32[]{:S(2)}, u32[]{:S(2)}) collective-permute-start(bf16[64,4096]{1,0:T(8,128)(2,1)S(1)} %collective-permute-done.17.refs_5_), channel_id=1, source_target_pairs={{0,192},{1,193},{2,194},{3,195},{4,196},{5,197},{6,198},{7,199},{8... | collective-permute-start | bytes 1572872 | tf_op jit(solution)/shard_map/ppermute | solution.py:44
  73.3 6.6 %collective-permute-done.16.refs_4_ = bf16[64,4096]{1,0:T(8,128)(2,1)S(1)} collective-permute-done((bf16[64,4096]{1,0:T(8,128)(2,1)S(1)}, bf16[64,4096]{1,0:T(8,128)(2,1)S(1)}, u32[]{:S(2)}, u32[]{:S(2)}) %collective-permute-start.16) | collective-permute-done | bytes 524320 | tf_op jit(solution)/shard_map/ppermute | solution.py:44
  79.9 2.5 %collective-permute-start.7 = (bf16[48,4096]{1,0:T(8,128)(2,1)S(1)}, bf16[48,4096]{1,0:T(8,128)(2,1)S(1)}, u32[]{:S(2)}, u32[]{:S(2)}) collective-permute-start(bf16[48,4096]{1,0:T(8,128)(2,1)S(1)} %shard_map.96.refs_0_.refs_8_), channel_id=1, source_target_pairs={{0,24},{1,25},{2,26},{3,27},{4,28},{5,29},{6,30},{7,31},{8,0},{9,1... | collective-permute-start | bytes 1179656 | tf_op jit(solution)/shard_map/ppermute | solution.py:44
  87.8 3.4 %collective-permute-done.19.refs_7_ = bf16[64,4096]{1,0:T(8,128)(2,1)S(1)} collective-permute-done((bf16[64,4096]{1,0:T(8,128)(2,1)S(1)}, bf16[64,4096]{1,0:T(8,128)(2,1)S(1)}, u32[]{:S(2)}, u32[]{:S(2)}) %collective-permute-start.19) | collective-permute-done | bytes 524320 | tf_op jit(solution)/shard_map/ppermute | solution.py:44
  91.1 2.4 %shard_map.100 = (bf16[128,512]{1,0:T(8,128)(2,1)S(1)}, bf16[128,512]{1,0:T(8,128)(2,1)S(1)}, bf16[256,512]{1,0:T(8,128)(2,1)S(1)}) custom-call(bf16[256,4096]{1,0:T(8,128)(2,1)S(1)} %shard_map.94.x, bf16[256,896]{1,0:T(8,128)(2,1)S(1)} %shard_map.95.cot, bf16[64,4096]{1,0:T(8,128)(2,1)S(1)} %shard_map.98.refs_0_, bf16[64,4096]{1,0:T(8,128)(2,1)S(1)} %shard_map.99.refs_1_, ...), custom_call_target="tpu_custom_call" | custom-call | tf_op jit(solution)/shard_map/pallas_call | solution.py:323
  94.3 2.2 %shard_map.101 = (bf16[128,896]{1,0:T(8,128)(2,1)S(1)}, bf16[128,896]{1,0:T(8,128)(2,1)S(1)}, bf16[256,384]{1,0:T(8,128)(2,1)S(1)}) custom-call(bf16[256,4096]{1,0:T(8,128)(2,1)S(1)} %shard_map.94.x, bf16[256,896]{1,0:T(8,128)(2,1)S(1)} %shard_map.95.cot, bf16[48,4096]{1,0:T(8,128)(2,1)S(1)} %shard_map.96.refs_0_.refs_8_, ...), custom_call_target="tpu_custom_call" | custom-call | tf_op jit(solution)/shard_map/pallas_call | solution.py:323
  97.2 3.8 %shard_map.103 = (bf16[2,4,128,512]{3,2,1,0:T(8,128)(2,1)S(1)}, bf16[2,4,128,512]{3,2,1,0:T(8,128)(2,1)S(1)}) custom-call(bf16[256,512]{1,0:T(8,128)(2,1)S(1)} %get-tuple-element.42.dd_a.dd, bf16[256,384]{1,0:T(8,128)(2,1)S(1)} %get-tuple-element.43.dd_b.dd, bf16[64,4096]{1,0:T(8,128)(2,1)S(1)} %shard_map.98.refs_0_, ...), custom_call_target="tpu_custom_call" | custom-call | tf_op jit(solution)/shard_map/pallas_call | solution.py:342
  101.0 7.4 %collective-permute-start.21 = (bf16[2,4,128,512]{3,2,1,0:T(8,128)(2,1)S(1)}, bf16[2,4,128,512]{3,2,1,0:T(8,128)(2,1)S(1)}, u32[]{:S(2)}, u32[]{:S(2)}) collective-permute-start(bf16[2,4,128,512]{3,2,1,0:T(8,128)(2,1)S(1)} %get-tuple-element.45), channel_id=1, source_target_pairs={{0,1},{1,0},{2,3},{3,2},{4,5},{5,4},{6,7},{7,6},{8,9},{9,8},{10,11... | collective-permute-start | bytes 3145736 | tf_op jit(solution)/shard_map/ppermute | solution.py:44
  108.4 2.4 %shard_map.108 = (bf16[96,4096]{1,0:T(8,128)(2,1)S(1)}, bf16[96,4096]{1,0:T(8,128)(2,1)}, bf16[96,4096]{1,0:T(8,128)(2,1)S(1)}, bf16[96,4096]{1,0:T(8,128)(2,1)S(1)}) custom-call(bf16[256,384]{1,0:T(8,128)(2,1)S(1)} %get-tuple-element.43.dd_b.dd, bf16[256,4096]{1,0:T(8,128)(2,1)S(1)} %shard_map.94.x), custom_call_target="tpu_custom_call" | custom-call | tf_op jit(solution)/shard_map/pallas_call | solution.py:331
  113.6 3.4 %collective-permute-start.28 = (bf16[96,4096]{1,0:T(8,128)(2,1)}, bf16[96,4096]{1,0:T(8,128)(2,1)}, u32[]{:S(2)}, u32[]{:S(2)}) collective-permute-start(bf16[96,4096]{1,0:T(8,128)(2,1)} %get-tuple-element.55), channel_id=1, source_target_pairs={{0,24},{1,25},{2,26},{3,27},{4,28},{5,29},{6,30},{7,31},{8,0},{9,1... | collective-permute-start | bytes 2359304 | tf_op jit(solution)/shard_map/ppermute | solution.py:44
  118.2 6.5 %all-to-all-start.1 = ((bf16[8,128,512]{2,1,0:T(8,128)(2,1)}), bf16[8,128,512]{2,1,0:T(8,128)(2,1)S(1)}, u32[]{:S(2)}, u32[]{:S(2)}) async-start(bf16[8,128,512]{2,1,0:T(8,128)(2,1)} %shard_map.104), calls=%async_computation.1 | async-start | bytes 2097152 | tf_op jit(solution)/shard_map/all_to_all | solution.py:48
  124.7 1.9 shard_map.106
  126.6 3.5 %collective-permute-start.22 = (bf16[128,4096]{1,0:T(8,128)(2,1)S(1)}, bf16[128,4096]{1,0:T(8,128)(2,1)S(1)}, u32[]{:S(2)}, u32[]{:S(2)}) collective-permute-start(bf16[128,4096]{1,0:T(8,128)(2,1)S(1)} %get-tuple-element.47), channel_id=1, source_target_pairs={{0,192},{1,193},{2,194},{3,195},{4,196},{5,197},{6,198},{7,199},{8... | collective-permute-start | bytes 3145736 | tf_op jit(solution)/shard_map/ppermute | solution.py:44
  131.4 2.8 %collective-permute-done.28.right = bf16[96,4096]{1,0:T(8,128)(2,1)} collective-permute-done((bf16[96,4096]{1,0:T(8,128)(2,1)}, bf16[96,4096]{1,0:T(8,128)(2,1)}, u32[]{:S(2)}, u32[]{:S(2)}) %collective-permute-start.28) | collective-permute-done | bytes 786464 | tf_op jit(solution)/shard_map/ppermute | solution.py:44
  134.2 2.2 %collective-permute-start.30 = (bf16[96,4096]{1,0:T(8,128)(2,1)S(1)}, bf16[96,4096]{1,0:T(8,128)(2,1)S(1)}, u32[]{:S(2)}, u32[]{:S(2)}) collective-permute-start(bf16[96,4096]{1,0:T(8,128)(2,1)S(1)} %copy-done.10), channel_id=1, source_target_pairs={{0,16},{1,17},{2,18},{3,19},{4,20},{5,21},{6,22},{7,23},{8,24},{9,... | collective-permute-start | bytes 2359304 | tf_op jit(solution)/shard_map/ppermute | solution.py:44
  136.4 15.4 %collective-permute-done.29.left = bf16[96,4096]{1,0:T(8,128)(2,1)S(1)} collective-permute-done((bf16[96,4096]{1,0:T(8,128)(2,1)S(1)}, bf16[96,4096]{1,0:T(8,128)(2,1)S(1)}, u32[]{:S(2)}, u32[]{:S(2)}) %collective-permute-start.29) | collective-permute-done | bytes 786464 | tf_op jit(solution)/shard_map/ppermute | solution.py:44
  151.7 5.1 %collective-permute-start.20 = (bf16[128,896]{1,0:T(8,128)(2,1)}, bf16[128,896]{1,0:T(8,128)(2,1)S(1)}, u32[]{:S(2)}, u32[]{:S(2)}) collective-permute-start(bf16[128,896]{1,0:T(8,128)(2,1)} %copy-done.13), channel_id=1, source_target_pairs={{0,32},{1,33},{2,34},{3,35},{4,36},{5,37},{6,38},{7,39},{8,40},{9,... | collective-permute-start | bytes 688136 | tf_op jit(solution)/shard_map/ppermute | solution.py:44
  156.8 9.4 %collective-permute-done.30.far = bf16[96,4096]{1,0:T(8,128)(2,1)S(1)} collective-permute-done((bf16[96,4096]{1,0:T(8,128)(2,1)S(1)}, bf16[96,4096]{1,0:T(8,128)(2,1)S(1)}, u32[]{:S(2)}, u32[]{:S(2)}) %collective-permute-start.30) | collective-permute-done | bytes 786464 | tf_op jit(solution)/shard_map/ppermute | solution.py:44
  169.2 4.9 %collective-permute-done.22.right = bf16[128,4096]{1,0:T(8,128)(2,1)S(1)} collective-permute-done((bf16[128,4096]{1,0:T(8,128)(2,1)S(1)}, bf16[128,4096]{1,0:T(8,128)(2,1)S(1)}, u32[]{:S(2)}, u32[]{:S(2)}) %collective-permute-start.22) | collective-permute-done | bytes 1048608 | tf_op jit(solution)/shard_map/ppermute | solution.py:44
  174.1 2.4 %collective-permute-done.24.far = bf16[128,4096]{1,0:T(8,128)(2,1)S(1)} collective-permute-done((bf16[128,4096]{1,0:T(8,128)(2,1)S(1)}, bf16[128,4096]{1,0:T(8,128)(2,1)S(1)}, u32[]{:S(2)}, u32[]{:S(2)}) %collective-permute-start.24) | collective-permute-done | bytes 1048608 | tf_op jit(solution)/shard_map/ppermute | solution.py:44
  181.3 2.0 %shard_map.102 = bf16[128,896]{1,0:T(8,128)(2,1)} custom-call(bf16[128,896]{1,0:T(8,128)(2,1)S(1)} %copy-done.6, bf16[128,896]{1,0:T(8,128)(2,1)S(1)} %collective-permute-done.20.partner), custom_call_target="tpu_custom_call" | custom-call | tf_op jit(solution)/shard_map/pallas_call | solution.py:350
  183.3 5.6 %collective-permute-done.32.refs_6_ = bf16[24,4096]{1,0:T(8,128)(2,1)S(1)} collective-permute-done((bf16[24,4096]{1,0:T(8,128)(2,1)S(1)}, bf16[24,4096]{1,0:T(8,128)(2,1)S(1)}, u32[]{:S(2)}, u32[]{:S(2)}) %collective-permute-start.32) | collective-permute-done | bytes 196640 | tf_op jit(solution)/shard_map/ppermute | solution.py:44
  (86 shorter events, 37.9 us)
Async XLA Ops:
  2.9 38.2 %all-to-all-start = ((bf16[8,128,512]{2,1,0:T(8,128)(2,1)}), bf16[8,128,512]{2,1,0:T(8,128)(2,1)S(1)}, u32[]{:S(2)}, u32[]{:S(2)}) async-start(bf16[8,128,512]{2,1,0:T(8,128)(2,1)} %get-tuple-element.34), calls=%async_computation | async-start | bytes 2097152 | tf_op jit(solution)/shard_map/all_to_all | solution.py:48
  14.5 27.1 %collective-permute-start.3 = (bf16[24,4096]{1,0:T(8,128)(2,1)S(1)}, bf16[24,4096]{1,0:T(8,128)(2,1)S(1)}, u32[]{:S(2)}, u32[]{:S(2)}) collective-permute-start(bf16[24,4096]{1,0:T(8,128)(2,1)S(1)} %get-tuple-element.36.first), channel_id=1, source_target_pairs={{0,192},{1,193},{2,194},{3,195},{4,196},{5,197},{6,198},{7,199},{8... | collective-permute-start | bytes 589832 | tf_op jit(solution)/shard_map/ppermute | solution.py:44
  15.9 30.7 %collective-permute-start.12 = (bf16[32,4096]{1,0:T(8,128)(2,1)S(1)}, bf16[32,4096]{1,0:T(8,128)(2,1)S(1)}, u32[]{:S(2)}, u32[]{:S(2)}) collective-permute-start(bf16[32,4096]{1,0:T(8,128)(2,1)S(1)} %get-tuple-element.37.first), channel_id=1, source_target_pairs={{0,24},{1,25},{2,26},{3,27},{4,28},{5,29},{6,30},{7,31},{8,0},{9,1... | collective-permute-start | bytes 786440 | tf_op jit(solution)/shard_map/ppermute | solution.py:44
  17.4 27.9 %collective-permute-start.4 = (bf16[24,4096]{1,0:T(8,128)(2,1)S(1)}, bf16[24,4096]{1,0:T(8,128)(2,1)}, u32[]{:S(2)}, u32[]{:S(2)}) collective-permute-start(bf16[24,4096]{1,0:T(8,128)(2,1)S(1)} %get-tuple-element.36.first), channel_id=1, source_target_pairs={{0,128},{1,129},{2,130},{3,131},{4,132},{5,133},{6,134},{7,135},{8... | collective-permute-start | bytes 589832 | tf_op jit(solution)/shard_map/ppermute | solution.py:44
  20.1 44.0 %collective-permute-start.14 = (bf16[64,4096]{1,0:T(8,128)(2,1)S(1)}, bf16[64,4096]{1,0:T(8,128)(2,1)S(1)}, u32[]{:S(2)}, u32[]{:S(2)}) collective-permute-start(bf16[64,4096]{1,0:T(8,128)(2,1)S(1)} %shard_map.98.refs_0_), channel_id=1, source_target_pairs={{0,64},{1,65},{2,66},{3,67},{4,68},{5,69},{6,70},{7,71},{8,72},{9,... | collective-permute-start | bytes 1572872 | tf_op jit(solution)/shard_map/ppermute | solution.py:44
  41.1 43.2 %collective-permute-start = (bf16[8,128,512]{2,1,0:T(8,128)(2,1)S(1)}, bf16[8,128,512]{2,1,0:T(8,128)(2,1)S(1)}, u32[]{:S(2)}, u32[]{:S(2)}) collective-permute-start(bf16[8,128,512]{2,1,0:T(8,128)(2,1)S(1)} %all-to-all-done.own), channel_id=1, source_target_pairs={{0,1},{1,0},{2,3},{3,2},{4,5},{5,4},{6,7},{7,6},{8,9},{9,8},{10,11... | collective-permute-start | bytes 3145736 | tf_op jit(solution)/shard_map/ppermute | solution.py:44
  41.6 9.3 %collective-permute-start.13 = (bf16[32,4096]{1,0:T(8,128)(2,1)S(1)}, bf16[32,4096]{1,0:T(8,128)(2,1)S(1)}, u32[]{:S(2)}, u32[]{:S(2)}) collective-permute-start(bf16[32,4096]{1,0:T(8,128)(2,1)S(1)} %get-tuple-element.37.first), channel_id=1, source_target_pairs={{0,16},{1,17},{2,18},{3,19},{4,20},{5,21},{6,22},{7,23},{8,24},{9,... | collective-permute-start | bytes 786440 | tf_op jit(solution)/shard_map/ppermute | solution.py:44
  45.3 16.2 %collective-permute-start.5 = (bf16[48,4096]{1,0:T(8,128)(2,1)S(1)}, bf16[48,4096]{1,0:T(8,128)(2,1)S(1)}, u32[]{:S(2)}, u32[]{:S(2)}) collective-permute-start(bf16[48,4096]{1,0:T(8,128)(2,1)S(1)} %shard_map.96.refs_0_.refs_8_), channel_id=1, source_target_pairs={{0,8},{1,9},{2,10},{3,11},{4,12},{5,13},{6,14},{7,15},{8,16},{9,17... | collective-permute-start | bytes 1179656 | tf_op jit(solution)/shard_map/ppermute | solution.py:44
  46.6 14.8 %collective-permute-start.8 = (bf16[48,4096]{1,0:T(8,128)(2,1)S(1)}, bf16[48,4096]{1,0:T(8,128)(2,1)S(1)}, u32[]{:S(2)}, u32[]{:S(2)}) collective-permute-start(bf16[48,4096]{1,0:T(8,128)(2,1)S(1)} %shard_map.97.refs_1_.refs_9_), channel_id=1, source_target_pairs={{0,24},{1,25},{2,26},{3,27},{4,28},{5,29},{6,30},{7,31},{8,0},{9,1... | collective-permute-start | bytes 1179656 | tf_op jit(solution)/shard_map/ppermute | solution.py:44
  58.7 9.9 %collective-permute-start.17 = (bf16[64,4096]{1,0:T(8,128)(2,1)S(1)}, bf16[64,4096]{1,0:T(8,128)(2,1)S(1)}, u32[]{:S(2)}, u32[]{:S(2)}) collective-permute-start(bf16[64,4096]{1,0:T(8,128)(2,1)S(1)} %shard_map.99.refs_1_), channel_id=1, source_target_pairs={{0,192},{1,193},{2,194},{3,195},{4,196},{5,197},{6,198},{7,199},{8... | collective-permute-start | bytes 1572872 | tf_op jit(solution)/shard_map/ppermute | solution.py:44
  61.4 10.6 %collective-permute-start.15 = (bf16[64,4096]{1,0:T(8,128)(2,1)S(1)}, bf16[64,4096]{1,0:T(8,128)(2,1)S(1)}, u32[]{:S(2)}, u32[]{:S(2)}) collective-permute-start(bf16[64,4096]{1,0:T(8,128)(2,1)S(1)} %shard_map.99.refs_1_), channel_id=1, source_target_pairs={{0,64},{1,65},{2,66},{3,67},{4,68},{5,69},{6,70},{7,71},{8,72},{9,... | collective-permute-start | bytes 1572872 | tf_op jit(solution)/shard_map/ppermute | solution.py:44
  61.5 18.4 %collective-permute-start.16 = (bf16[64,4096]{1,0:T(8,128)(2,1)S(1)}, bf16[64,4096]{1,0:T(8,128)(2,1)S(1)}, u32[]{:S(2)}, u32[]{:S(2)}) collective-permute-start(bf16[64,4096]{1,0:T(8,128)(2,1)S(1)} %shard_map.98.refs_0_), channel_id=1, source_target_pairs={{0,192},{1,193},{2,194},{3,195},{4,196},{5,197},{6,198},{7,199},{8... | collective-permute-start | bytes 1572872 | tf_op jit(solution)/shard_map/ppermute | solution.py:44
  64.1 18.9 %collective-permute-start.18 = (bf16[64,4096]{1,0:T(8,128)(2,1)S(1)}, bf16[64,4096]{1,0:T(8,128)(2,1)S(1)}, u32[]{:S(2)}, u32[]{:S(2)}) collective-permute-start(bf16[64,4096]{1,0:T(8,128)(2,1)S(1)} %collective-permute-done.14.refs_2_), channel_id=1, source_target_pairs={{0,64},{1,65},{2,66},{3,67},{4,68},{5,69},{6,70},{7,71},{8,72},{9,... | collective-permute-start | bytes 1572872 | tf_op jit(solution)/shard_map/ppermute | solution.py:44
  68.7 22.5 %collective-permute-start.19 = (bf16[64,4096]{1,0:T(8,128)(2,1)S(1)}, bf16[64,4096]{1,0:T(8,128)(2,1)S(1)}, u32[]{:S(2)}, u32[]{:S(2)}) collective-permute-start(bf16[64,4096]{1,0:T(8,128)(2,1)S(1)} %collective-permute-done.17.refs_5_), channel_id=1, source_target_pairs={{0,192},{1,193},{2,194},{3,195},{4,196},{5,197},{6,198},{7,199},{8... | collective-permute-start | bytes 1572872 | tf_op jit(solution)/shard_map/ppermute | solution.py:44
  72.1 21.5 %collective-permute-start.6 = (bf16[48,4096]{1,0:T(8,128)(2,1)S(1)}, bf16[48,4096]{1,0:T(8,128)(2,1)S(1)}, u32[]{:S(2)}, u32[]{:S(2)}) collective-permute-start(bf16[48,4096]{1,0:T(8,128)(2,1)S(1)} %shard_map.97.refs_1_.refs_9_), channel_id=1, source_target_pairs={{0,8},{1,9},{2,10},{3,11},{4,12},{5,13},{6,14},{7,15},{8,16},{9,17... | collective-permute-start | bytes 1179656 | tf_op jit(solution)/shard_map/ppermute | solution.py:44
  79.9 13.7 %collective-permute-start.7 = (bf16[48,4096]{1,0:T(8,128)(2,1)S(1)}, bf16[48,4096]{1,0:T(8,128)(2,1)S(1)}, u32[]{:S(2)}, u32[]{:S(2)}) collective-permute-start(bf16[48,4096]{1,0:T(8,128)(2,1)S(1)} %shard_map.96.refs_0_.refs_8_), channel_id=1, source_target_pairs={{0,24},{1,25},{2,26},{3,27},{4,28},{5,29},{6,30},{7,31},{8,0},{9,1... | collective-permute-start | bytes 1179656 | tf_op jit(solution)/shard_map/ppermute | solution.py:44
  83.0 11.3 %collective-permute-start.9 = (bf16[48,4096]{1,0:T(8,128)(2,1)S(1)}, bf16[48,4096]{1,0:T(8,128)(2,1)S(1)}, u32[]{:S(2)}, u32[]{:S(2)}) collective-permute-start(bf16[48,4096]{1,0:T(8,128)(2,1)S(1)} %collective-permute-done.5.refs_2_.refs_10_), channel_id=1, source_target_pairs={{0,8},{1,9},{2,10},{3,11},{4,12},{5,13},{6,14},{7,15},{8,16},{9,17... | collective-permute-start | bytes 1179656 | tf_op jit(solution)/shard_map/ppermute | solution.py:44
  84.3 10.0 %collective-permute-start.10 = (bf16[48,4096]{1,0:T(8,128)(2,1)S(1)}, bf16[48,4096]{1,0:T(8,128)(2,1)S(1)}, u32[]{:S(2)}, u32[]{:S(2)}) collective-permute-start(bf16[48,4096]{1,0:T(8,128)(2,1)S(1)} %collective-permute-done.8.refs_5_.refs_13_), channel_id=1, source_target_pairs={{0,24},{1,25},{2,26},{3,27},{4,28},{5,29},{6,30},{7,31},{8,0},{9,1... | collective-permute-start | bytes 1179656 | tf_op jit(solution)/shard_map/ppermute | solution.py:44
  101.0 15.9 %collective-permute-start.21 = (bf16[2,4,128,512]{3,2,1,0:T(8,128)(2,1)S(1)}, bf16[2,4,128,512]{3,2,1,0:T(8,128)(2,1)S(1)}, u32[]{:S(2)}, u32[]{:S(2)}) collective-permute-start(bf16[2,4,128,512]{3,2,1,0:T(8,128)(2,1)S(1)} %get-tuple-element.45), channel_id=1, source_target_pairs={{0,1},{1,0},{2,3},{3,2},{4,5},{5,4},{6,7},{7,6},{8,9},{9,8},{10,11... | collective-permute-start | bytes 3145736 | tf_op jit(solution)/shard_map/ppermute | solution.py:44
  113.6 20.6 %collective-permute-start.28 = (bf16[96,4096]{1,0:T(8,128)(2,1)}, bf16[96,4096]{1,0:T(8,128)(2,1)}, u32[]{:S(2)}, u32[]{:S(2)}) collective-permute-start(bf16[96,4096]{1,0:T(8,128)(2,1)} %get-tuple-element.55), channel_id=1, source_target_pairs={{0,24},{1,25},{2,26},{3,27},{4,28},{5,29},{6,30},{7,31},{8,0},{9,1... | collective-permute-start | bytes 2359304 | tf_op jit(solution)/shard_map/ppermute | solution.py:44
  118.2 73.3 %all-to-all-start.1 = ((bf16[8,128,512]{2,1,0:T(8,128)(2,1)}), bf16[8,128,512]{2,1,0:T(8,128)(2,1)S(1)}, u32[]{:S(2)}, u32[]{:S(2)}) async-start(bf16[8,128,512]{2,1,0:T(8,128)(2,1)} %shard_map.104), calls=%async_computation.1 | async-start | bytes 2097152 | tf_op jit(solution)/shard_map/all_to_all | solution.py:48
  126.6 47.5 %collective-permute-start.22 = (bf16[128,4096]{1,0:T(8,128)(2,1)S(1)}, bf16[128,4096]{1,0:T(8,128)(2,1)S(1)}, u32[]{:S(2)}, u32[]{:S(2)}) collective-permute-start(bf16[128,4096]{1,0:T(8,128)(2,1)S(1)} %get-tuple-element.47), channel_id=1, source_target_pairs={{0,192},{1,193},{2,194},{3,195},{4,196},{5,197},{6,198},{7,199},{8... | collective-permute-start | bytes 3145736 | tf_op jit(solution)/shard_map/ppermute | solution.py:44
  130.1 44.0 %collective-permute-start.23 = (bf16[128,4096]{1,0:T(8,128)(2,1)S(1)}, bf16[128,4096]{1,0:T(8,128)(2,1)S(1)}, u32[]{:S(2)}, u32[]{:S(2)}) collective-permute-start(bf16[128,4096]{1,0:T(8,128)(2,1)S(1)} %get-tuple-element.48), channel_id=1, source_target_pairs={{0,64},{1,65},{2,66},{3,67},{4,68},{5,69},{6,70},{7,71},{8,72},{9,... | collective-permute-start | bytes 3145736 | tf_op jit(solution)/shard_map/ppermute | solution.py:44
  130.1 46.5 %collective-permute-start.24 = (bf16[128,4096]{1,0:T(8,128)(2,1)S(1)}, bf16[128,4096]{1,0:T(8,128)(2,1)S(1)}, u32[]{:S(2)}, u32[]{:S(2)}) collective-permute-start(bf16[128,4096]{1,0:T(8,128)(2,1)S(1)} %get-tuple-element.49), channel_id=1, source_target_pairs={{0,128},{1,129},{2,130},{3,131},{4,132},{5,133},{6,134},{7,135},{8... | collective-permute-start | bytes 3145736 | tf_op jit(solution)/shard_map/ppermute | solution.py:44
  131.4 20.4 %collective-permute-start.29 = (bf16[96,4096]{1,0:T(8,128)(2,1)S(1)}, bf16[96,4096]{1,0:T(8,128)(2,1)S(1)}, u32[]{:S(2)}, u32[]{:S(2)}) collective-permute-start(bf16[96,4096]{1,0:T(8,128)(2,1)S(1)} %copy-done.12), channel_id=1, source_target_pairs={{0,8},{1,9},{2,10},{3,11},{4,12},{5,13},{6,14},{7,15},{8,16},{9,17... | collective-permute-start | bytes 2359304 | tf_op jit(solution)/shard_map/ppermute | solution.py:44
  134.2 32.1 %collective-permute-start.30 = (bf16[96,4096]{1,0:T(8,128)(2,1)S(1)}, bf16[96,4096]{1,0:T(8,128)(2,1)S(1)}, u32[]{:S(2)}, u32[]{:S(2)}) collective-permute-start(bf16[96,4096]{1,0:T(8,128)(2,1)S(1)} %copy-done.10), channel_id=1, source_target_pairs={{0,16},{1,17},{2,18},{3,19},{4,20},{5,21},{6,22},{7,23},{8,24},{9,... | collective-permute-start | bytes 2359304 | tf_op jit(solution)/shard_map/ppermute | solution.py:44
  151.7 28.0 %collective-permute-start.20 = (bf16[128,896]{1,0:T(8,128)(2,1)}, bf16[128,896]{1,0:T(8,128)(2,1)S(1)}, u32[]{:S(2)}, u32[]{:S(2)}) collective-permute-start(bf16[128,896]{1,0:T(8,128)(2,1)} %copy-done.13), channel_id=1, source_target_pairs={{0,32},{1,33},{2,34},{3,35},{4,36},{5,37},{6,38},{7,39},{8,40},{9,... | collective-permute-start | bytes 688136 | tf_op jit(solution)/shard_map/ppermute | solution.py:44
  167.8 12.0 %collective-permute-start.31 = (bf16[24,4096]{1,0:T(8,128)(2,1)S(1)}, bf16[24,4096]{1,0:T(8,128)(2,1)S(1)}, u32[]{:S(2)}, u32[]{:S(2)}) collective-permute-start(bf16[24,4096]{1,0:T(8,128)(2,1)S(1)} %get-tuple-element.59), channel_id=1, source_target_pairs={{0,192},{1,193},{2,194},{3,195},{4,196},{5,197},{6,198},{7,199},{8... | collective-permute-start | bytes 589832 | tf_op jit(solution)/shard_map/ppermute | solution.py:44
  177.1 11.8 %collective-permute-start.25 = (bf16[32,4096]{1,0:T(8,128)(2,1)S(1)}, bf16[32,4096]{1,0:T(8,128)(2,1)S(1)}, u32[]{:S(2)}, u32[]{:S(2)}) collective-permute-start(bf16[32,4096]{1,0:T(8,128)(2,1)S(1)} %get-tuple-element.51), channel_id=1, source_target_pairs={{0,24},{1,25},{2,26},{3,27},{4,28},{5,29},{6,30},{7,31},{8,0},{9,1... | collective-permute-start | bytes 786440 | tf_op jit(solution)/shard_map/ppermute | solution.py:44
  178.5 10.3 %collective-permute-start.26 = (bf16[32,4096]{1,0:T(8,128)(2,1)S(1)}, bf16[32,4096]{1,0:T(8,128)(2,1)S(1)}, u32[]{:S(2)}, u32[]{:S(2)}) collective-permute-start(bf16[32,4096]{1,0:T(8,128)(2,1)S(1)} %get-tuple-element.52), channel_id=1, source_target_pairs={{0,8},{1,9},{2,10},{3,11},{4,12},{5,13},{6,14},{7,15},{8,16},{9,17... | collective-permute-start | bytes 786440 | tf_op jit(solution)/shard_map/ppermute | solution.py:44
  178.6 11.8 %collective-permute-start.27 = (bf16[32,4096]{1,0:T(8,128)(2,1)S(1)}, bf16[32,4096]{1,0:T(8,128)(2,1)S(1)}, u32[]{:S(2)}, u32[]{:S(2)}) collective-permute-start(bf16[32,4096]{1,0:T(8,128)(2,1)S(1)} %get-tuple-element.53), channel_id=1, source_target_pairs={{0,16},{1,17},{2,18},{3,19},{4,20},{5,21},{6,22},{7,23},{8,24},{9,... | collective-permute-start | bytes 786440 | tf_op jit(solution)/shard_map/ppermute | solution.py:44
  179.8 9.1 %collective-permute-start.32 = (bf16[24,4096]{1,0:T(8,128)(2,1)S(1)}, bf16[24,4096]{1,0:T(8,128)(2,1)S(1)}, u32[]{:S(2)}, u32[]{:S(2)}) collective-permute-start(bf16[24,4096]{1,0:T(8,128)(2,1)S(1)} %get-tuple-element.60), channel_id=1, source_target_pairs={{0,64},{1,65},{2,66},{3,67},{4,68},{5,69},{6,70},{7,71},{8,72},{9,... | collective-permute-start | bytes 589832 | tf_op jit(solution)/shard_map/ppermute | solution.py:44
  (18 other events, 224.3 us)

commit v4 on v3

--- a/solution.py
+++ b/solution.py
@@ -248,13 +248,6 @@
             out[first + zl] = (own[s].astype(F32) + other[s].astype(F32)).astype(BF16)
 
 
-def total_kernel(parts, out):
-    total = parts[0].astype(F32)
-    for n in range(1, NZ):
-        total = total + parts[n].astype(F32)
-    out[...] = total.astype(BF16)
-
-
 def stage_kernel(own, right, left, far, *outs):
     rows = own.shape[0] // 4
     for n, out in enumerate(outs):
@@ -264,8 +257,27 @@
         out[...] = total.astype(BF16)
 
 
+def relay_kernel(left, right, from_right, from_left, left_out, right_out):
+    left_out[...] = (left[...].astype(F32) + from_right[...].astype(F32)).astype(BF16)
+    right_out[...] = (right[...].astype(F32) + from_left[...].astype(F32)).astype(BF16)
+
+
+def halves_kernel(own_lo, own_hi, r_lo, r_hi, l_lo, l_hi, *outs):
+    rows = own_lo.shape[0] // 2
+    lo = own_lo[...].astype(F32) + r_lo[...].astype(F32) + l_lo[...].astype(F32)
+    hi = own_hi[...].astype(F32) + r_hi[...].astype(F32) + l_hi[...].astype(F32)
+    outs[0][...] = lo[:rows].astype(BF16)
+    outs[1][...] = lo[rows:].astype(BF16)
+    outs[2][...] = hi[:rows].astype(BF16)
+    outs[3][...] = hi[rows:].astype(BF16)
+
+
 def finish_kernel(*refs):
-    a, b, gate, up = refs[:4], refs[4:8], refs[8], refs[9]
+    a, b, parts, gate, up, token_grad = refs[:4], refs[4:8], *refs[8:]
+    total = parts[0].astype(F32)
+    for n in range(1, NZ):
+        total = total + parts[n].astype(F32)
+    token_grad[...] = total.astype(BF16)
     ta = sum(r[...].astype(F32) for r in a) * (1.0 / GROUPS)
     tb = sum(r[...].astype(F32) for r in b) * (1.0 / GROUPS)
     gate[...] = jnp.concatenate([ta[:HALF_A], tb[:HALF_B]], axis=0)
@@ -286,11 +298,33 @@
     return [lo, hi, left_lo, left_hi, right_lo, right_hi, far_lo, far_hi]
 
 
-def reduce_plane(parts, first, second):
+def spread_rows(pieces, first):
+    return [pieces[0]] + [shift(p, **{first: r}) for p, r in zip(pieces[1:], REL[1:])]
+
+
+def reduce_direct(parts, first, second):
     arrived = [parts[0]] + [shift(p, **{second: r}) for p, r in zip(parts[1:], REL[1:])]
     rows = parts[0].shape[0] // 4
     pieces = call(stage_kernel, tuple(shape(rows, D) for _ in REL))(*arrived)
-    return [pieces[0]] + [shift(p, **{first: r}) for p, r in zip(pieces[1:], REL[1:])]
+    return spread_rows(pieces, first)
+
+
+def reduce_ring(parts, first, second):
+    own_lo, own_hi, left_lo, left_hi, right_lo, right_hi, far_lo, far_hi = parts
+    n = far_lo.shape[0]
+    from_right = shift(far_lo, **{second: -1})
+    from_left = shift(far_hi, **{second: 1})
+    r_hi = shift(left_hi, **{second: -1})
+    l_lo = shift(right_lo, **{second: 1})
+    left_lo, right_hi = call(relay_kernel, (shape(n, D), shape(n, D)))(
+        left_lo, right_hi, from_right, from_left
+    )
+    r_lo = shift(left_lo, **{second: -1})
+    l_hi = shift(right_hi, **{second: 1})
+    pieces = call(halves_kernel, tuple(shape(n // 2, D) for _ in REL))(
+        own_lo, own_hi, r_lo, r_hi, l_lo, l_hi
+    )
+    return spread_rows(pieces, first)
 
 
 def body(tokens, gate_codes, gate_scales, up_codes, up_scales, cotangent):
@@ -326,17 +360,14 @@
             scratch_shapes=[pltpu.VMEM((2 * TOK, width), F32)],
         )(whole, cot, *w, *before)
 
-    def weight_grad(dd):
-        outs = tuple(shape(dd.shape[1] // 4, D) for _ in REL)
+    def weight_grad(dd, count):
+        outs = (shape(dd.shape[1] // count, D),) * count
         return call(weight_grad_kernel, outs)(dd, whole)
 
     hm_a, hp_a, dd_a = forward(wa, HALF_A, 0)
     hidden_mine, hidden_sent, dd_b = forward(wb, HALF_B, WIDE_A, hm_a, hp_a)
-    sums_a = reduce_plane(weight_grad(dd_a), "dx", "dy")
-    sums_b = reduce_plane(weight_grad(dd_b), "dy", "dx")
-    gate_grad, up_grad = call(
-        finish_kernel, (shape(ROWS, D, F32), shape(ROWS, D, F32))
-    )(*sums_a, *sums_b)
+    sums_a = reduce_ring(weight_grad(dd_a, 8), "dx", "dy")
+    sums_b = reduce_direct(weight_grad(dd_b, 4), "dy", "dx")
 
     quad = jax.ShapeDtypeStruct((2, NZL, TOK, SLICE), BF16)
     own_tg, other_tg = call(token_grad_kernel, (quad, quad), 20)(
@@ -345,7 +376,9 @@
     cube = (NZ, TOK, SLICE)
     received = shift(other_tg, dc=1)
     blocks = call(pair_sum_kernel, cube_shape, 8)(own_tg.reshape(cube), received.reshape(cube))
-    token_grad = call(total_kernel, shape(TOK, SLICE))(exchange_z(blocks))
+    gate_grad, up_grad, token_grad = call(
+        finish_kernel, (shape(ROWS, D, F32), shape(ROWS, D, F32), shape(TOK, SLICE))
+    )(*sums_a, *sums_b, exchange_z(blocks))
 
     hidden = call(
         collect_kernel,

time: 194 us -> 192 us (0.990)
  starting transfers between devices: 74 us -> 80.4 us
  waiting for transfers between devices: 87.2 us -> 84 us
  Pallas kernels: 24 us -> 21.5 us
    ppermute x34 -> x37, starting transfers between devices: 58.5 us -> 65.3 us  [shift(): return lax.ppermute(value, AXES, pairs)]
    ppermute x34 -> x37, waiting for transfers between devices: 68.3 us -> 64.4 us  [shift(): return lax.ppermute(value, AXES, pairs)]
    unnamed x28 -> x24, local copies, waits for them, and re-layouts: 6.25 us -> 5.1 us
  transfers between devices with their start and end apart: 36 -> 39, of which waited for: 16 -> 14; matrix products, arithmetic and copies ran while one was open for 0% -> 0% of each run, Pallas kernels for 8% -> 6%
where the time goes in v4:
time: 192 us
  waiting for transfers between devices  84 us (44%)
  starting transfers between devices  80.4 us (42%)
  Pallas kernels  21.5 us (11%)
  local copies, waits for them, and re-layouts  5.1 us (3%)
    ppermute x37, starting transfers between devices, shift(): return lax.ppermute(value, AXES, pairs)  65.3 us
    ppermute x37, waiting for transfers between devices, shift(): return lax.ppermute(value, AXES, pairs)  64.4 us
    all_to_all x2, waiting for transfers between devices, exchange_z(): return lax.all_to_all(value, ('zh', 'zl'), 0, 0, tiled=True)  19.6 us
    all_to_all x2, starting transfers between devices, exchange_z(): return lax.all_to_all(value, ('zh', 'zl'), 0, 0, tiled=True)  15.2 us
    unnamed x24, local copies, waits for them, and re-layouts  5.1 us
    pallas_call x2, Pallas kernels, forward(): call(functools.partial(forward_kernel, shard, half, lower), (shape(TOK, t...  4.6 us
  transfers between devices with their start and end apart: 39, of which 14 were waited for; matrix products, arithmetic and copies ran while one was open for 0% of the time, Pallas kernels for 6%

profile of v4, /device:TPU:1, one launch (start us, length us, event | category | flops | bytes accessed | tf_op | source)
XLA Modules:
  0.0 191.9 jit_solution(3836240281729955867)
XLA Ops:
  0.6 2.3 %shard_map.93 = (bf16[32,4096]{1,0:T(8,128)(2,1)S(1)}, bf16[24,4096]{1,0:T(8,128)(2,1)S(1)}, bf16[8,128,512]{2,1,0:T(8,128)(2,1)}, bf16[128,448]{1,0:T(8,128)(2,1)S(1)}) custom-call(bf16[128,512]{1,0:T(8,128)(2,1)} %tokens.1, bf16[128,896]{1,0:T(8,128)(2,1)} %mine.1, bf16[28,4096]{1,0:T(8,128)(2,1)} %refs_0_.1, f32[16,28]{1,0:T(8,128)} %bitcast.6, ...), custom_call_target="tpu_custom_call" | custom-call | tf_op jit(solution)/shard_map/pallas_call | solution.py:335
  3.6 9.0 %all-to-all-start = ((bf16[8,128,512]{2,1,0:T(8,128)(2,1)}), bf16[8,128,512]{2,1,0:T(8,128)(2,1)S(1)}, u32[]{:S(2)}, u32[]{:S(2)}) async-start(bf16[8,128,512]{2,1,0:T(8,128)(2,1)} %get-tuple-element.41), calls=%async_computation | async-start | bytes 2097152 | tf_op jit(solution)/shard_map/all_to_all | solution.py:48
  13.9 2.9 %collective-permute-start.4 = (bf16[24,4096]{1,0:T(8,128)(2,1)S(1)}, bf16[24,4096]{1,0:T(8,128)(2,1)S(1)}, u32[]{:S(2)}, u32[]{:S(2)}) collective-permute-start(bf16[24,4096]{1,0:T(8,128)(2,1)S(1)} %get-tuple-element.43.first), channel_id=1, source_target_pairs={{0,128},{1,129},{2,130},{3,131},{4,132},{5,133},{6,134},{7,135},{8... | collective-permute-start | bytes 589832 | tf_op jit(solution)/shard_map/ppermute | solution.py:44
  17.2 2.5 %collective-permute-start.13 = (bf16[32,4096]{1,0:T(8,128)(2,1)S(1)}, bf16[32,4096]{1,0:T(8,128)(2,1)S(1)}, u32[]{:S(2)}, u32[]{:S(2)}) collective-permute-start(bf16[32,4096]{1,0:T(8,128)(2,1)S(1)} %get-tuple-element.44.first), channel_id=1, source_target_pairs={{0,16},{1,17},{2,18},{3,19},{4,20},{5,21},{6,22},{7,23},{8,24},{9,... | collective-permute-start | bytes 786440 | tf_op jit(solution)/shard_map/ppermute | solution.py:44
  19.6 2.3 %collective-permute-start.3 = (bf16[24,4096]{1,0:T(8,128)(2,1)S(1)}, bf16[24,4096]{1,0:T(8,128)(2,1)}, u32[]{:S(2)}, u32[]{:S(2)}) collective-permute-start(bf16[24,4096]{1,0:T(8,128)(2,1)S(1)} %get-tuple-element.43.first), channel_id=1, source_target_pairs={{0,192},{1,193},{2,194},{3,195},{4,196},{5,197},{6,198},{7,199},{8... | collective-permute-start | bytes 589832 | tf_op jit(solution)/shard_map/ppermute | solution.py:44
  22.2 19.6 %all-to-all-done.own = bf16[8,128,512]{2,1,0:T(8,128)(2,1)S(1)} async-done(((bf16[8,128,512]{2,1,0:T(8,128)(2,1)}), bf16[8,128,512]{2,1,0:T(8,128)(2,1)S(1)}, u32[]{:S(2)}, u32[]{:S(2)}) %all-to-all-start) | async-done | bytes 1048608 | tf_op jit(solution)/shard_map/all_to_all | solution.py:48
  42.9 2.5 %collective-permute-start.12 = (bf16[32,4096]{1,0:T(8,128)(2,1)S(1)}, bf16[32,4096]{1,0:T(8,128)(2,1)S(1)}, u32[]{:S(2)}, u32[]{:S(2)}) collective-permute-start(bf16[32,4096]{1,0:T(8,128)(2,1)S(1)} %get-tuple-element.44.first), channel_id=1, source_target_pairs={{0,24},{1,25},{2,26},{3,27},{4,28},{5,29},{6,30},{7,31},{8,0},{9,1... | collective-permute-start | bytes 786440 | tf_op jit(solution)/shard_map/ppermute | solution.py:44
  47.4 2.7 %collective-permute-start.8 = (bf16[48,4096]{1,0:T(8,128)(2,1)S(1)}, bf16[48,4096]{1,0:T(8,128)(2,1)S(1)}, u32[]{:S(2)}, u32[]{:S(2)}) collective-permute-start(bf16[48,4096]{1,0:T(8,128)(2,1)S(1)} %shard_map.97.refs_1_.refs_9_), channel_id=1, source_target_pairs={{0,24},{1,25},{2,26},{3,27},{4,28},{5,29},{6,30},{7,31},{8,0},{9,1... | collective-permute-start | bytes 1179656 | tf_op jit(solution)/shard_map/ppermute | solution.py:44
  51.3 7.7 %collective-permute-done.1.partner = bf16[128,448]{1,0:T(8,128)(2,1)S(1)} collective-permute-done((bf16[128,448]{1,0:T(8,128)(2,1)}, bf16[128,448]{1,0:T(8,128)(2,1)S(1)}, u32[]{:S(2)}, u32[]{:S(2)}) %collective-permute-start.1) | collective-permute-done | bytes 114720 | tf_op jit(solution)/shard_map/ppermute | solution.py:44
  59.1 2.7 %collective-permute-start.17 = (bf16[64,4096]{1,0:T(8,128)(2,1)S(1)}, bf16[64,4096]{1,0:T(8,128)(2,1)S(1)}, u32[]{:S(2)}, u32[]{:S(2)}) collective-permute-start(bf16[64,4096]{1,0:T(8,128)(2,1)S(1)} %shard_map.99.refs_1_), channel_id=1, source_target_pairs={{0,192},{1,193},{2,194},{3,195},{4,196},{5,197},{6,198},{7,199},{8... | collective-permute-start | bytes 1572872 | tf_op jit(solution)/shard_map/ppermute | solution.py:44
  63.4 5.1 %collective-permute-done.17.refs_5_ = bf16[64,4096]{1,0:T(8,128)(2,1)S(1)} collective-permute-done((bf16[64,4096]{1,0:T(8,128)(2,1)S(1)}, bf16[64,4096]{1,0:T(8,128)(2,1)S(1)}, u32[]{:S(2)}, u32[]{:S(2)}) %collective-permute-start.17) | collective-permute-done | bytes 524320 | tf_op jit(solution)/shard_map/ppermute | solution.py:44
  68.4 3.4 %collective-permute-start.19 = (bf16[64,4096]{1,0:T(8,128)(2,1)S(1)}, bf16[64,4096]{1,0:T(8,128)(2,1)S(1)}, u32[]{:S(2)}, u32[]{:S(2)}) collective-permute-start(bf16[64,4096]{1,0:T(8,128)(2,1)S(1)} %collective-permute-done.17.refs_5_), channel_id=1, source_target_pairs={{0,192},{1,193},{2,194},{3,195},{4,196},{5,197},{6,198},{7,199},{8... | collective-permute-start | bytes 1572872 | tf_op jit(solution)/shard_map/ppermute | solution.py:44
  71.9 7.8 %collective-permute-done.16.refs_4_ = bf16[64,4096]{1,0:T(8,128)(2,1)S(1)} collective-permute-done((bf16[64,4096]{1,0:T(8,128)(2,1)S(1)}, bf16[64,4096]{1,0:T(8,128)(2,1)S(1)}, u32[]{:S(2)}, u32[]{:S(2)}) %collective-permute-start.16) | collective-permute-done | bytes 524320 | tf_op jit(solution)/shard_map/ppermute | solution.py:44
  79.7 3.4 %collective-permute-start.7 = (bf16[48,4096]{1,0:T(8,128)(2,1)S(1)}, bf16[48,4096]{1,0:T(8,128)(2,1)S(1)}, u32[]{:S(2)}, u32[]{:S(2)}) collective-permute-start(bf16[48,4096]{1,0:T(8,128)(2,1)S(1)} %shard_map.96.refs_0_.refs_8_), channel_id=1, source_target_pairs={{0,24},{1,25},{2,26},{3,27},{4,28},{5,29},{6,30},{7,31},{8,0},{9,1... | collective-permute-start | bytes 1179656 | tf_op jit(solution)/shard_map/ppermute | solution.py:44
  83.9 2.5 %collective-permute-start.10 = (bf16[48,4096]{1,0:T(8,128)(2,1)S(1)}, bf16[48,4096]{1,0:T(8,128)(2,1)S(1)}, u32[]{:S(2)}, u32[]{:S(2)}) collective-permute-start(bf16[48,4096]{1,0:T(8,128)(2,1)S(1)} %collective-permute-done.8.refs_5_.refs_13_), channel_id=1, source_target_pairs={{0,24},{1,25},{2,26},{3,27},{4,28},{5,29},{6,30},{7,31},{8,0},{9,1... | collective-permute-start | bytes 1179656 | tf_op jit(solution)/shard_map/ppermute | solution.py:44
  88.5 2.4 %collective-permute-done.19.refs_7_ = bf16[64,4096]{1,0:T(8,128)(2,1)S(1)} collective-permute-done((bf16[64,4096]{1,0:T(8,128)(2,1)S(1)}, bf16[64,4096]{1,0:T(8,128)(2,1)S(1)}, u32[]{:S(2)}, u32[]{:S(2)}) %collective-permute-start.19) | collective-permute-done | bytes 524320 | tf_op jit(solution)/shard_map/ppermute | solution.py:44
  90.9 2.4 %shard_map.100 = (bf16[128,512]{1,0:T(8,128)(2,1)S(1)}, bf16[128,512]{1,0:T(8,128)(2,1)S(1)}, bf16[256,512]{1,0:T(8,128)(2,1)S(1)}) custom-call(bf16[256,4096]{1,0:T(8,128)(2,1)S(1)} %shard_map.94.x, bf16[256,896]{1,0:T(8,128)(2,1)S(1)} %shard_map.95.cot, bf16[64,4096]{1,0:T(8,128)(2,1)S(1)} %shard_map.98.refs_0_, bf16[64,4096]{1,0:T(8,128)(2,1)S(1)} %shard_map.99.refs_1_, ...), custom_call_target="tpu_custom_call" | custom-call | tf_op jit(solution)/shard_map/pallas_call | solution.py:357
  98.1 3.8 %shard_map.108 = (bf16[2,4,128,512]{3,2,1,0:T(8,128)(2,1)S(1)}, bf16[2,4,128,512]{3,2,1,0:T(8,128)(2,1)S(1)}) custom-call(bf16[256,512]{1,0:T(8,128)(2,1)S(1)} %get-tuple-element.49.dd.dd_a, bf16[256,384]{1,0:T(8,128)(2,1)S(1)} %get-tuple-element.64.dd.dd_b, bf16[64,4096]{1,0:T(8,128)(2,1)S(1)} %shard_map.98.refs_0_, ...), custom_call_target="tpu_custom_call" | custom-call | tf_op jit(solution)/shard_map/pallas_call | solution.py:373
  101.9 12.1 %collective-permute-start.36 = (bf16[2,4,128,512]{3,2,1,0:T(8,128)(2,1)S(1)}, bf16[2,4,128,512]{3,2,1,0:T(8,128)(2,1)S(1)}, u32[]{:S(2)}, u32[]{:S(2)}) collective-permute-start(bf16[2,4,128,512]{3,2,1,0:T(8,128)(2,1)S(1)} %get-tuple-element.74), channel_id=1, source_target_pairs={{0,1},{1,0},{2,3},{3,2},{4,5},{5,4},{6,7},{7,6},{8,9},{9,8},{10,11... | collective-permute-start | bytes 3145736 | tf_op jit(solution)/shard_map/ppermute | solution.py:44
  114.0 2.3 %collective-permute-done.36 = bf16[2,4,128,512]{3,2,1,0:T(8,128)(2,1)S(1)} collective-permute-done((bf16[2,4,128,512]{3,2,1,0:T(8,128)(2,1)S(1)}, bf16[2,4,128,512]{3,2,1,0:T(8,128)(2,1)S(1)}, u32[]{:S(2)}, u32[]{:S(2)}) %collective-permute-start.36) | collective-permute-done | bytes 1048608 | tf_op jit(solution)/shard_map/ppermute | solution.py:44
  117.5 6.2 %all-to-all-start.1 = ((bf16[8,128,512]{2,1,0:T(8,128)(2,1)}), bf16[8,128,512]{2,1,0:T(8,128)(2,1)S(1)}, u32[]{:S(2)}, u32[]{:S(2)}) async-start(bf16[8,128,512]{2,1,0:T(8,128)(2,1)} %shard_map.109), calls=%async_computation.1 | async-start | bytes 2097152 | tf_op jit(solution)/shard_map/all_to_all | solution.py:48
  129.7 3.5 %collective-permute-start.21 = (bf16[64,4096]{1,0:T(8,128)(2,1)S(1)}, bf16[64,4096]{1,0:T(8,128)(2,1)S(1)}, u32[]{:S(2)}, u32[]{:S(2)}) collective-permute-start(bf16[64,4096]{1,0:T(8,128)(2,1)S(1)} %get-tuple-element.54), channel_id=1, source_target_pairs={{0,192},{1,193},{2,194},{3,195},{4,196},{5,197},{6,198},{7,199},{8... | collective-permute-start | bytes 1572872 | tf_op jit(solution)/shard_map/ppermute | solution.py:44
  133.2 10.1 %collective-permute-done.21.from_right = bf16[64,4096]{1,0:T(8,128)(2,1)S(1)} collective-permute-done((bf16[64,4096]{1,0:T(8,128)(2,1)S(1)}, bf16[64,4096]{1,0:T(8,128)(2,1)S(1)}, u32[]{:S(2)}, u32[]{:S(2)}) %collective-permute-start.21) | collective-permute-done | bytes 524320 | tf_op jit(solution)/shard_map/ppermute | solution.py:44
  143.2 3.4 %collective-permute-start.24 = (bf16[64,4096]{1,0:T(8,128)(2,1)S(1)}, bf16[64,4096]{1,0:T(8,128)(2,1)S(1)}, u32[]{:S(2)}, u32[]{:S(2)}) collective-permute-start(bf16[64,4096]{1,0:T(8,128)(2,1)S(1)} %get-tuple-element.57), channel_id=1, source_target_pairs={{0,192},{1,193},{2,194},{3,195},{4,196},{5,197},{6,198},{7,199},{8... | collective-permute-start | bytes 1572872 | tf_op jit(solution)/shard_map/ppermute | solution.py:44
  146.9 2.8 %collective-permute-start.23 = (bf16[64,4096]{1,0:T(8,128)(2,1)S(1)}, bf16[64,4096]{1,0:T(8,128)(2,1)S(1)}, u32[]{:S(2)}, u32[]{:S(2)}) collective-permute-start(bf16[64,4096]{1,0:T(8,128)(2,1)S(1)} %get-tuple-element.56), channel_id=1, source_target_pairs={{0,192},{1,193},{2,194},{3,195},{4,196},{5,197},{6,198},{7,199},{8... | collective-permute-start | bytes 1572872 | tf_op jit(solution)/shard_map/ppermute | solution.py:44
  149.7 13.1 %collective-permute-done.31.left = bf16[96,4096]{1,0:T(8,128)(2,1)S(1)} collective-permute-done((bf16[96,4096]{1,0:T(8,128)(2,1)S(1)}, bf16[96,4096]{1,0:T(8,128)(2,1)S(1)}, u32[]{:S(2)}, u32[]{:S(2)}) %collective-permute-start.31) | collective-permute-done | bytes 786464 | tf_op jit(solution)/shard_map/ppermute | solution.py:44
  163.5 3.0 %collective-permute-start.20 = (bf16[128,896]{1,0:T(8,128)(2,1)S(1)}, bf16[128,896]{1,0:T(8,128)(2,1)S(1)}, u32[]{:S(2)}, u32[]{:S(2)}) collective-permute-start(bf16[128,896]{1,0:T(8,128)(2,1)S(1)} %copy-done.10), channel_id=1, source_target_pairs={{0,32},{1,33},{2,34},{3,35},{4,36},{5,37},{6,38},{7,39},{8,40},{9,... | collective-permute-start | bytes 688136 | tf_op jit(solution)/shard_map/ppermute | solution.py:44
  167.0 3.5 %collective-permute-start.33 = (bf16[24,4096]{1,0:T(8,128)(2,1)S(1)}, bf16[24,4096]{1,0:T(8,128)(2,1)S(1)}, u32[]{:S(2)}, u32[]{:S(2)}) collective-permute-start(bf16[24,4096]{1,0:T(8,128)(2,1)S(1)} %get-tuple-element.70), channel_id=1, source_target_pairs={{0,192},{1,193},{2,194},{3,195},{4,196},{5,197},{6,198},{7,199},{8... | collective-permute-start | bytes 589832 | tf_op jit(solution)/shard_map/ppermute | solution.py:44
  170.5 6.3 %collective-permute-done.26.l_hi = bf16[64,4096]{1,0:T(8,128)(2,1)S(1)} collective-permute-done((bf16[64,4096]{1,0:T(8,128)(2,1)S(1)}, bf16[64,4096]{1,0:T(8,128)(2,1)S(1)}, u32[]{:S(2)}, u32[]{:S(2)}) %collective-permute-start.26) | collective-permute-done | bytes 524320 | tf_op jit(solution)/shard_map/ppermute | solution.py:44
  178.7 3.1 %collective-permute-start.35 = (bf16[24,4096]{1,0:T(8,128)(2,1)S(1)}, bf16[24,4096]{1,0:T(8,128)(2,1)S(1)}, u32[]{:S(2)}, u32[]{:S(2)}) collective-permute-start(bf16[24,4096]{1,0:T(8,128)(2,1)S(1)} %get-tuple-element.72), channel_id=1, source_target_pairs={{0,128},{1,129},{2,130},{3,131},{4,132},{5,133},{6,134},{7,135},{8... | collective-permute-start | bytes 589832 | tf_op jit(solution)/shard_map/ppermute | solution.py:44
  184.4 3.9 %collective-permute-done.35.refs_7_ = bf16[24,4096]{1,0:T(8,128)(2,1)S(1)} collective-permute-done((bf16[24,4096]{1,0:T(8,128)(2,1)S(1)}, bf16[24,4096]{1,0:T(8,128)(2,1)S(1)}, u32[]{:S(2)}, u32[]{:S(2)}) %collective-permute-start.35) | collective-permute-done | bytes 196640 | tf_op jit(solution)/shard_map/ppermute | solution.py:44
  188.4 2.3 %collective-permute-done.28.refs_2_ = bf16[32,4096]{1,0:T(8,128)(2,1)S(1)} collective-permute-done((bf16[32,4096]{1,0:T(8,128)(2,1)S(1)}, bf16[32,4096]{1,0:T(8,128)(2,1)S(1)}, u32[]{:S(2)}, u32[]{:S(2)}) %collective-permute-start.28) | collective-permute-done | bytes 262176 | tf_op jit(solution)/shard_map/ppermute | solution.py:44
  (88 shorter events, 30.5 us)
Async XLA Ops:
  3.6 38.2 %all-to-all-start = ((bf16[8,128,512]{2,1,0:T(8,128)(2,1)}), bf16[8,128,512]{2,1,0:T(8,128)(2,1)S(1)}, u32[]{:S(2)}, u32[]{:S(2)}) async-start(bf16[8,128,512]{2,1,0:T(8,128)(2,1)} %get-tuple-element.41), calls=%async_computation | async-start | bytes 2097152 | tf_op jit(solution)/shard_map/all_to_all | solution.py:48
  16.8 25.5 %collective-permute-start.2 = (bf16[24,4096]{1,0:T(8,128)(2,1)S(1)}, bf16[24,4096]{1,0:T(8,128)(2,1)S(1)}, u32[]{:S(2)}, u32[]{:S(2)}) collective-permute-start(bf16[24,4096]{1,0:T(8,128)(2,1)S(1)} %get-tuple-element.43.first), channel_id=1, source_target_pairs={{0,64},{1,65},{2,66},{3,67},{4,68},{5,69},{6,70},{7,71},{8,72},{9,... | collective-permute-start | bytes 589832 | tf_op jit(solution)/shard_map/ppermute | solution.py:44
  17.2 30.3 %collective-permute-start.13 = (bf16[32,4096]{1,0:T(8,128)(2,1)S(1)}, bf16[32,4096]{1,0:T(8,128)(2,1)S(1)}, u32[]{:S(2)}, u32[]{:S(2)}) collective-permute-start(bf16[32,4096]{1,0:T(8,128)(2,1)S(1)} %get-tuple-element.44.first), channel_id=1, source_target_pairs={{0,16},{1,17},{2,18},{3,19},{4,20},{5,21},{6,22},{7,23},{8,24},{9,... | collective-permute-start | bytes 786440 | tf_op jit(solution)/shard_map/ppermute | solution.py:44
  19.6 26.8 %collective-permute-start.3 = (bf16[24,4096]{1,0:T(8,128)(2,1)S(1)}, bf16[24,4096]{1,0:T(8,128)(2,1)}, u32[]{:S(2)}, u32[]{:S(2)}) collective-permute-start(bf16[24,4096]{1,0:T(8,128)(2,1)S(1)} %get-tuple-element.43.first), channel_id=1, source_target_pairs={{0,192},{1,193},{2,194},{3,195},{4,196},{5,197},{6,198},{7,199},{8... | collective-permute-start | bytes 589832 | tf_op jit(solution)/shard_map/ppermute | solution.py:44
  21.9 41.3 %collective-permute-start.14 = (bf16[64,4096]{1,0:T(8,128)(2,1)S(1)}, bf16[64,4096]{1,0:T(8,128)(2,1)S(1)}, u32[]{:S(2)}, u32[]{:S(2)}) collective-permute-start(bf16[64,4096]{1,0:T(8,128)(2,1)S(1)} %shard_map.98.refs_0_), channel_id=1, source_target_pairs={{0,64},{1,65},{2,66},{3,67},{4,68},{5,69},{6,70},{7,71},{8,72},{9,... | collective-permute-start | bytes 1572872 | tf_op jit(solution)/shard_map/ppermute | solution.py:44
  41.8 42.2 %collective-permute-start = (bf16[8,128,512]{2,1,0:T(8,128)(2,1)S(1)}, bf16[8,128,512]{2,1,0:T(8,128)(2,1)S(1)}, u32[]{:S(2)}, u32[]{:S(2)}) collective-permute-start(bf16[8,128,512]{2,1,0:T(8,128)(2,1)S(1)} %all-to-all-done.own), channel_id=1, source_target_pairs={{0,1},{1,0},{2,3},{3,2},{4,5},{5,4},{6,7},{7,6},{8,9},{9,8},{10,11... | collective-permute-start | bytes 3145736 | tf_op jit(solution)/shard_map/ppermute | solution.py:44
  46.4 15.4 %collective-permute-start.5 = (bf16[48,4096]{1,0:T(8,128)(2,1)S(1)}, bf16[48,4096]{1,0:T(8,128)(2,1)S(1)}, u32[]{:S(2)}, u32[]{:S(2)}) collective-permute-start(bf16[48,4096]{1,0:T(8,128)(2,1)S(1)} %shard_map.96.refs_0_.refs_8_), channel_id=1, source_target_pairs={{0,8},{1,9},{2,10},{3,11},{4,12},{5,13},{6,14},{7,15},{8,16},{9,17... | collective-permute-start | bytes 1179656 | tf_op jit(solution)/shard_map/ppermute | solution.py:44
  47.4 14.8 %collective-permute-start.8 = (bf16[48,4096]{1,0:T(8,128)(2,1)S(1)}, bf16[48,4096]{1,0:T(8,128)(2,1)S(1)}, u32[]{:S(2)}, u32[]{:S(2)}) collective-permute-start(bf16[48,4096]{1,0:T(8,128)(2,1)S(1)} %shard_map.97.refs_1_.refs_9_), channel_id=1, source_target_pairs={{0,24},{1,25},{2,26},{3,27},{4,28},{5,29},{6,30},{7,31},{8,0},{9,1... | collective-permute-start | bytes 1179656 | tf_op jit(solution)/shard_map/ppermute | solution.py:44
  61.8 17.9 %collective-permute-start.16 = (bf16[64,4096]{1,0:T(8,128)(2,1)S(1)}, bf16[64,4096]{1,0:T(8,128)(2,1)S(1)}, u32[]{:S(2)}, u32[]{:S(2)}) collective-permute-start(bf16[64,4096]{1,0:T(8,128)(2,1)S(1)} %shard_map.98.refs_0_), channel_id=1, source_target_pairs={{0,192},{1,193},{2,194},{3,195},{4,196},{5,197},{6,198},{7,199},{8... | collective-permute-start | bytes 1572872 | tf_op jit(solution)/shard_map/ppermute | solution.py:44
  62.3 20.8 %collective-permute-start.15 = (bf16[64,4096]{1,0:T(8,128)(2,1)S(1)}, bf16[64,4096]{1,0:T(8,128)(2,1)S(1)}, u32[]{:S(2)}, u32[]{:S(2)}) collective-permute-start(bf16[64,4096]{1,0:T(8,128)(2,1)S(1)} %shard_map.99.refs_1_), channel_id=1, source_target_pairs={{0,64},{1,65},{2,66},{3,67},{4,68},{5,69},{6,70},{7,71},{8,72},{9,... | collective-permute-start | bytes 1572872 | tf_op jit(solution)/shard_map/ppermute | solution.py:44
  63.3 19.8 %collective-permute-start.18 = (bf16[64,4096]{1,0:T(8,128)(2,1)S(1)}, bf16[64,4096]{1,0:T(8,128)(2,1)S(1)}, u32[]{:S(2)}, u32[]{:S(2)}) collective-permute-start(bf16[64,4096]{1,0:T(8,128)(2,1)S(1)} %collective-permute-done.14.refs_2_), channel_id=1, source_target_pairs={{0,64},{1,65},{2,66},{3,67},{4,68},{5,69},{6,70},{7,71},{8,72},{9,... | collective-permute-start | bytes 1572872 | tf_op jit(solution)/shard_map/ppermute | solution.py:44
  68.4 22.5 %collective-permute-start.19 = (bf16[64,4096]{1,0:T(8,128)(2,1)S(1)}, bf16[64,4096]{1,0:T(8,128)(2,1)S(1)}, u32[]{:S(2)}, u32[]{:S(2)}) collective-permute-start(bf16[64,4096]{1,0:T(8,128)(2,1)S(1)} %collective-permute-done.17.refs_5_), channel_id=1, source_target_pairs={{0,192},{1,193},{2,194},{3,195},{4,196},{5,197},{6,198},{7,199},{8... | collective-permute-start | bytes 1572872 | tf_op jit(solution)/shard_map/ppermute | solution.py:44
  79.7 13.6 %collective-permute-start.7 = (bf16[48,4096]{1,0:T(8,128)(2,1)S(1)}, bf16[48,4096]{1,0:T(8,128)(2,1)S(1)}, u32[]{:S(2)}, u32[]{:S(2)}) collective-permute-start(bf16[48,4096]{1,0:T(8,128)(2,1)S(1)} %shard_map.96.refs_0_.refs_8_), channel_id=1, source_target_pairs={{0,24},{1,25},{2,26},{3,27},{4,28},{5,29},{6,30},{7,31},{8,0},{9,1... | collective-permute-start | bytes 1179656 | tf_op jit(solution)/shard_map/ppermute | solution.py:44
  83.1 10.2 %collective-permute-start.6 = (bf16[48,4096]{1,0:T(8,128)(2,1)S(1)}, bf16[48,4096]{1,0:T(8,128)(2,1)S(1)}, u32[]{:S(2)}, u32[]{:S(2)}) collective-permute-start(bf16[48,4096]{1,0:T(8,128)(2,1)S(1)} %shard_map.97.refs_1_.refs_9_), channel_id=1, source_target_pairs={{0,8},{1,9},{2,10},{3,11},{4,12},{5,13},{6,14},{7,15},{8,16},{9,17... | collective-permute-start | bytes 1179656 | tf_op jit(solution)/shard_map/ppermute | solution.py:44
  83.1 12.0 %collective-permute-start.9 = (bf16[48,4096]{1,0:T(8,128)(2,1)S(1)}, bf16[48,4096]{1,0:T(8,128)(2,1)S(1)}, u32[]{:S(2)}, u32[]{:S(2)}) collective-permute-start(bf16[48,4096]{1,0:T(8,128)(2,1)S(1)} %collective-permute-done.5.refs_2_.refs_10_), channel_id=1, source_target_pairs={{0,8},{1,9},{2,10},{3,11},{4,12},{5,13},{6,14},{7,15},{8,16},{9,17... | collective-permute-start | bytes 1179656 | tf_op jit(solution)/shard_map/ppermute | solution.py:44
  83.9 11.2 %collective-permute-start.10 = (bf16[48,4096]{1,0:T(8,128)(2,1)S(1)}, bf16[48,4096]{1,0:T(8,128)(2,1)S(1)}, u32[]{:S(2)}, u32[]{:S(2)}) collective-permute-start(bf16[48,4096]{1,0:T(8,128)(2,1)S(1)} %collective-permute-done.8.refs_5_.refs_13_), channel_id=1, source_target_pairs={{0,24},{1,25},{2,26},{3,27},{4,28},{5,29},{6,30},{7,31},{8,0},{9,1... | collective-permute-start | bytes 1179656 | tf_op jit(solution)/shard_map/ppermute | solution.py:44
  101.9 14.4 %collective-permute-start.36 = (bf16[2,4,128,512]{3,2,1,0:T(8,128)(2,1)S(1)}, bf16[2,4,128,512]{3,2,1,0:T(8,128)(2,1)S(1)}, u32[]{:S(2)}, u32[]{:S(2)}) collective-permute-start(bf16[2,4,128,512]{3,2,1,0:T(8,128)(2,1)S(1)} %get-tuple-element.74), channel_id=1, source_target_pairs={{0,1},{1,0},{2,3},{3,2},{4,5},{5,4},{6,7},{7,6},{8,9},{9,8},{10,11... | collective-permute-start | bytes 3145736 | tf_op jit(solution)/shard_map/ppermute | solution.py:44
  117.5 73.2 %all-to-all-start.1 = ((bf16[8,128,512]{2,1,0:T(8,128)(2,1)}), bf16[8,128,512]{2,1,0:T(8,128)(2,1)S(1)}, u32[]{:S(2)}, u32[]{:S(2)}) async-start(bf16[8,128,512]{2,1,0:T(8,128)(2,1)} %shard_map.109), calls=%async_computation.1 | async-start | bytes 2097152 | tf_op jit(solution)/shard_map/all_to_all | solution.py:48
  126.2 20.7 %collective-permute-start.30 = (bf16[96,4096]{1,0:T(8,128)(2,1)S(1)}, bf16[96,4096]{1,0:T(8,128)(2,1)S(1)}, u32[]{:S(2)}, u32[]{:S(2)}) collective-permute-start(bf16[96,4096]{1,0:T(8,128)(2,1)S(1)} %get-tuple-element.66), channel_id=1, source_target_pairs={{0,24},{1,25},{2,26},{3,27},{4,28},{5,29},{6,30},{7,31},{8,0},{9,1... | collective-permute-start | bytes 2359304 | tf_op jit(solution)/shard_map/ppermute | solution.py:44
  126.3 36.4 %collective-permute-start.31 = (bf16[96,4096]{1,0:T(8,128)(2,1)S(1)}, bf16[96,4096]{1,0:T(8,128)(2,1)S(1)}, u32[]{:S(2)}, u32[]{:S(2)}) collective-permute-start(bf16[96,4096]{1,0:T(8,128)(2,1)S(1)} %get-tuple-element.67), channel_id=1, source_target_pairs={{0,8},{1,9},{2,10},{3,11},{4,12},{5,13},{6,14},{7,15},{8,16},{9,17... | collective-permute-start | bytes 2359304 | tf_op jit(solution)/shard_map/ppermute | solution.py:44
  129.7 13.6 %collective-permute-start.21 = (bf16[64,4096]{1,0:T(8,128)(2,1)S(1)}, bf16[64,4096]{1,0:T(8,128)(2,1)S(1)}, u32[]{:S(2)}, u32[]{:S(2)}) collective-permute-start(bf16[64,4096]{1,0:T(8,128)(2,1)S(1)} %get-tuple-element.54), channel_id=1, source_target_pairs={{0,192},{1,193},{2,194},{3,195},{4,196},{5,197},{6,198},{7,199},{8... | collective-permute-start | bytes 1572872 | tf_op jit(solution)/shard_map/ppermute | solution.py:44
  133.2 13.5 %collective-permute-start.22 = (bf16[64,4096]{1,0:T(8,128)(2,1)S(1)}, bf16[64,4096]{1,0:T(8,128)(2,1)S(1)}, u32[]{:S(2)}, u32[]{:S(2)}) collective-permute-start(bf16[64,4096]{1,0:T(8,128)(2,1)S(1)} %get-tuple-element.55), channel_id=1, source_target_pairs={{0,64},{1,65},{2,66},{3,67},{4,68},{5,69},{6,70},{7,71},{8,72},{9,... | collective-permute-start | bytes 1572872 | tf_op jit(solution)/shard_map/ppermute | solution.py:44
  133.2 30.4 %collective-permute-start.32 = (bf16[96,4096]{1,0:T(8,128)(2,1)S(1)}, bf16[96,4096]{1,0:T(8,128)(2,1)S(1)}, u32[]{:S(2)}, u32[]{:S(2)}) collective-permute-start(bf16[96,4096]{1,0:T(8,128)(2,1)S(1)} %get-tuple-element.68), channel_id=1, source_target_pairs={{0,16},{1,17},{2,18},{3,19},{4,20},{5,21},{6,22},{7,23},{8,24},{9,... | collective-permute-start | bytes 2359304 | tf_op jit(solution)/shard_map/ppermute | solution.py:44
  143.2 23.7 %collective-permute-start.24 = (bf16[64,4096]{1,0:T(8,128)(2,1)S(1)}, bf16[64,4096]{1,0:T(8,128)(2,1)S(1)}, u32[]{:S(2)}, u32[]{:S(2)}) collective-permute-start(bf16[64,4096]{1,0:T(8,128)(2,1)S(1)} %get-tuple-element.57), channel_id=1, source_target_pairs={{0,192},{1,193},{2,194},{3,195},{4,196},{5,197},{6,198},{7,199},{8... | collective-permute-start | bytes 1572872 | tf_op jit(solution)/shard_map/ppermute | solution.py:44
  146.7 23.8 %collective-permute-start.25 = (bf16[64,4096]{1,0:T(8,128)(2,1)S(1)}, bf16[64,4096]{1,0:T(8,128)(2,1)S(1)}, u32[]{:S(2)}, u32[]{:S(2)}) collective-permute-start(bf16[64,4096]{1,0:T(8,128)(2,1)S(1)} %get-tuple-element.58), channel_id=1, source_target_pairs={{0,64},{1,65},{2,66},{3,67},{4,68},{5,69},{6,70},{7,71},{8,72},{9,... | collective-permute-start | bytes 1572872 | tf_op jit(solution)/shard_map/ppermute | solution.py:44
  146.9 23.6 %collective-permute-start.23 = (bf16[64,4096]{1,0:T(8,128)(2,1)S(1)}, bf16[64,4096]{1,0:T(8,128)(2,1)S(1)}, u32[]{:S(2)}, u32[]{:S(2)}) collective-permute-start(bf16[64,4096]{1,0:T(8,128)(2,1)S(1)} %get-tuple-element.56), channel_id=1, source_target_pairs={{0,192},{1,193},{2,194},{3,195},{4,196},{5,197},{6,198},{7,199},{8... | collective-permute-start | bytes 1572872 | tf_op jit(solution)/shard_map/ppermute | solution.py:44
  162.8 14.0 %collective-permute-start.26 = (bf16[64,4096]{1,0:T(8,128)(2,1)S(1)}, bf16[64,4096]{1,0:T(8,128)(2,1)S(1)}, u32[]{:S(2)}, u32[]{:S(2)}) collective-permute-start(bf16[64,4096]{1,0:T(8,128)(2,1)S(1)} %get-tuple-element.59), channel_id=1, source_target_pairs={{0,64},{1,65},{2,66},{3,67},{4,68},{5,69},{6,70},{7,71},{8,72},{9,... | collective-permute-start | bytes 1572872 | tf_op jit(solution)/shard_map/ppermute | solution.py:44
  163.5 15.2 %collective-permute-start.20 = (bf16[128,896]{1,0:T(8,128)(2,1)S(1)}, bf16[128,896]{1,0:T(8,128)(2,1)S(1)}, u32[]{:S(2)}, u32[]{:S(2)}) collective-permute-start(bf16[128,896]{1,0:T(8,128)(2,1)S(1)} %copy-done.10), channel_id=1, source_target_pairs={{0,32},{1,33},{2,34},{3,35},{4,36},{5,37},{6,38},{7,39},{8,40},{9,... | collective-permute-start | bytes 688136 | tf_op jit(solution)/shard_map/ppermute | solution.py:44
  167.0 11.7 %collective-permute-start.33 = (bf16[24,4096]{1,0:T(8,128)(2,1)S(1)}, bf16[24,4096]{1,0:T(8,128)(2,1)S(1)}, u32[]{:S(2)}, u32[]{:S(2)}) collective-permute-start(bf16[24,4096]{1,0:T(8,128)(2,1)S(1)} %get-tuple-element.70), channel_id=1, source_target_pairs={{0,192},{1,193},{2,194},{3,195},{4,196},{5,197},{6,198},{7,199},{8... | collective-permute-start | bytes 589832 | tf_op jit(solution)/shard_map/ppermute | solution.py:44
  177.2 11.2 %collective-permute-start.27 = (bf16[32,4096]{1,0:T(8,128)(2,1)S(1)}, bf16[32,4096]{1,0:T(8,128)(2,1)S(1)}, u32[]{:S(2)}, u32[]{:S(2)}) collective-permute-start(bf16[32,4096]{1,0:T(8,128)(2,1)S(1)} %get-tuple-element.61), channel_id=1, source_target_pairs={{0,24},{1,25},{2,26},{3,27},{4,28},{5,29},{6,30},{7,31},{8,0},{9,1... | collective-permute-start | bytes 786440 | tf_op jit(solution)/shard_map/ppermute | solution.py:44
  177.3 13.5 %collective-permute-start.28 = (bf16[32,4096]{1,0:T(8,128)(2,1)S(1)}, bf16[32,4096]{1,0:T(8,128)(2,1)S(1)}, u32[]{:S(2)}, u32[]{:S(2)}) collective-permute-start(bf16[32,4096]{1,0:T(8,128)(2,1)S(1)} %get-tuple-element.62), channel_id=1, source_target_pairs={{0,8},{1,9},{2,10},{3,11},{4,12},{5,13},{6,14},{7,15},{8,16},{9,17... | collective-permute-start | bytes 786440 | tf_op jit(solution)/shard_map/ppermute | solution.py:44
  178.7 12.0 %collective-permute-start.29 = (bf16[32,4096]{1,0:T(8,128)(2,1)S(1)}, bf16[32,4096]{1,0:T(8,128)(2,1)S(1)}, u32[]{:S(2)}, u32[]{:S(2)}) collective-permute-start(bf16[32,4096]{1,0:T(8,128)(2,1)S(1)} %get-tuple-element.63), channel_id=1, source_target_pairs={{0,16},{1,17},{2,18},{3,19},{4,20},{5,21},{6,22},{7,23},{8,24},{9,... | collective-permute-start | bytes 786440 | tf_op jit(solution)/shard_map/ppermute | solution.py:44
  (19 other events, 241.9 us)
